TPU v7x, 128 devices: a whole 4x4x4 slice. The times are simulated.
128 devices in a mesh: seq: 16 (over y, z_lo, core), zero: 8 (over x, z_hi).
Axes of the slice: x: 4, y: 4, z: 4 (z_hi: 2, z_lo: 2; z = z_hi * 2 + z_lo), core: 2. Of those that a mesh axis runs over, the one named last changes fastest.
Arguments:
- hidden: bfloat16 [8, 2048, 1280], P('zero', 'seq'), may hold values from -6 to 6
- output_grad: bfloat16 [8, 2048, 2560], P('zero', 'seq'), may hold values from -6 to 6
- input_weight: bfloat16 [1280, 2856], P('zero'), may hold values from -0.15625 to 0.15625
- step_bias: float32 [40], replicated, may hold values from -7 to -2
- decay_log: float32 [40], replicated, may hold values from -4 to 1
- skip_gain: float32 [40], replicated, may hold values from 0.5 to 1.5
Outputs:
- hidden_grad: bfloat16 [8, 2048, 1280], P('zero', 'seq')
- weight_grad: float32 [1280, 2856], P(('seq', 'zero'))
- head_grads: float32 [3, 40], replicated
All inputs are finite; a program needn't handle non-finite values.
Results may differ from a plain program's by a relative error of at most 0.0049.
Values may be sent and summed in bfloat16 or wider, within the bound.
A program may use at most 192 MiB of HBM per device.

v0:
```python
import functools

import jax
import jax.numpy as jnp
from jax import lax
from jax.sharding import Mesh
from jax.sharding import PartitionSpec as P

HEADS = 40
HEAD_DIM = 64
STATE = 128
GROUP = 128
INNER = 2560
ZERO = ("zero_0", "zero_1")
SEQ = ("seq_0", "seq_1", "seq_2")
SEQ_ZERO = ("seq_0", "seq_1", "seq_2", "zero_0", "zero_1")


highest = lax.Precision.HIGHEST


def neutral_like(x, identity):
    return jax.tree.map(
        lambda part, zero: jnp.zeros_like(part) + jnp.asarray(zero, part.dtype), x, identity
    )


def prefix_by_axis(x, axes, combine, identity, reverse):
    before = start = neutral_like(x, identity)
    subtotal = x
    for axis in reversed(axes):
        length, index = (lax.axis_size(axis), lax.axis_index(axis))
        pieces = jax.tree.map(lambda part: lax.all_gather(part, axis), subtotal)
        inside, subtotal = (start, start)
        for k in reversed(range(length)) if reverse else range(length):
            passed = k > index if reverse else k < index
            subtotal = combine(subtotal, jax.tree.map(lambda part: part[k], pieces))
            inside = jax.tree.map(lambda new, old: jnp.where(passed, new, old), subtotal, inside)
        before = combine(inside, before)
    return before


def over_axes(x, axes):
    return functools.reduce(lax.psum, axes, x)


def state_mixer(columns, step_bias, decay_log, skip_gain, initial):
    length = columns.shape[0]
    blocks = length // GROUP
    values = jax.nn.silu(columns[:, :INNER])
    input_map = jax.nn.silu(columns[:, INNER : INNER + STATE]).reshape(blocks, GROUP, STATE)
    output_map = jax.nn.silu(columns[:, INNER + STATE : INNER + 2 * STATE]).reshape(
        blocks, GROUP, STATE
    )
    step_size = jax.nn.softplus(columns[:, INNER + 2 * STATE :] + step_bias)
    log_decay = -jnp.exp(decay_log) * step_size
    head_values = values.reshape(blocks, GROUP, HEADS, HEAD_DIM)
    scaled = head_values * step_size.reshape(blocks, GROUP, HEADS)[:, :, :, None]
    cumulative = jnp.cumsum(log_decay.reshape(blocks, GROUP, HEADS), axis=1)
    causal = (
        lax.broadcasted_iota(jnp.int32, (GROUP, GROUP), 0)
        >= lax.broadcasted_iota(jnp.int32, (GROUP, GROUP), 1)
    )[None, :, :, None]
    differences = cumulative[:, :, None, :] - cumulative[:, None, :, :]
    within = jnp.where(causal, jnp.exp(jnp.where(causal, differences, 0.0)), 0.0)
    scores = jnp.einsum("kqn,ksn->kqs", output_map, input_map, precision=highest)
    inside = jnp.einsum(
        "kqsh,kshp->kqhp", scores[:, :, :, None] * within, scaled, precision=highest
    )
    tail_decay = jnp.exp(cumulative[:, -1:, :] - cumulative)
    group_states = jnp.einsum(
        "kshp,ksn->khpn", scaled * tail_decay[:, :, :, None], input_map, precision=highest
    )
    totals = cumulative[:, -1, :]

    def advance(running, inputs):
        block_total, block_state = inputs
        return (jnp.exp(block_total)[:, None, None] * running + block_state, running)

    final_state, entering = lax.scan(advance, initial, (totals, group_states))
    from_state = (
        jnp.einsum("kqn,khpn->kqhp", output_map, entering, precision=highest)
        * jnp.exp(cumulative)[:, :, :, None]
    )
    mixed_out = inside + from_state + skip_gain[None, None, :, None] * head_values
    return (mixed_out.reshape(length, INNER), final_state, jnp.sum(totals, axis=0))


def combine_states(earlier, later):
    return (earlier[0] + later[0], jnp.exp(later[0])[:, None, None] * earlier[1] + later[1])


def body(hidden, output_grad, input_weight, step_bias, decay_log, skip_gain):
    tokens = hidden[0]
    cotangent = output_grad[0].astype(jnp.float32)
    gathered = lax.all_gather(input_weight, ZERO, axis=0, tiled=True)
    projected = jnp.dot(tokens, gathered, preferred_element_type=jnp.float32)
    initial = jnp.zeros((HEADS, HEAD_DIM, STATE), jnp.float32)
    unused, local_state, local_decay = state_mixer(
        projected, step_bias, decay_log, skip_gain, initial
    )
    identity = (jnp.zeros((HEADS,), jnp.float32), initial)
    before_decay, entering = prefix_by_axis(
        (local_decay, local_state), SEQ, combine_states, identity, False
    )

    def from_start(start_state):
        return state_mixer(projected, step_bias, decay_log, skip_gain, start_state)[0]

    unused_out, start_pull = jax.vjp(from_start, initial)
    direct = start_pull(cotangent)[0]
    after_decay, leaving_grad = prefix_by_axis(
        (local_decay, direct), SEQ, combine_states, identity, True
    )

    def local_pass(columns, bias_part, log_part, gain_part, start_state):
        results = state_mixer(columns, bias_part, log_part, gain_part, start_state)
        return (results[0], results[1])

    unused_pair, pullback = jax.vjp(
        local_pass, projected, step_bias, decay_log, skip_gain, entering
    )
    column_grad, bias_grad, log_grad, gain_grad, unused_grad = pullback((cotangent, leaving_grad))
    rounded = column_grad.astype(jnp.bfloat16)
    head_grads = over_axes(jnp.stack([bias_grad, log_grad, gain_grad]), SEQ_ZERO)
    token_grad = lax.dot_general(
        rounded, gathered, (((1,), (1,)), ((), ())), preferred_element_type=jnp.float32
    )
    columns = tokens
    weight_grad = lax.psum_scatter(
        lax.dot_general(
            columns, rounded, (((0,), (0,)), ((), ())), preferred_element_type=jnp.float32
        ),
        SEQ_ZERO,
        scatter_dimension=0,
        tiled=True,
    )
    return (token_grad.astype(jnp.bfloat16)[None], weight_grad, head_grads)


def solution(mesh):
    torus = Mesh(
        mesh.devices.reshape(4, 2, 2, 4, 2), ("seq_0", "seq_1", "seq_2", "zero_0", "zero_1")
    )
    in_specs = (P(ZERO, SEQ, None), P(ZERO, SEQ, None), P(ZERO, None), P(), P(), P())
    out_specs = (P(ZERO, SEQ, None), P(SEQ_ZERO, None), P())
    return jax.shard_map(body, mesh=torus, in_specs=in_specs, out_specs=out_specs, check_vma=False)
```

profile of v0, /device:TPU:1, one launch (start us, length us, event | category | flops | bytes accessed | tf_op | source)
XLA Modules:
  0.0 595.0 jit_solution(13336844289787323429)
XLA Ops:
  7.2 0.7 all-gather.13.cloned.1.call-update
  8.0 0.3 copy-done.18
  8.7 104.8 %all-gather.13.cloned.1.call-done = bf16[1280,2856]{1,0:T(8,128)(2,1)} async-done(((bf16[160,2856]{1,0:T(8,128)(2,1)}), bf16[1280,2856]{1,0:T(8,128)(2,1)}) %all-gather.13.cloned.1.call-update) | async-done | bytes 7311376 | tf_op jit(solution)/shard_map/all_gather | solution.py:96
  113.4 6.1 %fusion.67 = f32[128,2856]{0,1:T(8,128)S(1)} fusion(bf16[1280,2856]{1,0:T(8,128)(2,1)} %all-gather.13.cloned.1.call-done, bf16[1,128,1280]{2,1,0:T(8,128)(2,1)S(1)} %copy-done), kind=kOutput, calls=%fused_computation.98 | convolution fusion | flops 935854080 | bytes 9101312 | tf_op jit(solution)/shard_map/dot_general | solution.py:97
  120.3 1.1 copy-done.7
  121.3 2.3 convolution_add_fusion.1
  123.7 2.9 all-gather
  126.6 3.1 all-gather.3
  129.7 7.0 %all-gather.23.cloned.1.call-done = f32[80,64,128]{2,1,0:T(8,128)} async-done(((f32[40,64,128]{2,1,0:T(8,128)}), f32[80,64,128]{2,1,0:T(8,128)}) %all-gather.23.cloned.1.call-update) | async-done | bytes 2621456 | tf_op jit(solution)/shard_map/all_gather | solution.py:33
  136.7 3.1 bitcast_add_fusion.14
  139.9 42.4 %all-gather.15.cloned.1.call-done = f32[2,40,64,128]{3,2,1,0:T(8,128)} async-done(((f32[1,40,64,128]{3,2,1,0:T(8,128)}), f32[2,40,64,128]{3,2,1,0:T(8,128)}) %all-gather.15.cloned.1.call-update) | async-done | bytes 2621456 | tf_op jit(solution)/shard_map/all_gather | solution.py:33
  182.3 3.2 multiply_add_fusion.2
  185.8 7.9 %all-gather.4 = f32[4,1,40]{2,1,0:T(1,128)S(1)} all-gather(f32[1,1,40]{2,1,0:T(1,128)S(1)} %get-tuple-element.104), channel_id=1, replica_groups=mesh['seq_0'=4,'seq_1'=2,'seq_2'=2,'zero_0'=4,'zero_1'=2] {'seq_0'}, dimensions={0}, use_global_device_ids=true | all-gather | bytes 800 | tf_op jit(solution)/shard_map/all_gather | solution.py:33
  193.7 1.2 fusion.98
  194.8 48.8 %all-gather.17.cloned.1.call-done = f32[4,40,64,128]{3,2,1,0:T(8,128)} async-done(((f32[1,40,64,128]{3,2,1,0:T(8,128)}), f32[4,40,64,128]{3,2,1,0:T(8,128)}) %all-gather.17.cloned.1.call-update) | async-done | bytes 5242896 | tf_op jit(solution)/shard_map/all_gather | solution.py:33
  243.6 5.1 add_add_fusion.1
  248.8 1.2 convolution_bitcast_fusion.1
  250.3 3.2 multiply_add_fusion
  253.6 1.8 fusion.21
  255.5 1.0 copy-done.6
  256.5 1.1 copy-done.9
  257.6 2.3 convolution_add_fusion
  259.9 15.2 %all-gather.25.cloned.1.call-done = f32[80,64,128]{2,1,0:T(8,128)} async-done(((f32[40,64,128]{2,1,0:T(8,128)}), f32[80,64,128]{2,1,0:T(8,128)}) %all-gather.25.cloned.1.call-update) | async-done | bytes 2621456 | tf_op jit(solution)/shard_map/all_gather | solution.py:33
  275.1 3.0 bitcast_add_fusion.12
  278.2 42.4 %all-gather.19.cloned.1.call-done = f32[2,40,64,128]{3,2,1,0:T(8,128)} async-done(((f32[1,40,64,128]{3,2,1,0:T(8,128)}), f32[2,40,64,128]{3,2,1,0:T(8,128)}) %all-gather.19.cloned.1.call-update) | async-done | bytes 2621456 | tf_op jit(solution)/shard_map/all_gather | solution.py:33
  320.7 3.0 multiply_add_fusion.1
  324.1 5.8 fusion.12
  330.0 2.8 multiply_reduce_fusion
  333.1 1.1 convolution_bitcast_fusion.2
  334.2 4.3 fusion.72
  338.5 43.3 %all-gather.21.cloned.1.call-done = f32[4,40,64,128]{3,2,1,0:T(8,128)} async-done(((f32[1,40,64,128]{3,2,1,0:T(8,128)}), f32[4,40,64,128]{3,2,1,0:T(8,128)}) %all-gather.21.cloned.1.call-update) | async-done | bytes 5242896 | tf_op jit(solution)/shard_map/all_gather | solution.py:33
  381.8 5.9 add_add_fusion
  387.7 2.3 fusion.56
  390.0 2.3 fusion.50
  392.3 1.1 fusion.70
  393.4 5.4 fusion.27
  399.0 1.1 reduce_window_sum.32
  400.2 0.9 fusion.105
  401.1 8.6 %convolution_bitcast_fusion = f32[1280,2856]{0,1:T(8,128)} fusion(bf16[1,128,1280]{2,1,0:T(8,128)(2,1)S(1)} %copy-done, f32[128,2560]{0,1:T(8,128)} %get-tuple-element.109, f32[128,128]{0,1:T(8,128)S(1)} %fusion.72, f32[128,128]{0,1:T(8,128)S(1)} %fusion.70, f32[128,40]{0,1:T(8,128)S(1)} %get-tuple-element.91), kind=kOutput, calls=%fused_computation | convolution fusion | flops 937316352 | bytes 16412672 | tf_op jit(solution)/shard_map/dot_general | solution.py:131
  409.9 6.8 %psum.35 = f32[3,40]{1,0:T(4,128)S(1)} all-reduce(f32[3,40]{1,0:T(4,128)S(1)} %pad_maximum_fusion), channel_id=1, replica_groups=mesh['seq_0'=4,'seq_1'=2,'seq_2'=2,'zero_0'=4,'zero_1'=2] {'seq_0'}, use_global_device_ids=true, to_apply=%region_15.16 | all-reduce | flops 120 | bytes 960 | tf_op jit(solution)/shard_map/psum | solution.py:44
  416.8 3.8 psum.36
  420.6 6.2 %psum.37 = f32[3,40]{1,0:T(4,128)S(1)} all-reduce(f32[3,40]{1,0:T(4,128)S(1)} %psum.36), channel_id=1, replica_groups=mesh['seq_0'=4,'seq_1'=2,'seq_2'=2,'zero_0'=4,'zero_1'=2] {'seq_2'}, use_global_device_ids=true, to_apply=%region_17.18 | all-reduce | flops 120 | bytes 960 | tf_op jit(solution)/shard_map/psum | solution.py:44
  426.8 9.4 %psum.38 = f32[3,40]{1,0:T(4,128)S(1)} all-reduce(f32[3,40]{1,0:T(4,128)S(1)} %psum.37), channel_id=1, replica_groups=mesh['seq_0'=4,'seq_1'=2,'seq_2'=2,'zero_0'=4,'zero_1'=2] {'zero_0'}, use_global_device_ids=true, to_apply=%region_18.19 | all-reduce | flops 120 | bytes 960 | tf_op jit(solution)/shard_map/psum | solution.py:44
  436.2 5.8 psum.39
  442.0 6.2 %fusion.10 = bf16[1,128,1280]{2,1,0:T(8,128)(2,1)} fusion(bf16[1280,2856]{1,0:T(8,128)(2,1)} %all-gather.13.cloned.1.call-done, f32[128,2560]{0,1:T(8,128)S(1)} %copy-done.17, f32[128,128]{0,1:T(8,128)S(1)} %fusion.72, f32[128,128]{0,1:T(8,128)S(1)} %fusion.70, f32[128,40]{0,1:T(8,128)S(1)} %get-tuple-element.91), kind=kOutput, calls=%fused_computation.15 | convolution fusion | flops 937480192 | bytes 9101312 | tf_op jit(solution)/shard_map/dot_general | solution.py:126
  448.3 136.5 %all-reduce.9.cloned.1.call-done = f32[1280,2856]{0,1:T(8,128)} async-done(((f32[1280,2856]{0,1:T(8,128)}), f32[1280,2856]{0,1:T(8,128)}) %all-reduce.9.cloned.1.call-update) | async-done | bytes 14622736
  584.8 2.3 constant_dynamic-slice_fusion
  587.0 1.1 copy.92
  (94 shorter events, 3.2 us)
Async XLA Ops:
  7.2 106.3 %copy-start = (bf16[1,128,1280]{2,1,0:T(8,128)(2,1)S(1)}, bf16[1,128,1280]{2,1,0:T(8,128)(2,1)}, u32[]{:S(2)}) copy-start(bf16[1,128,1280]{2,1,0:T(8,128)(2,1)} %param.6) | copy-start | bytes 983044
  7.2 1.1 copy-start.18
  7.2 1.5 copy-start.21
  7.2 106.2 %all-gather.13.cloned.1.call-start = ((), (), s32[]{:S(2)}) async-start(), calls=%async_computation | async-start | bytes 8478720 | tf_op jit(solution)/shard_map/all_gather | solution.py:96
  7.9 128.7 %all-gather.23.cloned.1.call-start = ((), (), s32[]{:S(2)}) async-start(), calls=%async_computation.5 | async-start | bytes 3932160 | tf_op jit(solution)/shard_map/all_gather | solution.py:33
  8.7 111.5 %copy-start.11 = (bf16[1,128,2560]{1,2,0:T(8,128)(2,1)}, bf16[1,128,2560]{1,2,0:T(8,128)(2,1)S(1)}, u32[]{:S(2)}) copy-start(bf16[1,128,2560]{1,2,0:T(8,128)(2,1)S(1)} %copy.77) | copy-start | bytes 1966084
  8.7 110.9 %copy-start.19 = (f32[40]{0:T(128)S(1)}, f32[40]{0:T(128)}, u32[]{:S(2)}) copy-start(f32[40]{0:T(128)} %param.9) | copy-start | bytes 484
  119.6 4.0 copy-start.14
  120.2 1.1 copy-start.7
  123.6 58.7 %all-gather.15.cloned.1.call-start = ((), (), s32[]{:S(2)}) async-start(), calls=%async_computation.1 | async-start | bytes 3932160 | tf_op jit(solution)/shard_map/all_gather | solution.py:33
  139.8 103.8 %all-gather.17.cloned.1.call-start = ((), (), s32[]{:S(2)}) async-start(), calls=%async_computation.2 | async-start | bytes 6553600 | tf_op jit(solution)/shard_map/all_gather | solution.py:33
  182.3 61.3 %copy-start.1 = (f32[80,64,128]{2,1,0:T(8,128)S(1)}, f32[80,64,128]{2,1,0:T(8,128)}, u32[]{:S(2)}) copy-start(f32[80,64,128]{2,1,0:T(8,128)} %all-gather.23.cloned.1.call-done) | copy-start | bytes 7864324
  185.6 89.6 %all-gather.25.cloned.1.call-start = ((), (), s32[]{:S(2)}) async-start(), calls=%async_computation.6 | async-start | bytes 3932160 | tf_op jit(solution)/shard_map/all_gather | solution.py:33
  243.6 5.1 copy-start.15
  248.8 1.3 copy-start.10
  248.8 1.6 copy-start.12
  248.8 1.6 copy-start.20
  250.0 3.5 copy-start.16
  255.4 1.1 copy-start.6
  256.5 1.1 copy-start.9
  259.9 60.8 %all-gather.19.cloned.1.call-start = ((), (), s32[]{:S(2)}) async-start(), calls=%async_computation.3 | async-start | bytes 3932160 | tf_op jit(solution)/shard_map/all_gather | solution.py:33
  278.2 103.6 %all-gather.21.cloned.1.call-start = ((), (), s32[]{:S(2)}) async-start(), calls=%async_computation.4 | async-start | bytes 6553600 | tf_op jit(solution)/shard_map/all_gather | solution.py:33
  323.7 261.1 %all-reduce.9.cloned.1.call-start = ((), (), s32[]{:S(2)}) async-start(), calls=%async_computation.7 | async-start | bytes 29245440
  330.0 3.1 copy-start.22
  381.8 5.9 copy-start.8
  381.8 8.2 %copy-start.13 = (bf16[1,128,2560]{1,2,0:T(8,128)(2,1)S(1)}, bf16[1,128,2560]{1,2,0:T(8,128)(2,1)}, u32[]{:S(2)}) copy-start(bf16[1,128,2560]{1,2,0:T(8,128)(2,1)} %copy-done.11) | copy-start | bytes 1966084
  381.8 11.6 %copy-start.4 = (f32[2,40,64,128]{3,2,1,0:T(8,128)S(1)}, f32[2,40,64,128]{3,2,1,0:T(8,128)}, u32[]{:S(2)}) copy-start(f32[2,40,64,128]{3,2,1,0:T(8,128)} %all-gather.19.cloned.1.call-done) | copy-start | bytes 7864324
  381.8 11.6 %copy-start.5 = (f32[4,40,64,128]{3,2,1,0:T(8,128)S(1)}, f32[4,40,64,128]{3,2,1,0:T(8,128)}, u32[]{:S(2)}) copy-start(f32[4,40,64,128]{3,2,1,0:T(8,128)} %all-gather.21.cloned.1.call-done) | copy-start | bytes 15728644
  387.7 5.7 copy-start.3
  390.0 2.3 copy-start.23
  390.0 3.4 copy-start.2
  409.7 32.3 %copy-start.17 = (f32[128,2560]{0,1:T(8,128)S(1)}, f32[128,2560]{0,1:T(8,128)}, u32[]{:S(2)}) copy-start(f32[128,2560]{0,1:T(8,128)} %get-tuple-element.109) | copy-start | bytes 3932164
Sparse Core Ops, SparseCore 0:
  10.3 103.0 all-gather.12
  123.7 12.8 all-gather.22
  139.9 42.3 all-gather.14
  185.7 57.8 all-gather.16
  260.0 15.1 all-gather.24
  278.3 42.3 all-gather.18
  323.8 57.8 all-gather.20
  409.8 174.8 all-reduce.8
where the time goes:
time: 596 us; the launch traced here: 595 us
  waiting for transfers between devices  441 us (74%)
  matrix products  47.9 us (8%)
  blocking collectives  45.9 us (8%)
  other arithmetic  36.4 us (6%)
  between operations  14.6 us (2%)
  local copies, waits for them, and re-layouts  8.46 us (1%)
    all_gather x6, waiting for transfers between devices, prefix_by_axis(): pieces = jax.tree.map(lambda part: lax.all_gather(part, axis), subtotal)  199 us
    unnamed x9, waiting for transfers between devices  137 us
    all_gather x1, waiting for transfers between devices, body(): gathered = lax.all_gather(input_weight, ZERO, axis=0, tiled=True)  105 us
    psum x5, blocking collectives, over_axes(): return functools.reduce(lax.psum, axes, x)  32.1 us
    add x6, other arithmetic, combine_states(): jnp.exp(later[0])[:, None, None] * earlier[1] + later[1]  23.4 us
    all_gather x3, blocking collectives, prefix_by_axis(): pieces = jax.tree.map(lambda part: lax.all_gather(part, axis), subtotal)  13.8 us
  transfers between devices with their start and end apart: 8, of which 8 were waited for; matrix products, arithmetic and copies ran while one was open for 4% of the time, Pallas kernels for 0%

commit v1 on v0

v1 whole, which is shorter than its diff:
```python
import functools

import jax
import jax.numpy as jnp
from jax import lax
from jax.experimental import pallas as pl
from jax.experimental.pallas import tpu as pltpu
from jax.sharding import Mesh
from jax.sharding import PartitionSpec as P

HEADS = 40
STATE = 128
INNER = 2560
D = 1280
COLS = 640
ZERO = ("zero_0", "zero_1")
SEQ = ("seq_0", "seq_1", "seq_2")
SEQ_ZERO = ("seq_0", "seq_1", "seq_2", "zero_0", "zero_1")
MESH = pl.DeviceIdType.MESH
F32 = jnp.float32
BF16 = jnp.bfloat16
highest = lax.Precision.HIGHEST
NN = (((1,), (0,)), ((), ()))
NT = (((1,), (1,)), ((), ()))
TN = (((0,), (0,)), ((), ()))


def mm(a, b, dims=NN, precision=None):
    return lax.dot_general(a, b, dims, preferred_element_type=F32, precision=precision)


def ds(start, size, align=None):
    return pl.ds(pl.multiple_of(start, align or size), size)


def silu_grad(v):
    sig = jax.nn.sigmoid(v)
    return sig * (1.0 + v * (1.0 - sig))


def kernel(
    hid_ref, cot_ref, w_ref, par_ref,
    hg_ref, wg_ref, hd_ref,
    hidf, hidt, cot, wf, proj, bmf, cmf, stp, lgd, cums, sexp, ecs, tls, vv, xb, xt, oe, tot,
    sl, dl, stt, tts, str_, ttr, q1s, dxin, dbf, dcf, sb, db, dd, ipr, rr, rdt, gacc,
    t1s, t1r, t1d, t1dr, t2s, t2r, shr, hgp, hgs, hgr,
    dwa, dwb, sa1, ra1p, ra1m, sa2p, sa2m, ra2p, ra2m,
    sa3, ra3, sa4, ra4, sd, rd, heads_y, heads_x, heads_z, heads_g,
    ss, rs, ls,
):
    y, zl, c = (lax.axis_index(n) for n in SEQ)
    x, zh = (lax.axis_index(n) for n in ZERO)
    r = zl * 2 + c
    a = lax.rem(zl + zh, 2)
    g = a * 2 + c
    pending = []

    def send(i, src, dst, where, recv=None):
        copy = pltpu.make_async_remote_copy(
            src_ref=src, dst_ref=dst, send_sem=ss.at[i], recv_sem=rs.at[i if recv is None else recv],
            device_id=where, device_id_type=MESH,
        )
        copy.start()
        pending.append(copy)
        return copy

    def rank(k):
        zlk = lax.rem(zl + k // 2, 2)
        ck = lax.rem(c + k % 2, 2)
        return zlk, ck, {"seq_1": zlk, "seq_2": ck}

    def xdev(k):
        return {"zero_0": lax.rem(x + k + 4, 4)}

    def ydev(k):
        return {"seq_0": lax.rem(y + k + 4, 4)}

    zpair = {"seq_1": 1 - zl, "zero_1": 1 - zh}
    core = {"seq_2": 1 - c}

    def shard(xk, zk):
        return ds((lax.rem(xk + 4, 4) * 2 + zk) * 160, 160)

    mine = ds(r * 128, 128)
    own = shard(x, zh)
    other = shard(x, 1 - zh)
    w_z = send(6, w_ref, wf.at[own, :], zpair)
    w_p = send(7, w_ref, wf.at[own, :], xdev(1))
    w_m = send(8, w_ref, wf.at[own, :], xdev(-1))
    h_z = send(1, hid_ref, hidf.at[mine, :], rank(2)[2])
    h_c = send(0, hid_ref, hidf.at[mine, :], core)
    cots = []
    for k in (2, 3, 1):
        zlk, ck, dev = rank(k)
        gk = lax.rem(zlk + zh, 2) * 2 + ck
        cots.append(send(2 + k, cot_ref.at[:, ds(gk * COLS, COLS)], cot.at[mine, :], dev))
    local = [
        pltpu.make_async_copy(w_ref, wf.at[own, :], ls.at[0]),
        pltpu.make_async_copy(hid_ref, hidf.at[mine, :], ls.at[1]),
        pltpu.make_async_copy(cot_ref.at[:, ds(g * COLS, COLS)], cot.at[mine, :], ls.at[2]),
    ]
    for copy in local:
        copy.start()
    w_z.wait_recv()
    w_zp = send(9, wf.at[other, :], wf.at[other, :], xdev(1))
    w_zm = send(10, wf.at[other, :], wf.at[other, :], xdev(-1))
    h_z.wait_recv()
    zrows = ds((rank(2)[0] * 2 + c) * 128, 128)
    h_f = send(2, hidf.at[zrows, :], hidf.at[zrows, :], core)
    half = 512
    w_p.wait_recv()
    piece = wf.at[shard(x - 1, zh), 0:half]
    f1 = send(11, piece, piece, xdev(1))
    w_m.wait_recv()
    piece = wf.at[shard(x + 1, zh), half:1024]
    f2 = send(12, piece, piece, xdev(-1))
    for copy in local:
        copy.wait()
    h_c.wait_recv()
    h_f.wait_recv()
    for copy in cots:
        copy.wait_recv()

    def turn(i, carry):
        hidt[:, ds(i * 128, 128)] = hidf[ds(i * 128, 128), :].T
        return carry

    lax.fori_loop(0, 4, turn, 0)
    w_zp.wait_recv()
    piece = wf.at[shard(x - 1, 1 - zh), 0:half]
    f3 = send(13, piece, piece, xdev(1))
    w_zm.wait_recv()
    piece = wf.at[shard(x + 1, 1 - zh), half:1024]
    f4 = send(14, piece, piece, xdev(-1))
    for copy in (f1, f2, f3, f4):
        copy.wait_recv()

    rowi = lax.broadcasted_iota(jnp.int32, (128, 128), 0)
    coli = lax.broadcasted_iota(jnp.int32, (128, 128), 1)
    low = coli < 64
    causal = rowi >= coli
    anti = rowi <= coli
    tri = causal.astype(F32)
    upper = anti.astype(F32)
    strict = (rowi > coli).astype(F32)
    bias = par_ref[0:1, :]
    neg = -jnp.exp(par_ref[1:2, :])
    skip = par_ref[2:3, :]

    def pair(v, j, width=128):
        return jnp.where(low[0 : v.shape[0]], v[:, 2 * j : 2 * j + 1], v[:, 2 * j + 1 : 2 * j + 2])

    def forward(b, carry):
        rows = ds(b * 128, 128)
        p = mm(hidf[rows, :], wf[...])
        proj[rows, :] = p
        bm = jax.nn.silu(p[:, 640:768])
        cm = jax.nn.silu(p[:, 768:896])
        bmf[rows, :] = bm
        cmf[rows, :] = cm
        pre = p[:, 896:1024] + bias
        step = jnp.maximum(pre, 0.0) + jnp.log1p(jnp.exp(-jnp.abs(pre)))
        lg = neg * step
        cum = mm(tri, lg, NN, highest)
        stp[rows, :] = step
        lgd[rows, :] = lg
        cums[rows, :] = cum
        for j in range(5):
            cj = slice(128 * j, 128 * j + 128)
            ce = pair(cum, j)
            se = pair(step, j)
            ec = jnp.exp(ce)
            tl = jnp.exp(ce[127:128, :] - ce)
            val = jax.nn.silu(proj[rows, cj])
            xs = val * se
            sexp[rows, cj] = se
            ecs[rows, cj] = ec
            tls[rows, cj] = tl
            vv[rows, cj] = val
            xb[rows, cj] = xs.astype(BF16)
            xt[rows, cj] = (xs * tl).astype(BF16)
            oe[rows, cj] = (cot[rows, cj].astype(F32) * ec).astype(BF16)
            tot[ds(b * 8, 8), cj] = jnp.broadcast_to(ce[127:128, :], (8, 128))
        sl[b] = mm(bm.astype(BF16), xt[rows, :], TN)
        dl[b] = mm(cm.astype(BF16), oe[rows, :], TN)
        return carry

    lax.fori_loop(0, 4, forward, 0)

    def total(b, cj):
        return tot[8 * b : 8 * b + 1, cj]

    for j in range(5):
        cj = slice(128 * j, 128 * j + 128)
        s = sl[0, :, cj]
        d = dl[3, :, cj]
        for b in range(1, 4):
            s = jnp.exp(total(b, cj)) * s + sl[b, :, cj]
            d = jnp.exp(total(3 - b, cj)) * d + dl[3 - b, :, cj]
        stt[0, :, cj] = s.astype(BF16)
        stt[1, :, cj] = d.astype(BF16)
    tts[...] = tot[0:8, :] + tot[8:16, :] + tot[16:24, :] + tot[24:32, :]
    states = []
    for k in (1, 2, 3):
        wraps = lax.div(y + k, 4)
        states.append(send(14 + k, stt.at[wraps], str_.at[k - 1], ydev(k)))
        states.append(send(17 + k, tts, ttr.at[k - 1], ydev(k)))

    def inside(b, carry):
        rows = ds(b * 128, 128)
        bm = bmf[rows, :]
        cm = cmf[rows, :]
        scores = mm(cm, bm, NT, highest)
        scores_t = scores.T
        cum = cums[rows, :]
        cum_t = cum.T
        ds_ = jnp.zeros((128, 128), F32)
        for j in range(5):
            cj = slice(128 * j, 128 * j + 128)
            c0, c1 = cum[:, 2 * j : 2 * j + 1], cum[:, 2 * j + 1 : 2 * j + 2]
            r0, r1 = cum_t[2 * j : 2 * j + 1, :], cum_t[2 * j + 1 : 2 * j + 2, :]
            w0 = jnp.where(causal, jnp.exp(jnp.where(causal, c0 - r0, 0.0)), 0.0)
            w1 = jnp.where(causal, jnp.exp(jnp.where(causal, c1 - r1, 0.0)), 0.0)
            u0 = jnp.where(anti, jnp.exp(jnp.where(anti, r0 - c0, 0.0)), 0.0)
            u1 = jnp.where(anti, jnp.exp(jnp.where(anti, r1 - c1, 0.0)), 0.0)
            m = jnp.concatenate([scores * w0, scores * w1], axis=1).astype(BF16)
            mt = jnp.concatenate([scores_t * u0, scores_t * u1], axis=1).astype(BF16)
            x16 = xb[rows, cj]
            o16 = cot[rows, cj]
            zero = jnp.zeros_like(x16)
            xd = jnp.concatenate([jnp.where(low, x16, zero), jnp.where(low, zero, x16)], axis=0)
            od = jnp.concatenate([jnp.where(low, o16, zero), jnp.where(low, zero, o16)], axis=0)
            yy = mm(m, xd)
            pp = mm(o16, xd, NT)
            dx = mm(mt, od)
            ds_ = ds_ + w0 * pp[:, 0:128] + w1 * pp[:, 128:256]
            dxin[rows, cj] = dx
            q1s[rows, cj] = o16.astype(F32) * yy - x16.astype(F32) * dx
        dcf[rows, :] = mm(ds_, bm, NN, highest)
        dbf[rows, :] = mm(ds_, cm, TN, highest)
        return carry

    lax.fori_loop(0, 4, inside, 0)
    for copy in states:
        copy.wait_recv()

    lanes = lax.broadcasted_iota(jnp.int32, (256, 128), 0)
    outl = lax.broadcasted_iota(jnp.int32, (256, 128), 1)

    def sums(z, j):
        hi = z.astype(BF16)
        lo = (z - hi.astype(F32)).astype(BF16)
        pick = (outl == 2 * j + lax.rem(lax.div(lanes, 64), 2)).astype(F32).astype(BF16)
        return mm(jnp.concatenate([hi, lo], axis=1), pick)

    yes = [jnp.where(y >= k, 1.0, 0.0).astype(F32) for k in (1, 2, 3)]
    no = [jnp.where(y + k <= 3, 1.0, 0.0).astype(F32) for k in (1, 2, 3)]
    inner = [jnp.zeros((8, 128), F32) for _ in range(4)]
    for j in range(5):
        cj = slice(128 * j, 128 * j + 128)
        t = [ttr[k, 0:1, cj] for k in range(3)]
        got = [str_[k, :, cj].astype(F32) for k in range(3)]
        s = yes[0] * got[0] + (yes[1] * jnp.exp(t[0])) * got[1] + (yes[2] * jnp.exp(t[0] + t[1])) * got[2]
        d = no[0] * got[2] + (no[1] * jnp.exp(t[2])) * got[1] + (no[2] * jnp.exp(t[2] + t[1])) * got[0]
        for b in (3, 2, 1, 0):
            db[b, :, cj] = d.astype(BF16)
            dd[b] = d
            d = jnp.exp(total(b, cj)) * d + dl[b, :, cj]
        for b in range(4):
            sb[b, :, cj] = s.astype(BF16)
            grown = jnp.exp(total(b, cj)) * s
            inner[b] = inner[b] + sums((grown * dd[b]).reshape(16, 8, 128).sum(axis=0), j)
            s = grown + sl[b, :, cj]
    for b in range(4):
        ipr[8 * b : 8 * b + 8, :] = jnp.broadcast_to(inner[b].sum(axis=0, keepdims=True), (8, 128))

    gacc[...] = jnp.zeros_like(gacc)
    ownl = coli < 10

    def outside(b, carry):
        bias_sum, decay_sum = carry
        rows = ds(b * 128, 128)
        b16 = bmf[rows, :].astype(BF16)
        c16 = cmf[rows, :].astype(BF16)
        red = jnp.zeros((384, 128), F32)
        for j in range(5):
            cj = slice(128 * j, 128 * j + 128)
            o = cot[rows, cj].astype(F32)
            yst = mm(c16, sb[b, :, cj]) * ecs[rows, cj]
            dxst = mm(b16, db[b, :, cj]) * tls[rows, cj]
            se = sexp[rows, cj]
            val = vv[rows, cj]
            dxs = dxin[rows, cj] + dxst
            z = jnp.concatenate([q1s[rows, cj] + o * yst, xb[rows, cj].astype(F32) * dxst, dxs * val], axis=0)
            red = red + sums(z, j)
            dval = dxs * se + pair(skip, j) * o
            rr[rows, cj] = (dval * silu_grad(proj[rows, cj])).astype(BF16)
            gacc[:, cj] = gacc[:, cj] + (o * val).reshape(16, 8, 128).sum(axis=0)
        dcf[rows, :] = dcf[rows, :] + mm(oe[rows, :], sb[b], NT)
        dbf[rows, :] = dbf[rows, :] + mm(xt[rows, :], db[b], NT)
        dlog = mm(upper, red[0:128], NN, highest) + mm(strict, red[128:256], NN, highest)
        dlog = dlog + ipr[ds(b * 8, 8), :][0:1, :]
        dlog = jnp.where(ownl, dlog, 0.0)
        ddt = (red[256:384] + neg * dlog) * jax.nn.sigmoid(proj[rows, 896:1024] + bias)
        ddt = jnp.where(ownl, ddt, 0.0)
        rdt[rows, :] = ddt.astype(BF16)
        bias_sum = bias_sum + ddt.reshape(16, 8, 128).sum(axis=0)
        decay_sum = decay_sum + (dlog * lgd[rows, :]).reshape(16, 8, 128).sum(axis=0)
        return bias_sum, decay_sum

    zero8 = jnp.zeros((8, 128), F32)
    bias_sum, decay_sum = lax.fori_loop(0, 4, outside, (zero8, zero8))
    gain_sum = zero8
    for j in range(5):
        gain_sum = gain_sum + sums(gacc[:, 128 * j : 128 * j + 128], j)
    row8 = lax.broadcasted_iota(jnp.int32, (8, 128), 0)
    packed = jnp.where(
        row8 == 0, bias_sum.sum(axis=0, keepdims=True),
        jnp.where(row8 == 1, decay_sum.sum(axis=0, keepdims=True),
                  jnp.where(row8 == 2, gain_sum.sum(axis=0, keepdims=True), 0.0)),
    )
    place = jnp.where(jnp.logical_and(rowi < 10, coli == rowi + 10 * g), 1.0, 0.0).astype(F32)
    heads_y[y] = mm(packed, place, NN, highest)
    head_y = [send(50 + k, heads_y.at[y], heads_y.at[y], ydev(k)) for k in (1, 2, 3)]

    first = c == 0
    spread = mm(rdt[...], place.astype(BF16)).astype(BF16)
    t1d[...] = spread
    t1s[...] = jnp.where(first, dcf[...], dbf[...])
    t1 = [send(21, t1s, t1r, core), send(22, t1d, t1dr, core)]

    def weights(target, lo, hi):
        def step(i, carry):
            rows = ds(i * 320, 320)
            target[rows, :] = mm(hidt[rows, :], rr[:, lo:hi])
            return carry

        lax.fori_loop(0, 4, step, 0)

    def ring_first(n, target, index, dev):
        far = ds(lax.rem(index + 2, 4) * 320, 320)
        sa1[n] = target[far, :].astype(BF16)
        return (
            send(24 + 4 * n, sa1.at[n, 0:160, :], ra1p.at[n], dev(1)),
            send(25 + 4 * n, sa1.at[n, 160:320, :], ra1m.at[n], dev(-1)),
        )

    def ring_second(n, target, index, dev, firsts):
        nxt = lax.rem(index + 1, 4) * 320
        prv = lax.rem(index + 3, 4) * 320
        firsts[0].wait_recv()
        sa2p[n, 0:160, :] = (target[ds(nxt, 160, 160), :] + ra1p[n].astype(F32)).astype(BF16)
        sa2p[n, 160:320, :] = target[ds(nxt + 160, 160, 160), :].astype(BF16)
        up = send(26 + 4 * n, sa2p.at[n], ra2p.at[n], dev(1))
        firsts[1].wait_recv()
        sa2m[n, 0:160, :] = target[ds(prv, 160, 160), :].astype(BF16)
        sa2m[n, 160:320, :] = (target[ds(prv + 160, 160, 160), :] + ra1m[n].astype(F32)).astype(BF16)
        down = send(27 + 4 * n, sa2m.at[n], ra2m.at[n], dev(-1))
        return up, down

    def second_stage(n, target, index, seconds, other_index, dev):
        for copy in seconds:
            copy.wait_recv()
        here = ds(index * 320, 320)
        summed = target[here, :] + ra2p[n].astype(F32) + ra2m[n].astype(F32)
        target[here, :] = summed
        sa3[n] = summed.astype(BF16)
        return [
            send(31 + 3 * n + k, sa3.at[n, ds(lax.rem(other_index + k, 4) * 80, 80), :], ra3.at[n, k - 1], dev(k))
            for k in (1, 2, 3)
        ]

    def third_stage(n, target, index, other_index, thirds):
        for copy in thirds:
            copy.wait_recv()
        rows = ds(index * 320 + other_index * 80, 80)
        sa4[n] = target[rows, :] + ra3[n, 0].astype(F32) + ra3[n, 1].astype(F32) + ra3[n, 2].astype(F32)
        return send(38 + n, sa4.at[n, ds((1 - zh) * 40, 40), :], ra4.at[n], zpair)

    weights(dwa, 0, 384)
    a1 = ring_first(0, dwa, y, ydev)
    for copy in t1:
        copy.wait_recv()
    mixed = jnp.where(first, dbf[...], dcf[...]) + t1r[...]
    dt2 = spread.astype(F32) + t1dr[...].astype(F32)
    north = a == 0
    t2s[...] = jnp.where(north, dt2, mixed).astype(BF16)
    t2 = send(23, t2s, t2r, rank(2)[2])

    def token(i, carry):
        rows = ds(i * 128, 128)
        hgp[rows, :] = mm(rr[rows, 0:640], wf[:, 0:640], NT) + mm(rdt[rows, :], wf[:, 896:1024], NT)
        return carry

    lax.fori_loop(0, 4, token, 0)
    a2 = ring_second(0, dwa, y, ydev, a1)
    t2.wait_recv()
    came = t2r[...].astype(F32)
    tile = proj[:, ds(640 + 128 * c, 128)]
    upper_pick = ((mixed + came) * silu_grad(tile)).astype(BF16).astype(F32)
    lower_pick = jnp.where(first, dt2 + came, 0.0)
    rr[:, 640:768] = jnp.where(north, upper_pick, lower_pick).astype(BF16)
    shr[...] = jnp.where(north, upper_pick, 0.0).astype(BF16)
    weights(dwb, 384, 768)
    b1 = ring_first(1, dwb, x, xdev)

    def shared(i, carry):
        rows = ds(i * 128, 128)
        hgp[rows, :] = hgp[rows, :] + mm(shr[rows, :], wf[:, ds(640 + 128 * c, 128)], NT)
        return carry

    lax.fori_loop(0, 4, shared, 0)
    hgc = []
    for k in (2, 3, 1):
        zlk, ck, dev = rank(k)
        hgs[k - 1] = hgp[ds((zlk * 2 + ck) * 128, 128), :].astype(BF16)
        hgc.append(send(47 + k, hgs.at[k - 1], hgr.at[k - 1], dev))
    b2 = ring_second(1, dwb, x, xdev, b1)
    a3 = second_stage(0, dwa, y, a2, x, xdev)
    for copy in head_y:
        copy.wait_recv()
    heads_x[x] = (heads_y[0] + heads_y[1]) + (heads_y[2] + heads_y[3])
    head_x = [send(53 + k, heads_x.at[x], heads_x.at[x], xdev(k)) for k in (1, 2, 3)]
    b3 = second_stage(1, dwb, x, b2, y, ydev)
    a4 = third_stage(0, dwa, y, x, a3)
    for copy in head_x:
        copy.wait_recv()
    heads_z[zh] = (heads_x[0] + heads_x[1]) + (heads_x[2] + heads_x[3])
    head_z = send(57, heads_z.at[zh], heads_z.at[zh], zpair)
    b4 = third_stage(1, dwb, x, y, b3)

    pick = lax.div(x, 2)
    part = lax.rem(x, 2) * 2 + zh
    to_me = [
        jnp.logical_and(x == r, zh == pick),
        jnp.logical_and(jnp.logical_and(x == y, y == r), zh == pick),
    ]
    moves = []

    def last(n, fourth, outer, inner_index):
        fourth.wait_recv()
        chunk = sa4[n, ds(zh * 40, 40), :] + ra4[n]
        for i in range(4):
            sd[n, i, 0:10, :] = chunk[10 * i : 10 * i + 10, :]
            dev = {
                "seq_0": outer,
                "seq_1": lax.div(inner_index, 2),
                "seq_2": lax.rem(inner_index, 2),
                "zero_0": zh * 2 + i // 2,
                "zero_1": jnp.int32(i % 2),
            }
            copy = pltpu.make_async_remote_copy(
                src_ref=sd.at[n, i], dst_ref=rd.at[n, g], send_sem=ss.at[40 + 4 * n + i],
                recv_sem=rs.at[40 + 4 * n + g], device_id=dev, device_id_type=MESH,
            )
            keep = jnp.logical_and(to_me[n], part == i)

            @pl.when(jnp.logical_not(keep))
            def _():
                copy.start()

            @pl.when(keep)
            def _():
                rd[n, g] = sd[n, i]

            moves.append((copy, keep))

    last(0, a4, y, x)
    head_z.wait_recv()
    heads_g[r] = heads_z[0] + heads_z[1]
    head_g = [send(57 + k, heads_g.at[r], heads_g.at[r], rank(k)[2]) for k in (1, 2, 3)]
    last(1, b4, x, y)
    for copy in hgc:
        copy.wait_recv()
    out = hgp[mine, :] + hgr[0].astype(F32) + hgr[1].astype(F32) + hgr[2].astype(F32)
    hg_ref[...] = out.astype(BF16)
    for copy in head_g:
        copy.wait_recv()
    hd_ref[...] = (heads_g[0] + heads_g[1]) + (heads_g[2] + heads_g[3])
    for n in range(2):
        for k in range(4):
            copy = pltpu.make_async_remote_copy(
                src_ref=sd.at[n, 0], dst_ref=rd.at[n, k], send_sem=ss.at[40 + 4 * n],
                recv_sem=rs.at[40 + 4 * n + k], device_id=core, device_id_type=MESH,
            )

            @pl.when(jnp.logical_not(jnp.logical_and(to_me[n], g == k)))
            def _():
                copy.wait_recv()

    for k in range(4):
        wg_ref[:, 640 * k : 640 * k + 384] = rd[0, k, 0:10, :]
        wg_ref[:, 640 * k + 384 : 640 * k + 640] = rd[1, k, 0:10, 0:256]
    wg_ref[:, 2560:2688] = rd[1, 0, 0:10, 256:384]
    wg_ref[:, 2688:2816] = rd[1, 1, 0:10, 256:384]
    wg_ref[:, 2816:2856] = rd[1, 2, 0:10, 256:296]
    for copy in pending:
        copy.wait_send()
    for copy, keep in moves:

        @pl.when(jnp.logical_not(keep))
        def _():
            copy.wait_send()


def scratch():
    def v(shape, dtype=F32):
        return pltpu.VMEM(shape, dtype)

    return [
        v((512, D), BF16), v((D, 512), BF16), v((512, COLS), BF16), v((D, 1024), BF16), v((512, 1024)),
        v((512, 128)), v((512, 128)), v((512, 128)), v((512, 128)), v((512, 128)),
        v((512, COLS)), v((512, COLS)), v((512, COLS)), v((512, COLS)),
        v((512, COLS), BF16), v((512, COLS), BF16), v((512, COLS), BF16), v((32, COLS)),
        v((4, 128, COLS)), v((4, 128, COLS)), v((2, 128, COLS), BF16), v((8, COLS)),
        v((3, 128, COLS), BF16), v((3, 8, COLS)),
        v((512, COLS)), v((512, COLS)), v((512, 128)), v((512, 128)),
        v((4, 128, COLS), BF16), v((4, 128, COLS), BF16), v((4, 128, 128)), v((32, 128)),
        v((512, 768), BF16), v((512, 128), BF16), v((8, COLS)),
        v((512, 128)), v((512, 128)), v((512, 128), BF16), v((512, 128), BF16),
        v((512, 128), BF16), v((512, 128), BF16), v((512, 128), BF16),
        v((512, D)), v((3, 128, D), BF16), v((3, 128, D), BF16),
        v((D, 384)), v((D, 384)), v((2, 320, 384), BF16), v((2, 160, 384), BF16), v((2, 160, 384), BF16),
        v((2, 320, 384), BF16), v((2, 320, 384), BF16), v((2, 320, 384), BF16), v((2, 320, 384), BF16),
        v((2, 320, 384), BF16), v((2, 3, 80, 384), BF16), v((2, 80, 384)), v((2, 40, 384)),
        v((2, 4, 16, 384)), v((2, 4, 16, 384)),
        v((4, 8, 128)), v((4, 8, 128)), v((2, 8, 128)), v((4, 8, 128)),
        pltpu.SemaphoreType.DMA((64,)), pltpu.SemaphoreType.DMA((64,)), pltpu.SemaphoreType.DMA((4,)),
    ]


def body(hidden, output_grad, input_weight, step_bias, decay_log, skip_gain):
    zl, c = lax.axis_index("seq_1"), lax.axis_index("seq_2")
    zh = lax.axis_index("zero_1")
    g = lax.rem(zl + zh, 2) * 2 + c
    w = jnp.concatenate(
        [
            lax.dynamic_slice(input_weight, (0, g * COLS), (160, COLS)),
            input_weight[:, INNER : INNER + 2 * STATE],
            lax.dynamic_slice(input_weight, (0, INNER + 2 * STATE + 10 * g), (160, 10)),
            jnp.zeros((160, 118), BF16),
        ],
        axis=1,
    )
    own = lax.dynamic_slice(jnp.stack([step_bias, decay_log, skip_gain]), (0, 10 * g), (3, 10))
    par = jnp.pad(own, ((0, 5), (0, 118)))
    anyspace = pl.BlockSpec(memory_space=pl.ANY)
    vmem = pl.BlockSpec(memory_space=pltpu.VMEM)
    hg, wg, hd = pl.pallas_call(
        kernel,
        out_shape=(
            jax.ShapeDtypeStruct((128, D), BF16),
            jax.ShapeDtypeStruct((10, 2856), F32),
            jax.ShapeDtypeStruct((8, 128), F32),
        ),
        in_specs=[anyspace, anyspace, anyspace, vmem],
        out_specs=(vmem, vmem, vmem),
        scratch_shapes=scratch(),
        compiler_params=pltpu.CompilerParams(has_side_effects=True, vmem_limit_bytes=64000000),
    )(hidden[0], output_grad[0], w, par)
    return (hg[None], wg, hd[0:3, 0:HEADS])


def solution(mesh):
    torus = Mesh(
        mesh.devices.reshape(4, 2, 2, 4, 2), ("seq_0", "seq_1", "seq_2", "zero_0", "zero_1")
    )
    in_specs = (P(ZERO, SEQ, None), P(ZERO, SEQ, None), P(ZERO, None), P(), P(), P())
    out_specs = (P(ZERO, SEQ, None), P(SEQ_ZERO, None), P())
    return jax.shard_map(body, mesh=torus, in_specs=in_specs, out_specs=out_specs, check_vma=False)
```

time: 596 us -> 105 us (0.18)
  the two profiles are of different devices: /device:TPU:1 before, /device:TPU:38 now
where the time goes in v1:
time: 105 us
  Pallas kernels  96.3 us (92%)
  local copies, waits for them, and re-layouts  6.98 us (7%)
    pallas_call x1, Pallas kernels, body(): pl.pallas_call(kernel, out_shape=(jax.ShapeDtypeStruct((128, D), BF16), j...  96.3 us
    unnamed x12, local copies, waits for them, and re-layouts  3.68 us

profile of v1, /device:TPU:38, one launch (start us, length us, event | category | flops | bytes accessed | tf_op | source)
XLA Modules:
  0.0 104.8 jit_solution(4677033503401880562)
XLA Ops:
  0.7 0.0 copy-start.2
  0.7 0.0 copy-start.3
  0.7 0.0 copy-start.4
  0.7 0.1 pad.11.clone
  0.8 0.5 copy-done.2
  1.3 0.0 copy-done.3
  1.3 0.0 copy-done.4
  1.4 0.1 constant_dynamic-slice_fusion
  1.4 0.6 pad.4.par_ref
  2.0 0.9 constant_dynamic-slice_fusion.1
  2.9 0.0 slice-start
  2.9 1.1 %constant_dynamic-slice_fusion.2 = bf16[160,640]{1,0:T(8,128)(2,1)S(1)} fusion(bf16[160,2856]{1,0:T(8,128)(2,1)} %param.8, s32[]{:T(128)S(6)} %select_n.9), kind=kLoop, calls=%fused_computation.4 | loop fusion | bytes 409604 | tf_op jit(solution)/shard_map/dynamic_slice | solution.py:538
  4.0 0.0 slice-done
  4.0 0.8 maximum_maximum_fusion.w_ref
  4.8 96.3 %shard_map.85 = (bf16[128,1280]{1,0:T(8,128)(2,1)}, f32[10,2856]{1,0:T(8,128)}, f32[8,128]{1,0:T(8,128)}) custom-call(bf16[128,1280]{1,0:T(8,128)(2,1)} %bitcast.7, bf16[128,2560]{1,0:T(8,128)(2,1)} %bitcast.6, bf16[160,1024]{1,0:T(8,128)(2,1)} %maximum_maximum_fusion.w_ref, f32[8,128]{1,0:T(8,128)} %pad.4.par_ref), custom_call_target="tpu_custom_call" | custom-call | tf_op jit(solution)/shard_map/pallas_call | solution.py:549
  101.1 0.0 copy-start.1
  101.1 0.7 copy-done.1
  101.8 0.6 slice.7
  102.3 0.0 copy-start
  102.3 1.8 %copy.11 = bf16[1,128,1280]{2,1,0:T(8,128)(2,1)} copy(bf16[1,128,1280]{2,1,0:T(8,128)(2,1)} %bitcast.8) | data formatting | bytes 655360
  104.1 0.0 copy-done
  104.1 0.7 copy.12
  (2 shorter events, 0.0 us)
Async XLA Ops:
  0.7 0.7 copy-start.2
  0.7 0.7 copy-start.3
  0.7 0.7 copy-start.4
  2.9 1.1 %slice-start = ((bf16[160,2856]{1,0:T(8,128)(2,1)}), bf16[160,256]{1,0:T(8,128)(2,1)S(1)}, s32[]{:S(2)}) async-start(bf16[160,2856]{1,0:T(8,128)(2,1)} %param.8), calls=%async_computation | async-start | bytes 163840 | tf_op jit(solution)/shard_map/slice | solution.py:539
  101.1 0.7 copy-start.1
  102.3 1.8 %copy-start = (f32[10,2856]{1,0:T(8,128)S(1)}, f32[10,2856]{1,0:T(8,128)}, u32[]{:S(2)}) copy-start(f32[10,2856]{1,0:T(8,128)} %get-tuple-element.13) | copy-start | bytes 342724

commit v2 on v0

v2 whole, which is shorter than its diff:
```python
import functools

import jax
import jax.numpy as jnp
from jax import lax
from jax.experimental import pallas as pl
from jax.experimental.pallas import tpu as pltpu
from jax.sharding import Mesh
from jax.sharding import PartitionSpec as P

HEADS = 40
STATE = 128
INNER = 2560
D = 1280
COLS = 640
ZERO = ("zero_0", "zero_1")
SEQ = ("seq_0", "seq_1", "seq_2")
SEQ_ZERO = ("seq_0", "seq_1", "seq_2", "zero_0", "zero_1")
MESH = pl.DeviceIdType.MESH
F32 = jnp.float32
BF16 = jnp.bfloat16
highest = lax.Precision.HIGHEST
NN = (((1,), (0,)), ((), ()))
NT = (((1,), (1,)), ((), ()))
TN = (((0,), (0,)), ((), ()))


def mm(a, b, dims=NN, precision=None):
    return lax.dot_general(a, b, dims, preferred_element_type=F32, precision=precision)


def ds(start, size, align=None):
    return pl.ds(pl.multiple_of(start, align or size), size)


def silu_grad(v):
    sig = jax.nn.sigmoid(v)
    return sig * (1.0 + v * (1.0 - sig))


def kernel(
    hid_ref, cot_ref, w_ref, bias_ref, decay_ref, skip_ref,
    hg_ref, wg_ref, hd_ref,
    hidf, hidt, cot, wraw, wf, projs, projv, bmf, cmf, lgd, cums, cumt, stp, gs, gts, dgs,
    sexp, ecs, tls, vv, xb, xt, oe, tot,
    sl, dl, stt, tts, str_, ttr, q1s, dxin, dbf, dcf, sb, db, dd, red,
    rr, rdt, t1s, t1r, t1d, t1dr, t2s, t2r, shr, hgp, hgs, hgr,
    dwa, sa1, ra1p, ra1m, sa2p, sa2m, ra2p, ra2m, sa3, ra3, sa4, ra4, sd, rd,
    dwb, sb1, rb1p, rb1m, sb2p, sb2m, rb2p, rb2m, sb3, rb3, sb4, rb4, sdb, rdb,
    dwc, sc1, rc1p, rc1m, sc2p, sc2m, rc2p, rc2m, sc3, rc3, sc4, rc4, sdc, rdc,
    heads_y, heads_x, heads_z, heads_g,
    ss, rs, ls,
):
    y, zl, c = (lax.axis_index(n) for n in SEQ)
    x, zh = (lax.axis_index(n) for n in ZERO)
    r = zl * 2 + c
    a = lax.rem(zl + zh, 2)
    g = a * 2 + c
    pending = []

    def send(i, src, dst, where):
        copy = pltpu.make_async_remote_copy(
            src_ref=src, dst_ref=dst, send_sem=ss.at[i], recv_sem=rs.at[i],
            device_id=where, device_id_type=MESH,
        )
        copy.start()
        pending.append(copy)
        return copy

    def rank(k):
        zlk = lax.rem(zl + k // 2, 2)
        ck = lax.rem(c + k % 2, 2)
        return zlk, ck, {"seq_1": zlk, "seq_2": ck}

    def xdev(k):
        return {"zero_0": lax.rem(x + k + 4, 4)}

    def ydev(k):
        return {"seq_0": lax.rem(y + k + 4, 4)}

    zpair = {"seq_1": 1 - zl, "zero_1": 1 - zh}
    core = {"seq_2": 1 - c}
    here_id = ds(r * 128, 128)

    def shard(xk, zk, lo=0, size=160):
        return ds((lax.rem(xk + 4, 4) * 2 + zk) * 160 + lo, size, 16)

    own = shard(x, zh)
    lane0 = 640 + 256 * c
    local = [
        pltpu.make_async_copy(w_ref, wraw, ls.at[0]),
        pltpu.make_async_copy(w_ref.at[:, ds(g * COLS, COLS, 128)], wf.at[own, 0:640], ls.at[1]),
        pltpu.make_async_copy(w_ref.at[:, ds(2560 + 128 * c, 128)], wf.at[own, ds(lane0, 128)], ls.at[2]),
        pltpu.make_async_copy(hid_ref, hidf.at[here_id, :], ls.at[3]),
        pltpu.make_async_copy(cot_ref.at[:, ds(g * COLS, COLS, 128)], cot.at[here_id, :], ls.at[4]),
    ]
    for copy in local:
        copy.start()

    pick = lax.div(x, 2)
    part = lax.rem(x, 2) * 2 + zh
    to_me = [
        jnp.logical_and(x == r, zh == pick),
        jnp.logical_and(jnp.logical_and(x == y, y == r), zh == pick),
    ]

    barrier = pltpu.get_barrier_semaphore()

    def greet(dev):
        pl.semaphore_signal(barrier, inc=1, device_id=dev, device_id_type=MESH)

    greet(zpair)
    for k in (1, 2, 3):
        greet(xdev(k))
        greet(ydev(k))
        greet(rank(k)[2])
    for n in range(2):
        for k in range(4):
            greet({
                "seq_0": y if n == 0 else r, "seq_1": jnp.int32(k // 2), "seq_2": jnp.int32(k % 2),
                "zero_0": r if n == 0 else y, "zero_1": pick,
            })

    coli = lax.broadcasted_iota(jnp.int32, (128, 128), 1)
    rowi = lax.broadcasted_iota(jnp.int32, (128, 128), 0)
    local[0].wait()
    tail = jnp.concatenate([wraw[:, 2816:2856].astype(F32), jnp.zeros((160, 88), F32)], axis=1)
    tail = pltpu.roll(tail, lax.rem(128 - 10 * g, 128), 1)
    keep10 = lax.broadcasted_iota(jnp.int32, (160, 128), 1) < 10
    wf[own, 768:896] = jnp.where(keep10, tail, 0.0).astype(BF16)

    def lanes10(ref):
        full = jnp.concatenate([ref[...], jnp.zeros((1, 88), F32)], axis=1)
        return pltpu.roll(jnp.broadcast_to(full, (8, 128)), lax.rem(128 - 10 * g, 128), 1)[0:1, :]

    bias = lanes10(bias_ref)
    neg = -jnp.exp(lanes10(decay_ref))
    skip = lanes10(skip_ref)
    for copy in local[1:]:
        copy.wait()
    pl.semaphore_wait(barrier, 18)

    def cols(m):
        return (ds(640 + 128 * c, 256, 128), slice(0, 256), slice(256, 512), slice(512, 640))[m]

    w = {}

    def wsend(m, i, rows, dev):
        ref = wf.at[rows, cols(m)]
        w[m, i] = send(9 * m + i, ref, ref, dev)

    def w_own_x(m):
        wsend(m, 1, own, xdev(1))
        wsend(m, 2, own, xdev(-1))

    def w_own_z(m):
        wsend(m, 0, own, zpair)

    def w_other(m):
        w[m, 0].wait_recv()
        wsend(m, 3, shard(x, 1 - zh), xdev(1))
        wsend(m, 4, shard(x, 1 - zh), xdev(-1))

    def w_forward(m):
        w[m, 1].wait_recv()
        wsend(m, 5, shard(x - 1, zh, 0, 80), xdev(1))
        w[m, 2].wait_recv()
        wsend(m, 6, shard(x + 1, zh, 80, 80), xdev(-1))

    def w_forward_other(m):
        w[m, 3].wait_recv()
        wsend(m, 7, shard(x - 1, 1 - zh, 0, 80), xdev(1))
        w[m, 4].wait_recv()
        wsend(m, 8, shard(x + 1, 1 - zh, 80, 80), xdev(-1))

    def w_across(m):
        wsend(m, 3, shard(x - 1, zh), zpair)
        wsend(m, 4, shard(x + 1, zh), zpair)

    def w_across_far(m):
        w[m, 5].wait_recv()
        wsend(m, 7, shard(x + 2, zh, 0, 80), zpair)
        w[m, 6].wait_recv()
        wsend(m, 8, shard(x + 2, zh, 80, 80), zpair)

    def w_done(m, which):
        for i in which:
            w[m, i].wait_recv()

    w_own_z(0)
    w_own_x(0)
    h_z = send(37, hid_ref, hidf.at[here_id, :], rank(2)[2])
    h_c = send(36, hid_ref, hidf.at[here_id, :], core)
    cots = []
    for k in (2, 3, 1):
        zlk, ck, dev = rank(k)
        gk = lax.rem(zlk + zh, 2) * 2 + ck
        cots.append(send(38 + k, cot_ref.at[:, ds(gk * COLS, COLS, 128)], cot.at[here_id, :], dev))
    w_own_z(1)
    w_own_x(1)
    w_other(0)
    w_own_x(2)
    w_own_z(2)
    w_forward(0)
    w_other(1)
    h_z.wait_recv()
    zrows = ds((rank(2)[0] * 2 + c) * 128, 128)
    h_f = send(38, hidf.at[zrows, :], hidf.at[zrows, :], core)
    w_own_x(3)
    w_own_z(3)
    w_forward_other(0)
    w_forward(1)
    w_done(0, (5, 6, 7, 8))
    mate = send(42, wf.at[:, ds(lane0, 128)], wf.at[:, ds(lane0, 128)], core)
    w_forward(2)
    w_across(2)
    h_c.wait_recv()
    h_f.wait_recv()
    w_forward_other(1)
    mate.wait_recv()

    low = coli < 64
    causal = rowi >= coli
    anti = rowi <= coli
    tri = causal.astype(F32)
    upper = anti.astype(F32)
    strict = (rowi > coli).astype(F32)

    def pair(v, j):
        return jnp.where(low[0 : v.shape[0]], v[:, 2 * j : 2 * j + 1], v[:, 2 * j + 1 : 2 * j + 2])

    def blocks(f, unroll=True):
        if unroll:
            for b in range(4):
                f(b, pl.ds(b * 128, 128))
        else:
            def step(b, carry):
                f(b, ds(b * 128, 128))
                return carry

            lax.fori_loop(0, 4, step, 0)

    def common(b, rows):
        p = mm(hidf[rows, :], wf[:, 640:1024])
        projs[rows, :] = p
        bm = jax.nn.silu(p[:, 0:128])
        cm = jax.nn.silu(p[:, 256:384])
        bmf[rows, :] = bm
        cmf[rows, :] = cm
        pre = p[:, 128:256] + bias
        step = jnp.maximum(pre, 0.0) + jnp.log1p(jnp.exp(-jnp.abs(pre)))
        lg = neg * step
        cum = mm(tri, lg, NN, highest)
        stp[rows, :] = step
        lgd[rows, :] = lg
        cums[rows, :] = cum
        cumt[b] = cum.T[0:16, :]
        scores = mm(cm, bm, NT, highest)
        gs[b] = scores
        gts[b] = scores.T
        dgs[b] = jnp.zeros((128, 128), F32)
        red[b] = jnp.zeros((384, 128), F32)

    blocks(common)
    for j in range(5):
        cj = slice(128 * j, 128 * j + 128)
        for b in range(4):
            last_row = cums[128 * b + 127 : 128 * b + 128, :]
            tot[8 * b : 8 * b + 8, cj] = pair(jnp.broadcast_to(last_row, (8, 128)), j)
    tts[...] = tot[0:8, :] + tot[8:16, :] + tot[16:24, :] + tot[24:32, :]
    totals = [send(43 + k, tts, ttr.at[k - 1], ydev(k)) for k in (1, 2, 3)]

    def total(b, cj):
        return tot[8 * b : 8 * b + 1, cj]

    states = {}

    def pair_forward(j):
        cj = slice(128 * j, 128 * j + 128)

        def project(b, rows):
            projv[rows, cj] = mm(hidf[rows, :], wf[:, cj])

        def local_part(b, rows):
            ce = pair(cums[rows, :], j)
            se = pair(stp[rows, :], j)
            ec = jnp.exp(ce)
            tl = jnp.exp(ce[127:128, :] - ce)
            val = jax.nn.silu(projv[rows, cj])
            xs = val * se
            sexp[rows, cj] = se
            ecs[rows, cj] = ec
            tls[rows, cj] = tl
            vv[rows, cj] = val
            xb[rows, cj] = xs.astype(BF16)
            x16 = (xs * tl).astype(BF16)
            o16 = (cot[rows, cj].astype(F32) * ec).astype(BF16)
            xt[rows, cj] = x16
            oe[rows, cj] = o16
            sl[b, :, cj] = mm(bmf[rows, :].astype(BF16), x16, TN)
            dl[b, :, cj] = mm(cmf[rows, :].astype(BF16), o16, TN)

        blocks(project)
        blocks(local_part)
        s = sl[0, :, cj]
        d = dl[3, :, cj]
        for b in range(1, 4):
            s = jnp.exp(total(b, cj)) * s + sl[b, :, cj]
            d = jnp.exp(total(3 - b, cj)) * d + dl[3 - b, :, cj]
        stt[0, :, cj] = s.astype(BF16)
        stt[1, :, cj] = d.astype(BF16)
        for k in (1, 2, 3):
            wraps = lax.div(y + k, 4)
            states[j, k] = send(47 + 3 * j + k - 1, stt.at[wraps, :, cj], str_.at[k - 1, :, cj], ydev(k))

    def pair_inside(j):
        cj = slice(128 * j, 128 * j + 128)

        def inside(b, rows):
            cum = cums[rows, :]
            c0, c1 = cum[:, 2 * j : 2 * j + 1], cum[:, 2 * j + 1 : 2 * j + 2]
            r0, r1 = cumt[b, 2 * j : 2 * j + 1, :], cumt[b, 2 * j + 1 : 2 * j + 2, :]
            w0 = jnp.where(causal, jnp.exp(jnp.where(causal, c0 - r0, 0.0)), 0.0)
            w1 = jnp.where(causal, jnp.exp(jnp.where(causal, c1 - r1, 0.0)), 0.0)
            u0 = jnp.where(anti, jnp.exp(jnp.where(anti, r0 - c0, 0.0)), 0.0)
            u1 = jnp.where(anti, jnp.exp(jnp.where(anti, r1 - c1, 0.0)), 0.0)
            scores, scores_t = gs[b], gts[b]
            m = jnp.concatenate([scores * w0, scores * w1], axis=1).astype(BF16)
            mt = jnp.concatenate([scores_t * u0, scores_t * u1], axis=1).astype(BF16)
            x16 = xb[rows, cj]
            o16 = cot[rows, cj]
            zero = jnp.zeros_like(x16)
            xd = jnp.concatenate([jnp.where(low, x16, zero), jnp.where(low, zero, x16)], axis=0)
            od = jnp.concatenate([jnp.where(low, o16, zero), jnp.where(low, zero, o16)], axis=0)
            yy = mm(m, xd)
            pp = mm(o16, xd, NT)
            dx = mm(mt, od)
            dgs[b] = dgs[b] + w0 * pp[:, 0:128] + w1 * pp[:, 128:256]
            dxin[rows, cj] = dx
            q1s[rows, cj] = o16.astype(F32) * yy - x16.astype(F32) * dx

        blocks(inside)

    for copy in cots:
        copy.wait_recv()
    w_done(1, (5, 6, 7, 8))
    w_forward(3)
    w_across(3)
    pair_forward(0)
    w_across_far(2)
    pair_inside(0)
    w_across_far(3)
    pair_forward(1)
    pair_inside(1)
    w_done(2, (0, 3, 4, 7, 8))
    pair_forward(2)
    pair_inside(2)
    pair_forward(3)
    pair_inside(3)
    w_done(3, (0, 3, 4, 7, 8))
    pair_forward(4)
    pair_inside(4)

    def turn(b, rows):
        hidt[:, rows] = hidf[rows, :].T
        dcf[rows, :] = mm(dgs[b], bmf[rows, :], NN, highest)
        dbf[rows, :] = mm(dgs[b], cmf[rows, :], TN, highest)

    blocks(turn)
    for copy in totals:
        copy.wait_recv()

    lanes = lax.broadcasted_iota(jnp.int32, (256, 128), 0)
    outl = lax.broadcasted_iota(jnp.int32, (256, 128), 1)

    def sums(z, j):
        hi = z.astype(BF16)
        lo = (z - hi.astype(F32)).astype(BF16)
        choose = (outl == 2 * j + lax.rem(lax.div(lanes, 64), 2)).astype(F32).astype(BF16)
        return mm(jnp.concatenate([hi, lo], axis=1), choose)

    yes = [jnp.where(y >= k, 1.0, 0.0).astype(F32) for k in (1, 2, 3)]
    no = [jnp.where(y + k <= 3, 1.0, 0.0).astype(F32) for k in (1, 2, 3)]
    inner = [jnp.zeros((8, 128), F32) for _ in range(4)]
    gain = [jnp.zeros((8, 128), F32)]

    def pair_outside(j):
        cj = slice(128 * j, 128 * j + 128)
        for k in (1, 2, 3):
            states[j, k].wait_recv()
        t = [ttr[k, 0:1, cj] for k in range(3)]
        got = [str_[k, :, cj].astype(F32) for k in range(3)]
        s = yes[0] * got[0] + (yes[1] * jnp.exp(t[0])) * got[1] + (yes[2] * jnp.exp(t[0] + t[1])) * got[2]
        d = no[0] * got[2] + (no[1] * jnp.exp(t[2])) * got[1] + (no[2] * jnp.exp(t[2] + t[1])) * got[0]
        for b in (3, 2, 1, 0):
            db[b, :, cj] = d.astype(BF16)
            dd[b] = d
            d = jnp.exp(total(b, cj)) * d + dl[b, :, cj]
        for b in range(4):
            sb[b, :, cj] = s.astype(BF16)
            grown = jnp.exp(total(b, cj)) * s
            inner[b] = inner[b] + sums((grown * dd[b]).reshape(16, 8, 128).sum(axis=0), j)
            s = grown + sl[b, :, cj]

        def outside(b, rows):
            o = cot[rows, cj].astype(F32)
            yst = mm(cmf[rows, :].astype(BF16), sb[b, :, cj]) * ecs[rows, cj]
            dxst = mm(bmf[rows, :].astype(BF16), db[b, :, cj]) * tls[rows, cj]
            val = vv[rows, cj]
            dxs = dxin[rows, cj] + dxst
            z = jnp.concatenate([q1s[rows, cj] + o * yst, xb[rows, cj].astype(F32) * dxst, dxs * val], axis=0)
            red[b] = red[b] + sums(z, j)
            dval = dxs * sexp[rows, cj] + pair(skip, j) * o
            rr[rows, cj] = (dval * silu_grad(projv[rows, cj])).astype(BF16)
            gain[0] = gain[0] + sums((o * val).reshape(16, 8, 128).sum(axis=0), j)

        blocks(outside)

    class Stream:
        def __init__(self, base, lo, hi, kind, bufs):
            self.base, self.lo, self.hi, self.kind = base, lo, hi, kind
            (self.dw, self.s1, self.r1p, self.r1m, self.s2p, self.s2m, self.r2p, self.r2m,
             self.s3, self.r3, self.s4, self.r4, self.sd, self.rd) = bufs
            self.index, self.dev, self.index2, self.dev2 = (y, ydev, x, xdev) if kind == 0 else (x, xdev, y, ydev)

        def first(self):
            for i in (2, 1, 3, 0):
                rows = ds(lax.rem(self.index + i, 4) * 320, 320)
                self.dw[rows, :] = mm(hidt[rows, :], rr[:, self.lo : self.hi])
                if i == 2:
                    self.s1[...] = self.dw[rows, :].astype(BF16)
                    self.one = (
                        send(self.base, self.s1.at[0:160, :], self.r1p, self.dev(1)),
                        send(self.base + 1, self.s1.at[160:320, :], self.r1m, self.dev(-1)),
                    )

        def second(self):
            nxt = lax.rem(self.index + 1, 4) * 320
            prv = lax.rem(self.index + 3, 4) * 320
            self.one[0].wait_recv()
            self.s2p[0:160, :] = (self.dw[ds(nxt, 160), :] + self.r1p[...].astype(F32)).astype(BF16)
            self.s2p[160:320, :] = self.dw[ds(nxt + 160, 160), :].astype(BF16)
            up = send(self.base + 2, self.s2p, self.r2p, self.dev(1))
            self.one[1].wait_recv()
            self.s2m[0:160, :] = self.dw[ds(prv, 160), :].astype(BF16)
            self.s2m[160:320, :] = (self.dw[ds(prv + 160, 160), :] + self.r1m[...].astype(F32)).astype(BF16)
            self.two = (up, send(self.base + 3, self.s2m, self.r2m, self.dev(-1)))

        def third(self):
            for copy in self.two:
                copy.wait_recv()
            here = ds(self.index * 320, 320)
            summed = self.dw[here, :] + self.r2p[...].astype(F32) + self.r2m[...].astype(F32)
            self.dw[here, :] = summed
            self.s3[...] = summed.astype(BF16)
            self.three = [
                send(self.base + 3 + k, self.s3.at[ds(lax.rem(self.index2 + k, 4) * 80, 80), :], self.r3.at[k - 1], self.dev2(k))
                for k in (2, 1, 3)
            ]

        def fourth(self):
            for copy in self.three:
                copy.wait_recv()
            rows = ds(self.index * 320 + self.index2 * 80, 80)
            self.s4[...] = self.dw[rows, :] + self.r3[0].astype(F32) + self.r3[1].astype(F32) + self.r3[2].astype(F32)
            self.four = send(self.base + 7, self.s4.at[ds((1 - zh) * 40, 40), :], self.r4, zpair)

        def owners(self):
            self.four.wait_recv()
            chunk = self.s4[ds(zh * 40, 40), :] + self.r4[...]
            self.moves = []
            for i in range(4):
                self.sd[i, 0:10, :] = chunk[10 * i : 10 * i + 10, :]
                dev = {
                    "seq_0": self.index,
                    "seq_1": lax.div(self.index2, 2),
                    "seq_2": lax.rem(self.index2, 2),
                    "zero_0": zh * 2 + i // 2,
                    "zero_1": jnp.int32(i % 2),
                }
                copy = pltpu.make_async_remote_copy(
                    src_ref=self.sd.at[i], dst_ref=self.rd.at[g], send_sem=ss.at[self.base + 8 + i],
                    recv_sem=rs.at[self.base + 8 + g], device_id=dev, device_id_type=MESH,
                )
                keep = jnp.logical_and(to_me[self.kind], part == i)

                @pl.when(jnp.logical_not(keep))
                def _():
                    copy.start()

                @pl.when(keep)
                def _():
                    self.rd[g] = self.sd[i]

                self.moves.append((copy, keep))

        def finish(self):
            for k in range(4):
                copy = pltpu.make_async_remote_copy(
                    src_ref=self.sd.at[0], dst_ref=self.rd.at[k], send_sem=ss.at[self.base + 8],
                    recv_sem=rs.at[self.base + 8 + k], device_id=core, device_id_type=MESH,
                )

                @pl.when(jnp.logical_not(jnp.logical_and(to_me[self.kind], g == k)))
                def _():
                    copy.wait_recv()

        def close(self):
            for copy, keep in self.moves:

                @pl.when(jnp.logical_not(keep))
                def _():
                    copy.wait_send()

    alpha = Stream(62, 0, 384, 0, (dwa, sa1, ra1p, ra1m, sa2p, sa2m, ra2p, ra2m, sa3, ra3, sa4, ra4, sd, rd))
    beta = Stream(74, 384, 640, 1, (dwb, sb1, rb1p, rb1m, sb2p, sb2m, rb2p, rb2m, sb3, rb3, sb4, rb4, sdb, rdb))
    gamma = Stream(86, 640, 768, 1, (dwc, sc1, rc1p, rc1m, sc2p, sc2m, rc2p, rc2m, sc3, rc3, sc4, rc4, sdc, rdc))

    pair_outside(0)
    pair_outside(1)
    pair_outside(2)
    alpha.first()
    pair_outside(3)
    pair_outside(4)
    beta.first()
    alpha.second()

    ownl = coli < 10
    bias_sum = decay_sum = jnp.zeros((8, 128), F32)
    for b in range(4):
        rows = slice(128 * b, 128 * b + 128)
        dcf[rows, :] = dcf[rows, :] + mm(oe[rows, :], sb[b], NT)
        dbf[rows, :] = dbf[rows, :] + mm(xt[rows, :], db[b], NT)
        dlog = mm(upper, red[b, 0:128], NN, highest) + mm(strict, red[b, 128:256], NN, highest)
        dlog = jnp.where(ownl, dlog + inner[b].sum(axis=0, keepdims=True), 0.0)
        ddt = (red[b, 256:384] + neg * dlog) * jax.nn.sigmoid(projs[rows, 128:256] + bias)
        ddt = jnp.where(ownl, ddt, 0.0)
        rdt[rows, :] = ddt.astype(BF16)
        bias_sum = bias_sum + ddt.reshape(16, 8, 128).sum(axis=0)
        decay_sum = decay_sum + (dlog * lgd[rows, :]).reshape(16, 8, 128).sum(axis=0)
    first = c == 0
    place = jnp.where(jnp.logical_and(rowi < 10, coli == rowi + 10 * g), 1.0, 0.0).astype(F32)
    spread = mm(rdt[...], place.astype(BF16)).astype(BF16)
    t1d[...] = spread
    t1s[...] = jnp.where(first, dcf[...], dbf[...])
    t1 = [send(98, t1s, t1r, core), send(99, t1d, t1dr, core)]
    row8 = lax.broadcasted_iota(jnp.int32, (8, 128), 0)
    packed = jnp.where(
        row8 == 0, bias_sum.sum(axis=0, keepdims=True),
        jnp.where(row8 == 1, decay_sum.sum(axis=0, keepdims=True),
                  jnp.where(row8 == 2, gain[0].sum(axis=0, keepdims=True), 0.0)),
    )
    heads_y[y] = mm(packed, place, NN, highest)
    head_y = [send(100 + k, heads_y.at[y], heads_y.at[y], ydev(k)) for k in (1, 2, 3)]
    beta.second()
    for copy in t1:
        copy.wait_recv()
    mixed = jnp.where(first, dbf[...], dcf[...]) + t1r[...]
    dt2 = spread.astype(F32) + t1dr[...].astype(F32)
    north = a == 0
    t2s[...] = jnp.where(north, dt2, mixed).astype(BF16)
    t2 = send(104, t2s, t2r, rank(2)[2])

    def token(b, rows):
        hgp[rows, :] = mm(rr[rows, 0:640], wf[:, 0:640], NT) + mm(rdt[rows, :], wf[:, 768:896], NT)

    blocks(token, False)
    t2.wait_recv()
    came = t2r[...].astype(F32)
    tile = projs[:, ds(256 * c, 128, 128)]
    upper_pick = ((mixed + came) * silu_grad(tile)).astype(BF16).astype(F32)
    lower_pick = jnp.where(first, dt2 + came, 0.0)
    rr[:, 640:768] = jnp.where(north, upper_pick, lower_pick).astype(BF16)
    shr[...] = jnp.where(north, upper_pick, 0.0).astype(BF16)
    gamma.first()
    hgc = []
    for k in (2, 3, 1):
        zlk, ck, dev = rank(k)
        rows = ds((zlk * 2 + ck) * 128, 128)
        hgs[k - 1] = (hgp[rows, :] + mm(shr[rows, :], wf[:, ds(lane0, 128)], NT)).astype(BF16)
        hgc.append(send(104 + k, hgs.at[k - 1], hgr.at[k - 1], dev))
    hgp[here_id, :] = hgp[here_id, :] + mm(shr[here_id, :], wf[:, ds(lane0, 128)], NT)
    gamma.second()
    alpha.third()
    beta.third()
    for copy in head_y:
        copy.wait_recv()
    heads_x[x] = (heads_y[0] + heads_y[1]) + (heads_y[2] + heads_y[3])
    head_x = [send(107 + k, heads_x.at[x], heads_x.at[x], xdev(k)) for k in (1, 2, 3)]
    gamma.third()
    beta.fourth()
    alpha.fourth()
    for copy in head_x:
        copy.wait_recv()
    heads_z[zh] = (heads_x[0] + heads_x[1]) + (heads_x[2] + heads_x[3])
    head_z = send(111, heads_z.at[zh], heads_z.at[zh], zpair)
    gamma.fourth()
    beta.owners()
    alpha.owners()
    gamma.owners()
    head_z.wait_recv()
    heads_g[r] = heads_z[0] + heads_z[1]
    head_g = [send(111 + k, heads_g.at[r], heads_g.at[r], rank(k)[2]) for k in (1, 2, 3)]
    for copy in hgc:
        copy.wait_recv()
    out = hgp[here_id, :] + hgr[0].astype(F32) + hgr[1].astype(F32) + hgr[2].astype(F32)
    hg_ref[...] = out.astype(BF16)
    beta.finish()
    for k in range(4):
        wg_ref[:, 640 * k + 384 : 640 * k + 640] = rdb[k, 0:10, :]
    alpha.finish()
    for k in range(4):
        wg_ref[:, 640 * k : 640 * k + 384] = rd[k, 0:10, :]
    gamma.finish()
    wg_ref[:, 2560:2688] = rdc[0, 0:10, :]
    wg_ref[:, 2688:2816] = rdc[1, 0:10, :]
    wg_ref[:, 2816:2856] = rdc[2, 0:10, 0:40]
    for copy in head_g:
        copy.wait_recv()
    hd_ref[...] = (heads_g[0] + heads_g[1]) + (heads_g[2] + heads_g[3])
    for copy in pending:
        copy.wait_send()
    for stream in (alpha, beta, gamma):
        stream.close()


def scratch():
    def v(shape, dtype=F32):
        return pltpu.VMEM(shape, dtype)

    def stream(n):
        half, whole = v((160, n), BF16), v((320, n), BF16)
        return [
            v((D, n)), whole, half, half, whole, whole, whole, whole, whole,
            v((3, 80, n), BF16), v((80, n)), v((40, n)), v((4, 16, n)), v((4, 16, n)),
        ]

    wide, wide16 = v((512, COLS)), v((512, COLS), BF16)
    thin, thin16 = v((512, 128)), v((512, 128), BF16)
    return [
        v((512, D), BF16), v((D, 512), BF16), wide16, v((160, 2856), BF16), v((D, 1024), BF16),
        v((512, 384)), wide, thin, thin, thin, thin, v((4, 16, 128)), thin,
        v((4, 128, 128)), v((4, 128, 128)), v((4, 128, 128)),
        wide, wide, wide, wide, wide16, wide16, wide16, v((32, COLS)),
        v((4, 128, COLS)), v((4, 128, COLS)), v((2, 128, COLS), BF16), v((8, COLS)),
        v((3, 128, COLS), BF16), v((3, 8, COLS)), wide, wide, thin, thin,
        v((4, 128, COLS), BF16), v((4, 128, COLS), BF16), v((4, 128, 128)), v((4, 384, 128)),
        v((512, 768), BF16), thin16, thin, thin, thin16, thin16, thin16, thin16, thin16,
        v((512, D)), v((3, 128, D), BF16), v((3, 128, D), BF16),
        *stream(384), *stream(256), *stream(128),
        v((4, 8, 128)), v((4, 8, 128)), v((2, 8, 128)), v((4, 8, 128)),
        pltpu.SemaphoreType.DMA((116,)), pltpu.SemaphoreType.DMA((116,)), pltpu.SemaphoreType.DMA((8,)),
    ]


def body(hidden, output_grad, input_weight, step_bias, decay_log, skip_gain):
    anyspace = pl.BlockSpec(memory_space=pl.ANY)
    vmem = pl.BlockSpec(memory_space=pltpu.VMEM)
    hg, wg, hd = pl.pallas_call(
        kernel,
        out_shape=(
            jax.ShapeDtypeStruct((128, D), BF16),
            jax.ShapeDtypeStruct((10, 2856), F32),
            jax.ShapeDtypeStruct((8, 128), F32),
        ),
        in_specs=[anyspace, anyspace, anyspace, vmem, vmem, vmem],
        out_specs=(vmem, vmem, vmem),
        scratch_shapes=scratch(),
        compiler_params=pltpu.CompilerParams(has_side_effects=True, collective_id=0, vmem_limit_bytes=64000000),
    )(hidden[0], output_grad[0], input_weight, step_bias[None], decay_log[None], skip_gain[None])
    return (hg[None], wg, hd[0:3, 0:HEADS])


def solution(mesh):
    torus = Mesh(
        mesh.devices.reshape(4, 2, 2, 4, 2), ("seq_0", "seq_1", "seq_2", "zero_0", "zero_1")
    )
    in_specs = (P(ZERO, SEQ, None), P(ZERO, SEQ, None), P(ZERO, None), P(), P(), P())
    out_specs = (P(ZERO, SEQ, None), P(SEQ_ZERO, None), P())
    return jax.shard_map(body, mesh=torus, in_specs=in_specs, out_specs=out_specs, check_vma=False)
```

time: 596 us -> 81.3 us (0.14)
  waiting for transfers between devices: 441 us -> 0 us
  Pallas kernels: 0 us -> 76.7 us
  matrix products: 47.9 us -> 0 us
  blocking collectives: 45.9 us -> 0 us
  other arithmetic: 36.4 us -> 0 us
  between operations: 14.6 us -> 0.65 us
    all_gather x7 -> x0, waiting for transfers between devices: 304 us -> none  [the longest x6 199 us: prefix_by_axis(): pieces = jax.tree.map(lambda part: lax.all_gather(part, axis), subtotal)]
    unnamed x9 -> x0, waiting for transfers between devices: 137 us -> none
    pallas_call x0 -> x1, Pallas kernels: none -> 76.7 us  [body(): pl.pallas_call(kernel, out_shape=(jax.ShapeDtypeStruct((128, D), BF16), j...]
    dot_general x14 -> x0, matrix products: 47.9 us -> none  [the longest x2 9.01 us: state_mixer(): jnp.einsum('kqsh,kshp->kqhp', scores[:, :, :, None] * within, scaled, pre...]
    psum x5 -> x0, blocking collectives: 32.1 us -> none  [over_axes(): return functools.reduce(lax.psum, axes, x)]
    add x7 -> x0, other arithmetic: 23.4 us -> none  [the longest x6 23.4 us: combine_states(): jnp.exp(later[0])[:, None, None] * earlier[1] + later[1]]
    all_gather x3 -> x0, blocking collectives: 13.8 us -> none  [prefix_by_axis(): pieces = jax.tree.map(lambda part: lax.all_gather(part, axis), subtotal)]
    reduce_sum x6 -> x0, other arithmetic: 11.2 us -> none  [the longest x1 5.44 us: advance(): jnp.exp(block_total)[:, None, None] * running + block_state]
  transfers between devices with their start and end apart: 8 -> 0, of which waited for: 8 -> 0; matrix products, arithmetic and copies ran while one was open for 4% -> 0% of each run, Pallas kernels for 0% -> 0%
where the time goes in v2:
time: 81.3 us; the launch traced here: 81 us
  Pallas kernels  76.7 us (94%)
  local copies, waits for them, and re-layouts  3.68 us (5%)
    pallas_call x1, Pallas kernels, body(): pl.pallas_call(kernel, out_shape=(jax.ShapeDtypeStruct((128, D), BF16), j...  76.7 us
    unnamed x6, local copies, waits for them, and re-layouts  3.1 us

profile of v2, /device:TPU:1, one launch (start us, length us, event | category | flops | bytes accessed | tf_op | source)
XLA Modules:
  0.0 81.0 jit_solution(17896689668494719581)
XLA Ops:
  0.6 76.7 %shard_map.85 = (bf16[128,1280]{1,0:T(8,128)(2,1)}, f32[10,2856]{1,0:T(8,128)}, f32[8,128]{1,0:T(8,128)}) custom-call(bf16[128,1280]{1,0:T(8,128)(2,1)} %bitcast.8, bf16[128,2560]{1,0:T(8,128)(2,1)} %bitcast.6, bf16[160,2856]{1,0:T(8,128)(2,1)} %w_ref.1, f32[1,40]{1,0:T(1,128)} %bitcast.9, f32[1,40]{1,0:T(1,128)} %bitcast.10, f32[1,40]{1,0:T(1,128)} %bitcast.11), custom_call_target="tpu_custom_call" | custom-call | tf_op jit(solution)/shard_map/pallas_call | solution.py:659
  77.3 0.0 copy-start.1
  77.3 0.7 copy-done.1
  78.0 0.6 slice.3
  78.6 0.0 copy-start
  78.6 1.8 %copy.11 = bf16[1,128,1280]{2,1,0:T(8,128)(2,1)} copy(bf16[1,128,1280]{2,1,0:T(8,128)(2,1)} %bitcast.7) | data formatting | bytes 655360
  80.3 0.0 copy-done
  80.3 0.7 copy.12
Async XLA Ops:
  77.3 0.7 copy-start.1
  78.6 1.8 %copy-start = (f32[10,2856]{1,0:T(8,128)S(1)}, f32[10,2856]{1,0:T(8,128)}, u32[]{:S(2)}) copy-start(f32[10,2856]{1,0:T(8,128)} %get-tuple-element.13) | copy-start | bytes 342724

commit v3 on v2

--- a/solution.py
+++ b/solution.py
@@ -41,14 +41,14 @@
 def kernel(
     hid_ref, cot_ref, w_ref, bias_ref, decay_ref, skip_ref,
     hg_ref, wg_ref, hd_ref,
-    hidf, hidt, cot, wraw, wf, projs, projv, bmf, cmf, lgd, cums, cumt, stp, gs, gts, dgs,
+    hidf, hidt, hidx, cot, wraw, wf, projs, projv, bmf, cmf, lgd, cums, cumt, stp, gs, gts, dgs,
     sexp, ecs, tls, vv, xb, xt, oe, tot,
     sl, dl, stt, tts, str_, ttr, q1s, dxin, dbf, dcf, sb, db, dd, red,
     rr, rdt, t1s, t1r, t1d, t1dr, t2s, t2r, shr, hgp, hgs, hgr,
     dwa, sa1, ra1p, ra1m, sa2p, sa2m, ra2p, ra2m, sa3, ra3, sa4, ra4, sd, rd,
     dwb, sb1, rb1p, rb1m, sb2p, sb2m, rb2p, rb2m, sb3, rb3, sb4, rb4, sdb, rdb,
     dwc, sc1, rc1p, rc1m, sc2p, sc2m, rc2p, rc2m, sc3, rc3, sc4, rc4, sdc, rdc,
-    heads_y, heads_x, heads_z, heads_g,
+    heads_y, heads_x, heads_z, heads_g, extras, hgo, wgo, hdo,
     ss, rs, ls,
 ):
     y, zl, c = (lax.axis_index(n) for n in SEQ)
@@ -97,13 +97,6 @@
     for copy in local:
         copy.start()
 
-    pick = lax.div(x, 2)
-    part = lax.rem(x, 2) * 2 + zh
-    to_me = [
-        jnp.logical_and(x == r, zh == pick),
-        jnp.logical_and(jnp.logical_and(x == y, y == r), zh == pick),
-    ]
-
     barrier = pltpu.get_barrier_semaphore()
 
     def greet(dev):
@@ -114,13 +107,6 @@
         greet(xdev(k))
         greet(ydev(k))
         greet(rank(k)[2])
-    for n in range(2):
-        for k in range(4):
-            greet({
-                "seq_0": y if n == 0 else r, "seq_1": jnp.int32(k // 2), "seq_2": jnp.int32(k % 2),
-                "zero_0": r if n == 0 else y, "zero_1": pick,
-            })
-
     coli = lax.broadcasted_iota(jnp.int32, (128, 128), 1)
     rowi = lax.broadcasted_iota(jnp.int32, (128, 128), 0)
     local[0].wait()
@@ -138,7 +124,7 @@
     skip = lanes10(skip_ref)
     for copy in local[1:]:
         copy.wait()
-    pl.semaphore_wait(barrier, 18)
+    pl.semaphore_wait(barrier, 10)
 
     def cols(m):
         return (ds(640 + 128 * c, 256, 128), slice(0, 256), slice(256, 512), slice(512, 640))[m]
@@ -190,33 +176,33 @@
     w_own_z(0)
     w_own_x(0)
     h_z = send(37, hid_ref, hidf.at[here_id, :], rank(2)[2])
+    w_own_z(1)
+    w_own_x(1)
     h_c = send(36, hid_ref, hidf.at[here_id, :], core)
     cots = []
     for k in (2, 3, 1):
         zlk, ck, dev = rank(k)
         gk = lax.rem(zlk + zh, 2) * 2 + ck
         cots.append(send(38 + k, cot_ref.at[:, ds(gk * COLS, COLS, 128)], cot.at[here_id, :], dev))
-    w_own_z(1)
-    w_own_x(1)
     w_other(0)
+    w_forward(0)
     w_own_x(2)
     w_own_z(2)
-    w_forward(0)
     w_other(1)
+    w_forward_other(0)
+    w_forward(1)
     h_z.wait_recv()
     zrows = ds((rank(2)[0] * 2 + c) * 128, 128)
     h_f = send(38, hidf.at[zrows, :], hidf.at[zrows, :], core)
     w_own_x(3)
     w_own_z(3)
-    w_forward_other(0)
-    w_forward(1)
     w_done(0, (5, 6, 7, 8))
     mate = send(42, wf.at[:, ds(lane0, 128)], wf.at[:, ds(lane0, 128)], core)
     w_forward(2)
     w_across(2)
+    w_forward_other(1)
     h_c.wait_recv()
     h_f.wait_recv()
-    w_forward_other(1)
     mate.wait_recv()
 
     low = coli < 64
@@ -278,9 +264,6 @@
     def pair_forward(j):
         cj = slice(128 * j, 128 * j + 128)
 
-        def project(b, rows):
-            projv[rows, cj] = mm(hidf[rows, :], wf[:, cj])
-
         def local_part(b, rows):
             ce = pair(cums[rows, :], j)
             se = pair(stp[rows, :], j)
@@ -300,7 +283,7 @@
             sl[b, :, cj] = mm(bmf[rows, :].astype(BF16), x16, TN)
             dl[b, :, cj] = mm(cmf[rows, :].astype(BF16), o16, TN)
 
-        blocks(project)
+        projv[:, cj] = mm(hidf[...], wf[:, cj])
         blocks(local_part)
         s = sl[0, :, cj]
         d = dl[3, :, cj]
@@ -341,14 +324,25 @@
 
         blocks(inside)
 
+    w_forward(3)
+    w_across(3)
+
+    i320 = lax.broadcasted_iota(jnp.int32, (320, 320), 0)
+    k320 = lax.broadcasted_iota(jnp.int32, (320, 320), 1)
+    tens = lax.shift_right_logical(i320 * 6554, 16)
+    source = ((tens & 3) * 8 + lax.shift_right_logical(tens, 2)) * 10 + i320 - tens * 10
+    perm = jnp.where(k320 == source, 1.0, 0.0).astype(F32).astype(BF16)
+    for q in range(4):
+        hidt[320 * q : 320 * q + 320, :] = mm(perm, hidf[:, 320 * q : 320 * q + 320], NT).astype(BF16)
     for copy in cots:
         copy.wait_recv()
     w_done(1, (5, 6, 7, 8))
-    w_forward(3)
-    w_across(3)
     pair_forward(0)
     w_across_far(2)
     pair_inside(0)
+    for p in range(4):
+        for q in range(4):
+            hidx[320 * p + 80 * q : 320 * p + 80 * q + 80, :] = hidt[320 * q + 80 * p : 320 * q + 80 * p + 80, :]
     w_across_far(3)
     pair_forward(1)
     pair_inside(1)
@@ -362,7 +356,6 @@
     pair_inside(4)
 
     def turn(b, rows):
-        hidt[:, rows] = hidf[rows, :].T
         dcf[rows, :] = mm(dgs[b], bmf[rows, :], NN, highest)
         dbf[rows, :] = mm(dgs[b], cmf[rows, :], TN, highest)
 
@@ -418,7 +411,7 @@
 
     class Stream:
         def __init__(self, base, lo, hi, kind, bufs):
-            self.base, self.lo, self.hi, self.kind = base, lo, hi, kind
+            self.base, self.lo, self.hi, self.left = base, lo, hi, hidx if kind else hidt
             (self.dw, self.s1, self.r1p, self.r1m, self.s2p, self.s2m, self.r2p, self.r2m,
              self.s3, self.r3, self.s4, self.r4, self.sd, self.rd) = bufs
             self.index, self.dev, self.index2, self.dev2 = (y, ydev, x, xdev) if kind == 0 else (x, xdev, y, ydev)
@@ -426,7 +419,7 @@
         def first(self):
             for i in (2, 1, 3, 0):
                 rows = ds(lax.rem(self.index + i, 4) * 320, 320)
-                self.dw[rows, :] = mm(hidt[rows, :], rr[:, self.lo : self.hi])
+                self.dw[rows, :] = mm(self.left[rows, :], rr[:, self.lo : self.hi])
                 if i == 2:
                     self.s1[...] = self.dw[rows, :].astype(BF16)
                     self.one = (
@@ -463,54 +456,22 @@
                 copy.wait_recv()
             rows = ds(self.index * 320 + self.index2 * 80, 80)
             self.s4[...] = self.dw[rows, :] + self.r3[0].astype(F32) + self.r3[1].astype(F32) + self.r3[2].astype(F32)
-            self.four = send(self.base + 7, self.s4.at[ds((1 - zh) * 40, 40), :], self.r4, zpair)
+            self.four = send(self.base + 11, self.s4.at[ds((1 - zh) * 40, 40), :], self.r4, zpair)
 
         def owners(self):
             self.four.wait_recv()
             chunk = self.s4[ds(zh * 40, 40), :] + self.r4[...]
-            self.moves = []
             for i in range(4):
                 self.sd[i, 0:10, :] = chunk[10 * i : 10 * i + 10, :]
-                dev = {
-                    "seq_0": self.index,
-                    "seq_1": lax.div(self.index2, 2),
-                    "seq_2": lax.rem(self.index2, 2),
-                    "zero_0": zh * 2 + i // 2,
-                    "zero_1": jnp.int32(i % 2),
-                }
-                copy = pltpu.make_async_remote_copy(
-                    src_ref=self.sd.at[i], dst_ref=self.rd.at[g], send_sem=ss.at[self.base + 8 + i],
-                    recv_sem=rs.at[self.base + 8 + g], device_id=dev, device_id_type=MESH,
-                )
-                keep = jnp.logical_and(to_me[self.kind], part == i)
-
-                @pl.when(jnp.logical_not(keep))
-                def _():
-                    copy.start()
-
-                @pl.when(keep)
-                def _():
-                    self.rd[g] = self.sd[i]
-
-                self.moves.append((copy, keep))
+            self.rd[g] = self.sd[r]
+            self.five = [
+                send(self.base + 7 + k, self.sd.at[(rank(k)[0] * 2 + rank(k)[1])], self.rd.at[g], rank(k)[2])
+                for k in (2, 3, 1)
+            ]
 
         def finish(self):
-            for k in range(4):
-                copy = pltpu.make_async_remote_copy(
-                    src_ref=self.sd.at[0], dst_ref=self.rd.at[k], send_sem=ss.at[self.base + 8],
-                    recv_sem=rs.at[self.base + 8 + k], device_id=core, device_id_type=MESH,
-                )
-
-                @pl.when(jnp.logical_not(jnp.logical_and(to_me[self.kind], g == k)))
-                def _():
-                    copy.wait_recv()
-
-        def close(self):
-            for copy, keep in self.moves:
-
-                @pl.when(jnp.logical_not(keep))
-                def _():
-                    copy.wait_send()
+            for copy in self.five:
+                copy.wait_recv()
 
     alpha = Stream(62, 0, 384, 0, (dwa, sa1, ra1p, ra1m, sa2p, sa2m, ra2p, ra2m, sa3, ra3, sa4, ra4, sd, rd))
     beta = Stream(74, 384, 640, 1, (dwb, sb1, rb1p, rb1m, sb2p, sb2m, rb2p, rb2m, sb3, rb3, sb4, rb4, sdb, rdb))
@@ -522,8 +483,6 @@
     alpha.first()
     pair_outside(3)
     pair_outside(4)
-    beta.first()
-    alpha.second()
 
     ownl = coli < 10
     bias_sum = decay_sum = jnp.zeros((8, 128), F32)
@@ -544,6 +503,7 @@
     t1d[...] = spread
     t1s[...] = jnp.where(first, dcf[...], dbf[...])
     t1 = [send(98, t1s, t1r, core), send(99, t1d, t1dr, core)]
+    beta.first()
     row8 = lax.broadcasted_iota(jnp.int32, (8, 128), 0)
     packed = jnp.where(
         row8 == 0, bias_sum.sum(axis=0, keepdims=True),
@@ -552,7 +512,7 @@
     )
     heads_y[y] = mm(packed, place, NN, highest)
     head_y = [send(100 + k, heads_y.at[y], heads_y.at[y], ydev(k)) for k in (1, 2, 3)]
-    beta.second()
+    alpha.second()
     for copy in t1:
         copy.wait_recv()
     mixed = jnp.where(first, dbf[...], dcf[...]) + t1r[...]
@@ -560,68 +520,84 @@
     north = a == 0
     t2s[...] = jnp.where(north, dt2, mixed).astype(BF16)
     t2 = send(104, t2s, t2r, rank(2)[2])
-
-    def token(b, rows):
-        hgp[rows, :] = mm(rr[rows, 0:640], wf[:, 0:640], NT) + mm(rdt[rows, :], wf[:, 768:896], NT)
-
-    blocks(token, False)
+    for n in range(5):
+        part = slice(256 * n, 256 * n + 256)
+        hgp[:, part] = mm(rr[:, 0:640], wf[part, 0:640], NT) + mm(rdt[...], wf[part, 768:896], NT)
+    mate_row = ds((zl * 2 + 1 - c) * 128, 128)
+    far_mate = ds(((1 - zl) * 2 + 1 - c) * 128, 128)
+    far_row = ds(((1 - zl) * 2 + c) * 128, 128)
+    hgs[1] = hgp[far_mate, :].astype(BF16)
+    hg_far = send(106, hgs.at[1], hgr.at[1], core)
+    hgs[0] = hgp[mate_row, :].astype(BF16)
+    hg_near = send(105, hgs.at[0], hgr.at[0], core)
+    beta.second()
+    hg_far.wait_recv()
+    hgs[2] = (hgp[far_row, :] + hgr[1].astype(F32)).astype(BF16)
     t2.wait_recv()
+    hg_z = send(107, hgs.at[2], hgr.at[2], rank(2)[2])
     came = t2r[...].astype(F32)
     tile = projs[:, ds(256 * c, 128, 128)]
     upper_pick = ((mixed + came) * silu_grad(tile)).astype(BF16).astype(F32)
     lower_pick = jnp.where(first, dt2 + came, 0.0)
     rr[:, 640:768] = jnp.where(north, upper_pick, lower_pick).astype(BF16)
-    shr[...] = jnp.where(north, upper_pick, 0.0).astype(BF16)
+    shr[...] = jnp.where(north, upper_pick, lower_pick).astype(BF16)
     gamma.first()
-    hgc = []
-    for k in (2, 3, 1):
-        zlk, ck, dev = rank(k)
-        rows = ds((zlk * 2 + ck) * 128, 128)
-        hgs[k - 1] = (hgp[rows, :] + mm(shr[rows, :], wf[:, ds(lane0, 128)], NT)).astype(BF16)
-        hgc.append(send(104 + k, hgs.at[k - 1], hgr.at[k - 1], dev))
-    hgp[here_id, :] = hgp[here_id, :] + mm(shr[here_id, :], wf[:, ds(lane0, 128)], NT)
+    extras[g] = shr[here_id, :]
+    extra = [
+        send(111 + k, shr.at[ds((rank(k)[0] * 2 + rank(k)[1]) * 128, 128), :], extras.at[g], rank(k)[2])
+        for k in (2, 3, 1)
+    ]
+    alpha.third()
     gamma.second()
-    alpha.third()
     beta.third()
     for copy in head_y:
         copy.wait_recv()
     heads_x[x] = (heads_y[0] + heads_y[1]) + (heads_y[2] + heads_y[3])
     head_x = [send(107 + k, heads_x.at[x], heads_x.at[x], xdev(k)) for k in (1, 2, 3)]
+    alpha.fourth()
+    for copy in extra:
+        copy.wait_recv()
+    hgp[here_id, :] = hgp[here_id, :] + mm(extras[0], wf[:, 640:768], NT) + mm(extras[1], wf[:, 896:1024], NT)
     gamma.third()
     beta.fourth()
-    alpha.fourth()
     for copy in head_x:
         copy.wait_recv()
     heads_z[zh] = (heads_x[0] + heads_x[1]) + (heads_x[2] + heads_x[3])
     head_z = send(111, heads_z.at[zh], heads_z.at[zh], zpair)
+    alpha.owners()
     gamma.fourth()
     beta.owners()
-    alpha.owners()
-    gamma.owners()
+    hg_near.wait_recv()
+    hg_z.wait_recv()
+    hgo[...] = (hgp[here_id, :] + hgr[0].astype(F32) + hgr[2].astype(F32)).astype(BF16)
+    hg_out = pltpu.make_async_copy(hgo, hg_ref, ls.at[5])
+    hg_out.start()
     head_z.wait_recv()
     heads_g[r] = heads_z[0] + heads_z[1]
-    head_g = [send(111 + k, heads_g.at[r], heads_g.at[r], rank(k)[2]) for k in (1, 2, 3)]
-    for copy in hgc:
-        copy.wait_recv()
-    out = hgp[here_id, :] + hgr[0].astype(F32) + hgr[1].astype(F32) + hgr[2].astype(F32)
-    hg_ref[...] = out.astype(BF16)
+    head_g = [send(114 + k, heads_g.at[r], heads_g.at[r], rank(k)[2]) for k in (1, 2, 3)]
+    gamma.owners()
+    alpha.finish()
+    for k in range(4):
+        wgo[:, 640 * k : 640 * k + 384] = rd[k, 0:10, :]
     beta.finish()
     for k in range(4):
-        wg_ref[:, 640 * k + 384 : 640 * k + 640] = rdb[k, 0:10, :]
-    alpha.finish()
-    for k in range(4):
-        wg_ref[:, 640 * k : 640 * k + 384] = rd[k, 0:10, :]
-    gamma.finish()
-    wg_ref[:, 2560:2688] = rdc[0, 0:10, :]
-    wg_ref[:, 2688:2816] = rdc[1, 0:10, :]
-    wg_ref[:, 2816:2856] = rdc[2, 0:10, 0:40]
+        wgo[:, 640 * k + 384 : 640 * k + 640] = rdb[k, 0:10, :]
     for copy in head_g:
         copy.wait_recv()
-    hd_ref[...] = (heads_g[0] + heads_g[1]) + (heads_g[2] + heads_g[3])
+    hdo[...] = (heads_g[0] + heads_g[1]) + (heads_g[2] + heads_g[3])
+    hd_out = pltpu.make_async_copy(hdo, hd_ref, ls.at[6])
+    hd_out.start()
+    gamma.finish()
+    wgo[:, 2560:2688] = rdc[0, 0:10, :]
+    wgo[:, 2688:2816] = rdc[1, 0:10, :]
+    wgo[:, 2816:2856] = rdc[2, 0:10, 0:40]
+    wg_out = pltpu.make_async_copy(wgo, wg_ref, ls.at[7])
+    wg_out.start()
     for copy in pending:
         copy.wait_send()
-    for stream in (alpha, beta, gamma):
-        stream.close()
+    hg_out.wait()
+    hd_out.wait()
+    wg_out.wait()
 
 
 def scratch():
@@ -638,7 +614,7 @@
     wide, wide16 = v((512, COLS)), v((512, COLS), BF16)
     thin, thin16 = v((512, 128)), v((512, 128), BF16)
     return [
-        v((512, D), BF16), v((D, 512), BF16), wide16, v((160, 2856), BF16), v((D, 1024), BF16),
+        v((512, D), BF16), v((D, 512), BF16), v((D, 512), BF16), wide16, v((160, 2856), BF16), v((D, 1024), BF16),
         v((512, 384)), wide, thin, thin, thin, thin, v((4, 16, 128)), thin,
         v((4, 128, 128)), v((4, 128, 128)), v((4, 128, 128)),
         wide, wide, wide, wide, wide16, wide16, wide16, v((32, COLS)),
@@ -648,8 +624,9 @@
         v((512, 768), BF16), thin16, thin, thin, thin16, thin16, thin16, thin16, thin16,
         v((512, D)), v((3, 128, D), BF16), v((3, 128, D), BF16),
         *stream(384), *stream(256), *stream(128),
-        v((4, 8, 128)), v((4, 8, 128)), v((2, 8, 128)), v((4, 8, 128)),
-        pltpu.SemaphoreType.DMA((116,)), pltpu.SemaphoreType.DMA((116,)), pltpu.SemaphoreType.DMA((8,)),
+        v((4, 8, 128)), v((4, 8, 128)), v((2, 8, 128)), v((4, 8, 128)), v((4, 128, 128), BF16),
+        v((128, D), BF16), v((10, 2856)), v((8, 128)),
+        pltpu.SemaphoreType.DMA((120,)), pltpu.SemaphoreType.DMA((120,)), pltpu.SemaphoreType.DMA((8,)),
     ]
 
 
@@ -664,7 +641,7 @@
             jax.ShapeDtypeStruct((8, 128), F32),
         ),
         in_specs=[anyspace, anyspace, anyspace, vmem, vmem, vmem],
-        out_specs=(vmem, vmem, vmem),
+        out_specs=(anyspace, anyspace, anyspace),
         scratch_shapes=scratch(),
         compiler_params=pltpu.CompilerParams(has_side_effects=True, collective_id=0, vmem_limit_bytes=64000000),
     )(hidden[0], output_grad[0], input_weight, step_bias[None], decay_log[None], skip_gain[None])

time: 81.3 us -> 76.8 us (0.945)
  Pallas kernels: 76.7 us -> 72.2 us
    pallas_call x1, Pallas kernels: 76.7 us -> 72.2 us  [body(): pl.pallas_call(kernel, out_shape=(jax.ShapeDtypeStruct((128, D), BF16), j...]
where the time goes in v3:
time: 76.8 us; the launch traced here: 76.6 us
  Pallas kernels  72.2 us (94%)
  local copies, waits for them, and re-layouts  3.68 us (5%)
    pallas_call x1, Pallas kernels, body(): pl.pallas_call(kernel, out_shape=(jax.ShapeDtypeStruct((128, D), BF16), j...  72.2 us
    unnamed x6, local copies, waits for them, and re-layouts  3.1 us

profile of v3, /device:TPU:1, one launch (start us, length us, event | category | flops | bytes accessed | tf_op | source)
XLA Modules:
  0.0 76.6 jit_solution(13546459698092866079)
XLA Ops:
  0.6 72.2 %shard_map.85 = (bf16[128,1280]{1,0:T(8,128)(2,1)}, f32[10,2856]{1,0:T(8,128)}, f32[8,128]{1,0:T(8,128)}) custom-call(bf16[128,1280]{1,0:T(8,128)(2,1)} %bitcast.8, bf16[128,2560]{1,0:T(8,128)(2,1)} %bitcast.6, bf16[160,2856]{1,0:T(8,128)(2,1)} %w_ref.1, f32[1,40]{1,0:T(1,128)} %bitcast.9, f32[1,40]{1,0:T(1,128)} %bitcast.10, f32[1,40]{1,0:T(1,128)} %bitcast.11), custom_call_target="tpu_custom_call" | custom-call | tf_op jit(solution)/shard_map/pallas_call | solution.py:636
  72.9 0.0 copy-start.1
  72.9 0.7 copy-done.1
  73.6 0.6 slice.3
  74.1 0.0 copy-start
  74.1 1.8 %copy.11 = bf16[1,128,1280]{2,1,0:T(8,128)(2,1)} copy(bf16[1,128,1280]{2,1,0:T(8,128)(2,1)} %bitcast.7) | data formatting | bytes 655360
  75.9 0.0 copy-done
  75.9 0.7 copy.12
Async XLA Ops:
  72.9 0.7 copy-start.1
  74.1 1.8 %copy-start = (f32[10,2856]{1,0:T(8,128)S(1)}, f32[10,2856]{1,0:T(8,128)}, u32[]{:S(2)}) copy-start(f32[10,2856]{1,0:T(8,128)} %get-tuple-element.13) | copy-start | bytes 342724

commit v4 on v3

--- a/solution.py
+++ b/solution.py
@@ -45,9 +45,9 @@
     sexp, ecs, tls, vv, xb, xt, oe, tot,
     sl, dl, stt, tts, str_, ttr, q1s, dxin, dbf, dcf, sb, db, dd, red,
     rr, rdt, t1s, t1r, t1d, t1dr, t2s, t2r, shr, hgp, hgs, hgr,
-    dwa, sa1, ra1p, ra1m, sa2p, sa2m, ra2p, ra2m, sa3, ra3, sa4, ra4, sd, rd,
-    dwb, sb1, rb1p, rb1m, sb2p, sb2m, rb2p, rb2m, sb3, rb3, sb4, rb4, sdb, rdb,
-    dwc, sc1, rc1p, rc1m, sc2p, sc2m, rc2p, rc2m, sc3, rc3, sc4, rc4, sdc, rdc,
+    dwa, sa1, ra1, sa2, ra2, sa3, ra3, sa4, ra4, sda, rda,
+    dwb, sb1, rb1, sb2, rb2, sb3, rb3, sb4, rb4, sdb, rdb,
+    dwc, sc1, rc1, sc2, rc2, sc3, rc3, sc4, rc4, sdc, rdc,
     heads_y, heads_x, heads_z, heads_g, extras, hgo, wgo, hdo,
     ss, rs, ls,
 ):
@@ -56,16 +56,26 @@
     r = zl * 2 + c
     a = lax.rem(zl + zh, 2)
     g = a * 2 + c
-    pending = []
-
-    def send(i, src, dst, where):
+
+    def send(i, src, dst, where, group):
         copy = pltpu.make_async_remote_copy(
-            src_ref=src, dst_ref=dst, send_sem=ss.at[i], recv_sem=rs.at[i],
+            src_ref=src, dst_ref=dst, send_sem=ss.at[group], recv_sem=rs.at[i],
             device_id=where, device_id_type=MESH,
         )
         copy.start()
-        pending.append(copy)
         return copy
+
+    def bytes_of(ref, i=0, group=0):
+        return pltpu.make_async_remote_copy(
+            src_ref=ref, dst_ref=ref, send_sem=ss.at[group], recv_sem=rs.at[i],
+            device_id={"seq_2": 1 - c}, device_id_type=MESH,
+        )
+
+    def got(i, ref):
+        bytes_of(ref, i=i).wait_recv()
+
+    def sent(group, ref):
+        bytes_of(ref, group=group).wait_send()
 
     def rank(k):
         zlk = lax.rem(zl + k // 2, 2)
@@ -133,7 +143,8 @@
 
     def wsend(m, i, rows, dev):
         ref = wf.at[rows, cols(m)]
-        w[m, i] = send(9 * m + i, ref, ref, dev)
+        slot = min(i, 5) if m < 2 else {1: 1, 2: 2, 5: 3, 6: 4}.get(i, 5)
+        w[m, i] = send(6 * m + slot, ref, ref, dev, m)
 
     def w_own_x(m):
         wsend(m, 1, own, xdev(1))
@@ -169,38 +180,36 @@
         w[m, 6].wait_recv()
         wsend(m, 8, shard(x + 2, zh, 80, 80), zpair)
 
-    def w_done(m, which):
-        for i in which:
-            w[m, i].wait_recv()
+    def w_done(m):
+        got(6 * m + 5, wf.at[0 : 320 if m < 2 else 640, cols(m)])
 
     w_own_z(0)
     w_own_x(0)
-    h_z = send(37, hid_ref, hidf.at[here_id, :], rank(2)[2])
+    h_z = send(24, hid_ref, hidf.at[here_id, :], rank(2)[2], 4)
     w_own_z(1)
     w_own_x(1)
-    h_c = send(36, hid_ref, hidf.at[here_id, :], core)
-    cots = []
+    h_c = send(25, hid_ref, hidf.at[here_id, :], core, 4)
     for k in (2, 3, 1):
         zlk, ck, dev = rank(k)
         gk = lax.rem(zlk + zh, 2) * 2 + ck
-        cots.append(send(38 + k, cot_ref.at[:, ds(gk * COLS, COLS, 128)], cot.at[here_id, :], dev))
+        send(27, cot_ref.at[:, ds(gk * COLS, COLS, 128)], cot.at[here_id, :], dev, 5)
+    w_own_z(2)
+    w_own_z(3)
     w_other(0)
     w_forward(0)
+    w_forward_other(0)
+    w_other(1)
     w_own_x(2)
-    w_own_z(2)
-    w_other(1)
-    w_forward_other(0)
     w_forward(1)
     h_z.wait_recv()
     zrows = ds((rank(2)[0] * 2 + c) * 128, 128)
-    h_f = send(38, hidf.at[zrows, :], hidf.at[zrows, :], core)
+    h_f = send(26, hidf.at[zrows, :], hidf.at[zrows, :], core, 4)
     w_own_x(3)
-    w_own_z(3)
-    w_done(0, (5, 6, 7, 8))
-    mate = send(42, wf.at[:, ds(lane0, 128)], wf.at[:, ds(lane0, 128)], core)
+    w_done(0)
+    mate = send(28, wf.at[:, ds(lane0, 128)], wf.at[:, ds(lane0, 128)], core, 6)
+    w_forward_other(1)
     w_forward(2)
     w_across(2)
-    w_forward_other(1)
     h_c.wait_recv()
     h_f.wait_recv()
     mate.wait_recv()
@@ -254,15 +263,17 @@
             last_row = cums[128 * b + 127 : 128 * b + 128, :]
             tot[8 * b : 8 * b + 8, cj] = pair(jnp.broadcast_to(last_row, (8, 128)), j)
     tts[...] = tot[0:8, :] + tot[8:16, :] + tot[16:24, :] + tot[24:32, :]
-    totals = [send(43 + k, tts, ttr.at[k - 1], ydev(k)) for k in (1, 2, 3)]
+    for k in (1, 2, 3):
+        send(29, tts, ttr.at[k - 1], ydev(k), 7)
 
     def total(b, cj):
         return tot[8 * b : 8 * b + 1, cj]
 
-    states = {}
-
     def pair_forward(j):
         cj = slice(128 * j, 128 * j + 128)
+
+        def project(b, rows):
+            projv[rows, cj] = mm(hidf[rows, :], wf[:, cj])
 
         def local_part(b, rows):
             ce = pair(cums[rows, :], j)
@@ -283,7 +294,7 @@
             sl[b, :, cj] = mm(bmf[rows, :].astype(BF16), x16, TN)
             dl[b, :, cj] = mm(cmf[rows, :].astype(BF16), o16, TN)
 
-        projv[:, cj] = mm(hidf[...], wf[:, cj])
+        blocks(project)
         blocks(local_part)
         s = sl[0, :, cj]
         d = dl[3, :, cj]
@@ -294,7 +305,7 @@
         stt[1, :, cj] = d.astype(BF16)
         for k in (1, 2, 3):
             wraps = lax.div(y + k, 4)
-            states[j, k] = send(47 + 3 * j + k - 1, stt.at[wraps, :, cj], str_.at[k - 1, :, cj], ydev(k))
+            send(30 + j, stt.at[wraps, :, cj], str_.at[k - 1, :, cj], ydev(k), 8)
 
     def pair_inside(j):
         cj = slice(128 * j, 128 * j + 128)
@@ -334,9 +345,8 @@
     perm = jnp.where(k320 == source, 1.0, 0.0).astype(F32).astype(BF16)
     for q in range(4):
         hidt[320 * q : 320 * q + 320, :] = mm(perm, hidf[:, 320 * q : 320 * q + 320], NT).astype(BF16)
-    for copy in cots:
-        copy.wait_recv()
-    w_done(1, (5, 6, 7, 8))
+    got(27, cot.at[0:384, :])
+    w_done(1)
     pair_forward(0)
     w_across_far(2)
     pair_inside(0)
@@ -346,12 +356,12 @@
     w_across_far(3)
     pair_forward(1)
     pair_inside(1)
-    w_done(2, (0, 3, 4, 7, 8))
+    w_done(2)
     pair_forward(2)
     pair_inside(2)
     pair_forward(3)
     pair_inside(3)
-    w_done(3, (0, 3, 4, 7, 8))
+    w_done(3)
     pair_forward(4)
     pair_inside(4)
 
@@ -360,8 +370,7 @@
         dbf[rows, :] = mm(dgs[b], cmf[rows, :], TN, highest)
 
     blocks(turn)
-    for copy in totals:
-        copy.wait_recv()
+    got(29, ttr)
 
     lanes = lax.broadcasted_iota(jnp.int32, (256, 128), 0)
     outl = lax.broadcasted_iota(jnp.int32, (256, 128), 1)
@@ -379,12 +388,11 @@
 
     def pair_outside(j):
         cj = slice(128 * j, 128 * j + 128)
-        for k in (1, 2, 3):
-            states[j, k].wait_recv()
+        got(30 + j, str_.at[:, :, cj])
         t = [ttr[k, 0:1, cj] for k in range(3)]
-        got = [str_[k, :, cj].astype(F32) for k in range(3)]
-        s = yes[0] * got[0] + (yes[1] * jnp.exp(t[0])) * got[1] + (yes[2] * jnp.exp(t[0] + t[1])) * got[2]
-        d = no[0] * got[2] + (no[1] * jnp.exp(t[2])) * got[1] + (no[2] * jnp.exp(t[2] + t[1])) * got[0]
+        came = [str_[k, :, cj].astype(F32) for k in range(3)]
+        s = yes[0] * came[0] + (yes[1] * jnp.exp(t[0])) * came[1] + (yes[2] * jnp.exp(t[0] + t[1])) * came[2]
+        d = no[0] * came[2] + (no[1] * jnp.exp(t[2])) * came[1] + (no[2] * jnp.exp(t[2] + t[1])) * came[0]
         for b in (3, 2, 1, 0):
             db[b, :, cj] = d.astype(BF16)
             dd[b] = d
@@ -410,11 +418,13 @@
         blocks(outside)
 
     class Stream:
-        def __init__(self, base, lo, hi, kind, bufs):
-            self.base, self.lo, self.hi, self.left = base, lo, hi, hidx if kind else hidt
-            (self.dw, self.s1, self.r1p, self.r1m, self.s2p, self.s2m, self.r2p, self.r2m,
-             self.s3, self.r3, self.s4, self.r4, self.sd, self.rd) = bufs
+        def __init__(self, base, group, lo, hi, kind, bufs):
+            self.base, self.group, self.lo, self.hi, self.left = base, group, lo, hi, hidx if kind else hidt
+            self.dw, self.s1, self.r1, self.s2, self.r2, self.s3, self.r3, self.s4, self.r4, self.sd, self.rd = bufs
             self.index, self.dev, self.index2, self.dev2 = (y, ydev, x, xdev) if kind == 0 else (x, xdev, y, ydev)
+
+        def send(self, i, src, dst, dev):
+            return send(self.base + i, src, dst, dev, self.group)
 
         def first(self):
             for i in (2, 1, 3, 0):
@@ -423,40 +433,37 @@
                 if i == 2:
                     self.s1[...] = self.dw[rows, :].astype(BF16)
                     self.one = (
-                        send(self.base, self.s1.at[0:160, :], self.r1p, self.dev(1)),
-                        send(self.base + 1, self.s1.at[160:320, :], self.r1m, self.dev(-1)),
+                        self.send(0, self.s1.at[0:160, :], self.r1.at[0], self.dev(1)),
+                        self.send(1, self.s1.at[160:320, :], self.r1.at[1], self.dev(-1)),
                     )
 
         def second(self):
             nxt = lax.rem(self.index + 1, 4) * 320
             prv = lax.rem(self.index + 3, 4) * 320
             self.one[0].wait_recv()
-            self.s2p[0:160, :] = (self.dw[ds(nxt, 160), :] + self.r1p[...].astype(F32)).astype(BF16)
-            self.s2p[160:320, :] = self.dw[ds(nxt + 160, 160), :].astype(BF16)
-            up = send(self.base + 2, self.s2p, self.r2p, self.dev(1))
+            self.s2[0, 0:160, :] = (self.dw[ds(nxt, 160), :] + self.r1[0].astype(F32)).astype(BF16)
+            self.s2[0, 160:320, :] = self.dw[ds(nxt + 160, 160), :].astype(BF16)
+            self.send(2, self.s2.at[0], self.r2.at[0], self.dev(1))
             self.one[1].wait_recv()
-            self.s2m[0:160, :] = self.dw[ds(prv, 160), :].astype(BF16)
-            self.s2m[160:320, :] = (self.dw[ds(prv + 160, 160), :] + self.r1m[...].astype(F32)).astype(BF16)
-            self.two = (up, send(self.base + 3, self.s2m, self.r2m, self.dev(-1)))
+            self.s2[1, 0:160, :] = self.dw[ds(prv, 160), :].astype(BF16)
+            self.s2[1, 160:320, :] = (self.dw[ds(prv + 160, 160), :] + self.r1[1].astype(F32)).astype(BF16)
+            self.send(2, self.s2.at[1], self.r2.at[1], self.dev(-1))
 
         def third(self):
-            for copy in self.two:
-                copy.wait_recv()
+            got(self.base + 2, self.r2)
             here = ds(self.index * 320, 320)
-            summed = self.dw[here, :] + self.r2p[...].astype(F32) + self.r2m[...].astype(F32)
+            summed = self.dw[here, :] + self.r2[0].astype(F32) + self.r2[1].astype(F32)
             self.dw[here, :] = summed
             self.s3[...] = summed.astype(BF16)
-            self.three = [
-                send(self.base + 3 + k, self.s3.at[ds(lax.rem(self.index2 + k, 4) * 80, 80), :], self.r3.at[k - 1], self.dev2(k))
-                for k in (2, 1, 3)
-            ]
+            for k in (2, 1, 3):
+                piece = self.s3.at[ds(lax.rem(self.index2 + k, 4) * 80, 80), :]
+                self.send(3, piece, self.r3.at[k - 1], self.dev2(k))
 
         def fourth(self):
-            for copy in self.three:
-                copy.wait_recv()
+            got(self.base + 3, self.r3)
             rows = ds(self.index * 320 + self.index2 * 80, 80)
             self.s4[...] = self.dw[rows, :] + self.r3[0].astype(F32) + self.r3[1].astype(F32) + self.r3[2].astype(F32)
-            self.four = send(self.base + 11, self.s4.at[ds((1 - zh) * 40, 40), :], self.r4, zpair)
+            self.four = self.send(4, self.s4.at[ds((1 - zh) * 40, 40), :], self.r4, zpair)
 
         def owners(self):
             self.four.wait_recv()
@@ -464,18 +471,19 @@
             for i in range(4):
                 self.sd[i, 0:10, :] = chunk[10 * i : 10 * i + 10, :]
             self.rd[g] = self.sd[r]
-            self.five = [
-                send(self.base + 7 + k, self.sd.at[(rank(k)[0] * 2 + rank(k)[1])], self.rd.at[g], rank(k)[2])
-                for k in (2, 3, 1)
-            ]
+            for k in (2, 3, 1):
+                zlk, ck, dev = rank(k)
+                self.send(5, self.sd.at[zlk * 2 + ck], self.rd.at[g], dev)
 
         def finish(self):
-            for copy in self.five:
-                copy.wait_recv()
-
-    alpha = Stream(62, 0, 384, 0, (dwa, sa1, ra1p, ra1m, sa2p, sa2m, ra2p, ra2m, sa3, ra3, sa4, ra4, sd, rd))
-    beta = Stream(74, 384, 640, 1, (dwb, sb1, rb1p, rb1m, sb2p, sb2m, rb2p, rb2m, sb3, rb3, sb4, rb4, sdb, rdb))
-    gamma = Stream(86, 640, 768, 1, (dwc, sc1, rc1p, rc1m, sc2p, sc2m, rc2p, rc2m, sc3, rc3, sc4, rc4, sdc, rdc))
+            got(self.base + 5, self.rd.at[0:3])
+
+        def close(self):
+            sent(self.group, self.dw.at[0:688, :])
+
+    alpha = Stream(46, 13, 0, 384, 0, (dwa, sa1, ra1, sa2, ra2, sa3, ra3, sa4, ra4, sda, rda))
+    beta = Stream(52, 14, 384, 640, 1, (dwb, sb1, rb1, sb2, rb2, sb3, rb3, sb4, rb4, sdb, rdb))
+    gamma = Stream(58, 15, 640, 768, 1, (dwc, sc1, rc1, sc2, rc2, sc3, rc3, sc4, rc4, sdc, rdc))
 
     pair_outside(0)
     pair_outside(1)
@@ -502,7 +510,7 @@
     spread = mm(rdt[...], place.astype(BF16)).astype(BF16)
     t1d[...] = spread
     t1s[...] = jnp.where(first, dcf[...], dbf[...])
-    t1 = [send(98, t1s, t1r, core), send(99, t1d, t1dr, core)]
+    t1 = [send(35, t1s, t1r, core, 9), send(36, t1d, t1dr, core, 9)]
     beta.first()
     row8 = lax.broadcasted_iota(jnp.int32, (8, 128), 0)
     packed = jnp.where(
@@ -511,7 +519,8 @@
                   jnp.where(row8 == 2, gain[0].sum(axis=0, keepdims=True), 0.0)),
     )
     heads_y[y] = mm(packed, place, NN, highest)
-    head_y = [send(100 + k, heads_y.at[y], heads_y.at[y], ydev(k)) for k in (1, 2, 3)]
+    for k in (1, 2, 3):
+        send(38, heads_y.at[y], heads_y.at[y], ydev(k), 10)
     alpha.second()
     for copy in t1:
         copy.wait_recv()
@@ -519,7 +528,7 @@
     dt2 = spread.astype(F32) + t1dr[...].astype(F32)
     north = a == 0
     t2s[...] = jnp.where(north, dt2, mixed).astype(BF16)
-    t2 = send(104, t2s, t2r, rank(2)[2])
+    t2 = send(37, t2s, t2r, rank(2)[2], 9)
     for n in range(5):
         part = slice(256 * n, 256 * n + 256)
         hgp[:, part] = mm(rr[:, 0:640], wf[part, 0:640], NT) + mm(rdt[...], wf[part, 768:896], NT)
@@ -527,43 +536,40 @@
     far_mate = ds(((1 - zl) * 2 + 1 - c) * 128, 128)
     far_row = ds(((1 - zl) * 2 + c) * 128, 128)
     hgs[1] = hgp[far_mate, :].astype(BF16)
-    hg_far = send(106, hgs.at[1], hgr.at[1], core)
+    hg_far = send(43, hgs.at[1], hgr.at[1], core, 11)
     hgs[0] = hgp[mate_row, :].astype(BF16)
-    hg_near = send(105, hgs.at[0], hgr.at[0], core)
+    hg_near = send(42, hgs.at[0], hgr.at[0], core, 11)
     beta.second()
     hg_far.wait_recv()
     hgs[2] = (hgp[far_row, :] + hgr[1].astype(F32)).astype(BF16)
     t2.wait_recv()
-    hg_z = send(107, hgs.at[2], hgr.at[2], rank(2)[2])
     came = t2r[...].astype(F32)
     tile = projs[:, ds(256 * c, 128, 128)]
     upper_pick = ((mixed + came) * silu_grad(tile)).astype(BF16).astype(F32)
     lower_pick = jnp.where(first, dt2 + came, 0.0)
     rr[:, 640:768] = jnp.where(north, upper_pick, lower_pick).astype(BF16)
     shr[...] = jnp.where(north, upper_pick, lower_pick).astype(BF16)
+    for k in (2, 3, 1):
+        zlk, ck, dev = rank(k)
+        send(45, shr.at[ds((zlk * 2 + ck) * 128, 128), :], extras.at[g], dev, 12)
+    hg_z = send(44, hgs.at[2], hgr.at[2], rank(2)[2], 11)
     gamma.first()
     extras[g] = shr[here_id, :]
-    extra = [
-        send(111 + k, shr.at[ds((rank(k)[0] * 2 + rank(k)[1]) * 128, 128), :], extras.at[g], rank(k)[2])
-        for k in (2, 3, 1)
-    ]
     alpha.third()
     gamma.second()
     beta.third()
-    for copy in head_y:
-        copy.wait_recv()
+    got(38, heads_y.at[0:3])
     heads_x[x] = (heads_y[0] + heads_y[1]) + (heads_y[2] + heads_y[3])
-    head_x = [send(107 + k, heads_x.at[x], heads_x.at[x], xdev(k)) for k in (1, 2, 3)]
+    for k in (1, 2, 3):
+        send(39, heads_x.at[x], heads_x.at[x], xdev(k), 10)
     alpha.fourth()
-    for copy in extra:
-        copy.wait_recv()
+    gamma.third()
+    got(45, extras.at[0:3])
     hgp[here_id, :] = hgp[here_id, :] + mm(extras[0], wf[:, 640:768], NT) + mm(extras[1], wf[:, 896:1024], NT)
-    gamma.third()
     beta.fourth()
-    for copy in head_x:
-        copy.wait_recv()
+    got(39, heads_x.at[0:3])
     heads_z[zh] = (heads_x[0] + heads_x[1]) + (heads_x[2] + heads_x[3])
-    head_z = send(111, heads_z.at[zh], heads_z.at[zh], zpair)
+    head_z = send(40, heads_z.at[zh], heads_z.at[zh], zpair, 10)
     alpha.owners()
     gamma.fourth()
     beta.owners()
@@ -574,16 +580,16 @@
     hg_out.start()
     head_z.wait_recv()
     heads_g[r] = heads_z[0] + heads_z[1]
-    head_g = [send(114 + k, heads_g.at[r], heads_g.at[r], rank(k)[2]) for k in (1, 2, 3)]
+    for k in (1, 2, 3):
+        send(41, heads_g.at[r], heads_g.at[r], rank(k)[2], 10)
     gamma.owners()
     alpha.finish()
     for k in range(4):
-        wgo[:, 640 * k : 640 * k + 384] = rd[k, 0:10, :]
+        wgo[:, 640 * k : 640 * k + 384] = rda[k, 0:10, :]
     beta.finish()
     for k in range(4):
         wgo[:, 640 * k + 384 : 640 * k + 640] = rdb[k, 0:10, :]
-    for copy in head_g:
-        copy.wait_recv()
+    got(41, heads_g.at[0:3])
     hdo[...] = (heads_g[0] + heads_g[1]) + (heads_g[2] + heads_g[3])
     hd_out = pltpu.make_async_copy(hdo, hd_ref, ls.at[6])
     hd_out.start()
@@ -593,8 +599,19 @@
     wgo[:, 2816:2856] = rdc[2, 0:10, 0:40]
     wg_out = pltpu.make_async_copy(wgo, wg_ref, ls.at[7])
     wg_out.start()
-    for copy in pending:
-        copy.wait_send()
+    for m in range(4):
+        sent(m, wf.at[0:1120, cols(m)])
+    sent(4, hidf.at[0:384, :])
+    sent(5, cot.at[0:384, :])
+    sent(6, wf.at[:, ds(lane0, 128)])
+    sent(7, ttr)
+    sent(8, str_)
+    sent(9, dwc.at[0:1024, :])
+    sent(10, bmf.at[0:80, :])
+    sent(11, hgs)
+    sent(12, extras.at[0:3])
+    for stream in (alpha, beta, gamma):
+        stream.close()
     hg_out.wait()
     hd_out.wait()
     wg_out.wait()
@@ -605,10 +622,9 @@
         return pltpu.VMEM(shape, dtype)
 
     def stream(n):
-        half, whole = v((160, n), BF16), v((320, n), BF16)
         return [
-            v((D, n)), whole, half, half, whole, whole, whole, whole, whole,
-            v((3, 80, n), BF16), v((80, n)), v((40, n)), v((4, 16, n)), v((4, 16, n)),
+            v((D, n)), v((320, n), BF16), v((2, 160, n), BF16), v((2, 320, n), BF16), v((2, 320, n), BF16),
+            v((320, n), BF16), v((3, 80, n), BF16), v((80, n)), v((40, n)), v((4, 16, n)), v((4, 16, n)),
         ]
 
     wide, wide16 = v((512, COLS)), v((512, COLS), BF16)
@@ -626,8 +642,14 @@
         *stream(384), *stream(256), *stream(128),
         v((4, 8, 128)), v((4, 8, 128)), v((2, 8, 128)), v((4, 8, 128)), v((4, 128, 128), BF16),
         v((128, D), BF16), v((10, 2856)), v((8, 128)),
-        pltpu.SemaphoreType.DMA((120,)), pltpu.SemaphoreType.DMA((120,)), pltpu.SemaphoreType.DMA((8,)),
+        pltpu.SemaphoreType.DMA((16,)), pltpu.SemaphoreType.DMA((64,)), pltpu.SemaphoreType.DMA((8,)),
     ]
+
+
+def emit(hg_ref, wg_ref, hd_ref, hg_out, wg_out, hd_out):
+    hg_out[...] = hg_ref[...]
+    wg_out[...] = wg_ref[...]
+    hd_out[...] = hd_ref[0:3, 0:HEADS]
 
 
 def body(hidden, output_grad, input_weight, step_bias, decay_log, skip_gain):
@@ -645,7 +667,17 @@
         scratch_shapes=scratch(),
         compiler_params=pltpu.CompilerParams(has_side_effects=True, collective_id=0, vmem_limit_bytes=64000000),
     )(hidden[0], output_grad[0], input_weight, step_bias[None], decay_log[None], skip_gain[None])
-    return (hg[None], wg, hd[0:3, 0:HEADS])
+    hg, wg, hd = pl.pallas_call(
+        emit,
+        out_shape=(
+            jax.ShapeDtypeStruct((128, D), BF16),
+            jax.ShapeDtypeStruct((10, 2856), F32),
+            jax.ShapeDtypeStruct((3, HEADS), F32),
+        ),
+        in_specs=[vmem, vmem, vmem],
+        out_specs=(vmem, vmem, vmem),
+    )(hg, wg, hd)
+    return (hg[None], wg, hd)
 
 
 def solution(mesh):

time: 76.8 us -> 71.6 us (0.932)
  local copies, waits for them, and re-layouts: 3.68 us -> 0 us
  Pallas kernels: 72.2 us -> 70.8 us
    pallas_call x1, Pallas kernels: 72.2 us -> 69 us  [body(): pl.pallas_call(kernel, out_shape=(jax.ShapeDtypeStruct((128, D), BF16), j...]
    unnamed x6 -> x0, local copies, waits for them, and re-layouts: 3.1 us -> none
    pallas_call x0 -> x1, Pallas kernels: none -> 1.88 us  [body(): pl.pallas_call(emit, out_shape=(jax.ShapeDtypeStruct((128, D), BF16), jax...]
where the time goes in v4:
time: 71.6 us; the launch traced here: 71.5 us
  Pallas kernels  70.8 us (99%)
    pallas_call x1, Pallas kernels, body(): pl.pallas_call(kernel, out_shape=(jax.ShapeDtypeStruct((128, D), BF16), j...  69 us
    pallas_call x1, Pallas kernels, body(): pl.pallas_call(emit, out_shape=(jax.ShapeDtypeStruct((128, D), BF16), jax...  1.88 us

profile of v4, /device:TPU:1, one launch (start us, length us, event | category | flops | bytes accessed | tf_op | source)
XLA Modules:
  0.0 71.5 jit_solution(462980058761151038)
XLA Ops:
  0.6 69.0 %shard_map.85 = (bf16[128,1280]{1,0:T(8,128)(2,1)}, f32[10,2856]{1,0:T(8,128)}, f32[8,128]{1,0:T(8,128)}) custom-call(bf16[128,1280]{1,0:T(8,128)(2,1)} %bitcast.7, bf16[128,2560]{1,0:T(8,128)(2,1)} %bitcast.6, bf16[160,2856]{1,0:T(8,128)(2,1)} %w_ref.1, f32[1,40]{1,0:T(1,128)} %bitcast.8, f32[1,40]{1,0:T(1,128)} %bitcast.9, f32[1,40]{1,0:T(1,128)} %bitcast.10), custom_call_target="tpu_custom_call" | custom-call | tf_op jit(solution)/shard_map/pallas_call | solution.py:658
  69.6 1.9 %shard_map.86 = (bf16[128,1280]{1,0:T(8,128)(2,1)}, f32[10,2856]{1,0:T(8,128)}, f32[3,40]{1,0:T(4,128)}) custom-call(bf16[128,1280]{1,0:T(8,128)(2,1)} %get-tuple-element.9.hg_ref, f32[10,2856]{1,0:T(8,128)} %get-tuple-element.10.wg_ref, f32[8,128]{1,0:T(8,128)} %get-tuple-element.11.hd_ref), custom_call_target="tpu_custom_call" | custom-call | tf_op jit(solution)/shard_map/pallas_call | solution.py:670

commit v5 on v4

--- a/solution.py
+++ b/solution.py
@@ -44,11 +44,11 @@
     hidf, hidt, hidx, cot, wraw, wf, projs, projv, bmf, cmf, lgd, cums, cumt, stp, gs, gts, dgs,
     sexp, ecs, tls, vv, xb, xt, oe, tot,
     sl, dl, stt, tts, str_, ttr, q1s, dxin, dbf, dcf, sb, db, dd, red,
-    rr, rdt, t1s, t1r, t1d, t1dr, t2s, t2r, shr, hgp, hgs, hgr,
+    rr, t1s, t1r, hgp, hgs, hgr,
     dwa, sa1, ra1, sa2, ra2, sa3, ra3, sa4, ra4, sda, rda,
     dwb, sb1, rb1, sb2, rb2, sb3, rb3, sb4, rb4, sdb, rdb,
     dwc, sc1, rc1, sc2, rc2, sc3, rc3, sc4, rc4, sdc, rdc,
-    heads_y, heads_x, heads_z, heads_g, extras, hgo, wgo, hdo,
+    heads_y, heads_x, heads_z, heads_g, hgo, wgo, hdo,
     ss, rs, ls,
 ):
     y, zl, c = (lax.axis_index(n) for n in SEQ)
@@ -186,8 +186,8 @@
     w_own_z(0)
     w_own_x(0)
     h_z = send(24, hid_ref, hidf.at[here_id, :], rank(2)[2], 4)
+    w_own_x(2)
     w_own_z(1)
-    w_own_x(1)
     h_c = send(25, hid_ref, hidf.at[here_id, :], core, 4)
     for k in (2, 3, 1):
         zlk, ck, dev = rank(k)
@@ -197,19 +197,20 @@
     w_own_z(3)
     w_other(0)
     w_forward(0)
+    w_forward(2)
+    w_across(2)
+    w_own_x(3)
     w_forward_other(0)
-    w_other(1)
-    w_own_x(2)
-    w_forward(1)
+    w_own_x(1)
     h_z.wait_recv()
     zrows = ds((rank(2)[0] * 2 + c) * 128, 128)
     h_f = send(26, hidf.at[zrows, :], hidf.at[zrows, :], core, 4)
-    w_own_x(3)
+    w_across_far(2)
+    w_forward(3)
+    w_across(3)
+    w_other(1)
     w_done(0)
     mate = send(28, wf.at[:, ds(lane0, 128)], wf.at[:, ds(lane0, 128)], core, 6)
-    w_forward_other(1)
-    w_forward(2)
-    w_across(2)
     h_c.wait_recv()
     h_f.wait_recv()
     mate.wait_recv()
@@ -256,7 +257,13 @@
         dgs[b] = jnp.zeros((128, 128), F32)
         red[b] = jnp.zeros((384, 128), F32)
 
-    blocks(common)
+    common(0, pl.ds(0, 128))
+    w_forward(1)
+    w_across_far(3)
+    common(1, pl.ds(128, 128))
+    common(2, pl.ds(256, 128))
+    w_forward_other(1)
+    common(3, pl.ds(384, 128))
     for j in range(5):
         cj = slice(128 * j, 128 * j + 128)
         for b in range(4):
@@ -335,9 +342,6 @@
 
         blocks(inside)
 
-    w_forward(3)
-    w_across(3)
-
     i320 = lax.broadcasted_iota(jnp.int32, (320, 320), 0)
     k320 = lax.broadcasted_iota(jnp.int32, (320, 320), 1)
     tens = lax.shift_right_logical(i320 * 6554, 16)
@@ -346,16 +350,6 @@
     for q in range(4):
         hidt[320 * q : 320 * q + 320, :] = mm(perm, hidf[:, 320 * q : 320 * q + 320], NT).astype(BF16)
     got(27, cot.at[0:384, :])
-    w_done(1)
-    pair_forward(0)
-    w_across_far(2)
-    pair_inside(0)
-    for p in range(4):
-        for q in range(4):
-            hidx[320 * p + 80 * q : 320 * p + 80 * q + 80, :] = hidt[320 * q + 80 * p : 320 * q + 80 * p + 80, :]
-    w_across_far(3)
-    pair_forward(1)
-    pair_inside(1)
     w_done(2)
     pair_forward(2)
     pair_inside(2)
@@ -364,6 +358,14 @@
     w_done(3)
     pair_forward(4)
     pair_inside(4)
+    for p in range(4):
+        for q in range(4):
+            hidx[320 * p + 80 * q : 320 * p + 80 * q + 80, :] = hidt[320 * q + 80 * p : 320 * q + 80 * p + 80, :]
+    w_done(1)
+    pair_forward(0)
+    pair_inside(0)
+    pair_forward(1)
+    pair_inside(1)
 
     def turn(b, rows):
         dcf[rows, :] = mm(dgs[b], bmf[rows, :], NN, highest)
@@ -481,16 +483,16 @@
         def close(self):
             sent(self.group, self.dw.at[0:688, :])
 
-    alpha = Stream(46, 13, 0, 384, 0, (dwa, sa1, ra1, sa2, ra2, sa3, ra3, sa4, ra4, sda, rda))
-    beta = Stream(52, 14, 384, 640, 1, (dwb, sb1, rb1, sb2, rb2, sb3, rb3, sb4, rb4, sdb, rdb))
-    gamma = Stream(58, 15, 640, 768, 1, (dwc, sc1, rc1, sc2, rc2, sc3, rc3, sc4, rc4, sdc, rdc))
-
+    alpha = Stream(46, 13, 256, 640, 0, (dwa, sa1, ra1, sa2, ra2, sa3, ra3, sa4, ra4, sda, rda))
+    beta = Stream(52, 14, 0, 256, 1, (dwb, sb1, rb1, sb2, rb2, sb3, rb3, sb4, rb4, sdb, rdb))
+    gamma = Stream(58, 15, 640, 896, 1, (dwc, sc1, rc1, sc2, rc2, sc3, rc3, sc4, rc4, sdc, rdc))
+
+    pair_outside(2)
+    pair_outside(3)
+    pair_outside(4)
+    alpha.first()
     pair_outside(0)
     pair_outside(1)
-    pair_outside(2)
-    alpha.first()
-    pair_outside(3)
-    pair_outside(4)
 
     ownl = coli < 10
     bias_sum = decay_sum = jnp.zeros((8, 128), F32)
@@ -502,15 +504,13 @@
         dlog = jnp.where(ownl, dlog + inner[b].sum(axis=0, keepdims=True), 0.0)
         ddt = (red[b, 256:384] + neg * dlog) * jax.nn.sigmoid(projs[rows, 128:256] + bias)
         ddt = jnp.where(ownl, ddt, 0.0)
-        rdt[rows, :] = ddt.astype(BF16)
+        rr[rows, 768:896] = ddt.astype(BF16)
         bias_sum = bias_sum + ddt.reshape(16, 8, 128).sum(axis=0)
         decay_sum = decay_sum + (dlog * lgd[rows, :]).reshape(16, 8, 128).sum(axis=0)
     first = c == 0
     place = jnp.where(jnp.logical_and(rowi < 10, coli == rowi + 10 * g), 1.0, 0.0).astype(F32)
-    spread = mm(rdt[...], place.astype(BF16)).astype(BF16)
-    t1d[...] = spread
     t1s[...] = jnp.where(first, dcf[...], dbf[...])
-    t1 = [send(35, t1s, t1r, core, 9), send(36, t1d, t1dr, core, 9)]
+    t1 = send(35, t1s, t1r, core, 9)
     beta.first()
     row8 = lax.broadcasted_iota(jnp.int32, (8, 128), 0)
     packed = jnp.where(
@@ -522,16 +522,17 @@
     for k in (1, 2, 3):
         send(38, heads_y.at[y], heads_y.at[y], ydev(k), 10)
     alpha.second()
-    for copy in t1:
-        copy.wait_recv()
+    t1.wait_recv()
     mixed = jnp.where(first, dbf[...], dcf[...]) + t1r[...]
-    dt2 = spread.astype(F32) + t1dr[...].astype(F32)
-    north = a == 0
-    t2s[...] = jnp.where(north, dt2, mixed).astype(BF16)
-    t2 = send(37, t2s, t2r, rank(2)[2], 9)
+    rr[:, 640:768] = (mixed * silu_grad(projs[:, ds(256 * c, 128, 128)])).astype(BF16)
+    gamma.first()
     for n in range(5):
         part = slice(256 * n, 256 * n + 256)
-        hgp[:, part] = mm(rr[:, 0:640], wf[part, 0:640], NT) + mm(rdt[...], wf[part, 768:896], NT)
+        hgp[:, part] = (
+            mm(rr[:, 0:640], wf[part, 0:640], NT)
+            + mm(rr[:, 640:768], wf[part, ds(lane0, 128)], NT)
+            + mm(rr[:, 768:896], wf[part, 768:896], NT)
+        )
     mate_row = ds((zl * 2 + 1 - c) * 128, 128)
     far_mate = ds(((1 - zl) * 2 + 1 - c) * 128, 128)
     far_row = ds(((1 - zl) * 2 + c) * 128, 128)
@@ -542,19 +543,7 @@
     beta.second()
     hg_far.wait_recv()
     hgs[2] = (hgp[far_row, :] + hgr[1].astype(F32)).astype(BF16)
-    t2.wait_recv()
-    came = t2r[...].astype(F32)
-    tile = projs[:, ds(256 * c, 128, 128)]
-    upper_pick = ((mixed + came) * silu_grad(tile)).astype(BF16).astype(F32)
-    lower_pick = jnp.where(first, dt2 + came, 0.0)
-    rr[:, 640:768] = jnp.where(north, upper_pick, lower_pick).astype(BF16)
-    shr[...] = jnp.where(north, upper_pick, lower_pick).astype(BF16)
-    for k in (2, 3, 1):
-        zlk, ck, dev = rank(k)
-        send(45, shr.at[ds((zlk * 2 + ck) * 128, 128), :], extras.at[g], dev, 12)
     hg_z = send(44, hgs.at[2], hgr.at[2], rank(2)[2], 11)
-    gamma.first()
-    extras[g] = shr[here_id, :]
     alpha.third()
     gamma.second()
     beta.third()
@@ -564,8 +553,6 @@
         send(39, heads_x.at[x], heads_x.at[x], xdev(k), 10)
     alpha.fourth()
     gamma.third()
-    got(45, extras.at[0:3])
-    hgp[here_id, :] = hgp[here_id, :] + mm(extras[0], wf[:, 640:768], NT) + mm(extras[1], wf[:, 896:1024], NT)
     beta.fourth()
     got(39, heads_x.at[0:3])
     heads_z[zh] = (heads_x[0] + heads_x[1]) + (heads_x[2] + heads_x[3])
@@ -585,18 +572,19 @@
     gamma.owners()
     alpha.finish()
     for k in range(4):
-        wgo[:, 640 * k : 640 * k + 384] = rda[k, 0:10, :]
+        wgo[:, 640 * k + 256 : 640 * k + 640] = rda[k, 0:10, :]
     beta.finish()
     for k in range(4):
-        wgo[:, 640 * k + 384 : 640 * k + 640] = rdb[k, 0:10, :]
+        wgo[:, 640 * k : 640 * k + 256] = rdb[k, 0:10, :]
     got(41, heads_g.at[0:3])
     hdo[...] = (heads_g[0] + heads_g[1]) + (heads_g[2] + heads_g[3])
     hd_out = pltpu.make_async_copy(hdo, hd_ref, ls.at[6])
     hd_out.start()
     gamma.finish()
-    wgo[:, 2560:2688] = rdc[0, 0:10, :]
-    wgo[:, 2688:2816] = rdc[1, 0:10, :]
-    wgo[:, 2816:2856] = rdc[2, 0:10, 0:40]
+    wgo[:, 2560:2688] = rdc[0, 0:10, 0:128] + rdc[2, 0:10, 0:128]
+    wgo[:, 2688:2816] = rdc[1, 0:10, 0:128] + rdc[3, 0:10, 0:128]
+    for k in range(4):
+        wgo[:, 2816 + 10 * k : 2826 + 10 * k] = rdc[k, 0:10, 128:138]
     wg_out = pltpu.make_async_copy(wgo, wg_ref, ls.at[7])
     wg_out.start()
     for m in range(4):
@@ -606,10 +594,9 @@
     sent(6, wf.at[:, ds(lane0, 128)])
     sent(7, ttr)
     sent(8, str_)
-    sent(9, dwc.at[0:1024, :])
+    sent(9, t1r)
     sent(10, bmf.at[0:80, :])
     sent(11, hgs)
-    sent(12, extras.at[0:3])
     for stream in (alpha, beta, gamma):
         stream.close()
     hg_out.wait()
@@ -628,7 +615,7 @@
         ]
 
     wide, wide16 = v((512, COLS)), v((512, COLS), BF16)
-    thin, thin16 = v((512, 128)), v((512, 128), BF16)
+    thin = v((512, 128))
     return [
         v((512, D), BF16), v((D, 512), BF16), v((D, 512), BF16), wide16, v((160, 2856), BF16), v((D, 1024), BF16),
         v((512, 384)), wide, thin, thin, thin, thin, v((4, 16, 128)), thin,
@@ -637,10 +624,10 @@
         v((4, 128, COLS)), v((4, 128, COLS)), v((2, 128, COLS), BF16), v((8, COLS)),
         v((3, 128, COLS), BF16), v((3, 8, COLS)), wide, wide, thin, thin,
         v((4, 128, COLS), BF16), v((4, 128, COLS), BF16), v((4, 128, 128)), v((4, 384, 128)),
-        v((512, 768), BF16), thin16, thin, thin, thin16, thin16, thin16, thin16, thin16,
+        v((512, 896), BF16), thin, thin,
         v((512, D)), v((3, 128, D), BF16), v((3, 128, D), BF16),
-        *stream(384), *stream(256), *stream(128),
-        v((4, 8, 128)), v((4, 8, 128)), v((2, 8, 128)), v((4, 8, 128)), v((4, 128, 128), BF16),
+        *stream(384), *stream(256), *stream(256),
+        v((4, 8, 128)), v((4, 8, 128)), v((2, 8, 128)), v((4, 8, 128)),
         v((128, D), BF16), v((10, 2856)), v((8, 128)),
         pltpu.SemaphoreType.DMA((16,)), pltpu.SemaphoreType.DMA((64,)), pltpu.SemaphoreType.DMA((8,)),
     ]

time: 71.6 us -> 69.7 us (0.973)
  Pallas kernels: 70.8 us -> 68.9 us
    pallas_call x1, Pallas kernels: 69 us -> 67.1 us  [body(): pl.pallas_call(kernel, out_shape=(jax.ShapeDtypeStruct((128, D), BF16), j...]
where the time goes in v5:
time: 69.7 us; the launch traced here: 69.6 us
  Pallas kernels  68.9 us (99%)
    pallas_call x1, Pallas kernels, body(): pl.pallas_call(kernel, out_shape=(jax.ShapeDtypeStruct((128, D), BF16), j...  67.1 us
    pallas_call x1, Pallas kernels, body(): pl.pallas_call(emit, out_shape=(jax.ShapeDtypeStruct((128, D), BF16), jax...  1.88 us

profile of v5, /device:TPU:1, one launch (start us, length us, event | category | flops | bytes accessed | tf_op | source)
XLA Modules:
  0.0 69.6 jit_solution(1457791767068293606)
XLA Ops:
  0.6 67.1 %shard_map.85 = (bf16[128,1280]{1,0:T(8,128)(2,1)}, f32[10,2856]{1,0:T(8,128)}, f32[8,128]{1,0:T(8,128)}) custom-call(bf16[128,1280]{1,0:T(8,128)(2,1)} %bitcast.7, bf16[128,2560]{1,0:T(8,128)(2,1)} %bitcast.6, bf16[160,2856]{1,0:T(8,128)(2,1)} %w_ref.1, f32[1,40]{1,0:T(1,128)} %bitcast.8, f32[1,40]{1,0:T(1,128)} %bitcast.9, f32[1,40]{1,0:T(1,128)} %bitcast.10), custom_call_target="tpu_custom_call" | custom-call | tf_op jit(solution)/shard_map/pallas_call | solution.py:645
  67.7 1.9 %shard_map.86 = (bf16[128,1280]{1,0:T(8,128)(2,1)}, f32[10,2856]{1,0:T(8,128)}, f32[3,40]{1,0:T(4,128)}) custom-call(bf16[128,1280]{1,0:T(8,128)(2,1)} %get-tuple-element.9.hg_ref, f32[10,2856]{1,0:T(8,128)} %get-tuple-element.10.wg_ref, f32[8,128]{1,0:T(8,128)} %get-tuple-element.11.hd_ref), custom_call_target="tpu_custom_call" | custom-call | tf_op jit(solution)/shard_map/pallas_call | solution.py:657

commit v6 on v5

--- a/solution.py
+++ b/solution.py
@@ -182,6 +182,10 @@
 
     def w_done(m):
         got(6 * m + 5, wf.at[0 : 320 if m < 2 else 640, cols(m)])
+
+    def hand(k):
+        ref = wf.at[ds(lax.rem(x + k + 4, 4) * 320, 320), ds(lane0, 128)]
+        send(28, ref, ref, core, 6)
 
     w_own_z(0)
     w_own_x(0)
@@ -202,6 +206,8 @@
     w_own_x(3)
     w_forward_other(0)
     w_own_x(1)
+    for k in (-1, 0, 1):
+        hand(k)
     h_z.wait_recv()
     zrows = ds((rank(2)[0] * 2 + c) * 128, 128)
     h_f = send(26, hidf.at[zrows, :], hidf.at[zrows, :], core, 4)
@@ -210,10 +216,9 @@
     w_across(3)
     w_other(1)
     w_done(0)
-    mate = send(28, wf.at[:, ds(lane0, 128)], wf.at[:, ds(lane0, 128)], core, 6)
+    hand(2)
     h_c.wait_recv()
     h_f.wait_recv()
-    mate.wait_recv()
 
     low = coli < 64
     causal = rowi >= coli
@@ -236,14 +241,9 @@
 
             lax.fori_loop(0, 4, step, 0)
 
-    def common(b, rows):
-        p = mm(hidf[rows, :], wf[:, 640:1024])
-        projs[rows, :] = p
-        bm = jax.nn.silu(p[:, 0:128])
-        cm = jax.nn.silu(p[:, 256:384])
-        bmf[rows, :] = bm
-        cmf[rows, :] = cm
-        pre = p[:, 128:256] + bias
+    def steps(b, rows):
+        projs[rows, ds(128 * c, 256, 128)] = mm(hidf[rows, :], wf[:, ds(640 + 128 * c, 256, 128)])
+        pre = projs[rows, 128:256] + bias
         step = jnp.maximum(pre, 0.0) + jnp.log1p(jnp.exp(-jnp.abs(pre)))
         lg = neg * step
         cum = mm(tri, lg, NN, highest)
@@ -251,19 +251,20 @@
         lgd[rows, :] = lg
         cums[rows, :] = cum
         cumt[b] = cum.T[0:16, :]
+        dgs[b] = jnp.zeros((128, 128), F32)
+        red[b] = jnp.zeros((384, 128), F32)
+
+    def maps(b, rows):
+        projs[rows, ds(256 - 256 * c, 128)] = mm(hidf[rows, :], wf[:, ds(896 - 256 * c, 128)])
+        bm = jax.nn.silu(projs[rows, 0:128])
+        cm = jax.nn.silu(projs[rows, 256:384])
+        bmf[rows, :] = bm
+        cmf[rows, :] = cm
         scores = mm(cm, bm, NT, highest)
         gs[b] = scores
         gts[b] = scores.T
-        dgs[b] = jnp.zeros((128, 128), F32)
-        red[b] = jnp.zeros((384, 128), F32)
-
-    common(0, pl.ds(0, 128))
-    w_forward(1)
-    w_across_far(3)
-    common(1, pl.ds(128, 128))
-    common(2, pl.ds(256, 128))
-    w_forward_other(1)
-    common(3, pl.ds(384, 128))
+
+    blocks(steps)
     for j in range(5):
         cj = slice(128 * j, 128 * j + 128)
         for b in range(4):
@@ -273,14 +274,32 @@
     for k in (1, 2, 3):
         send(29, tts, ttr.at[k - 1], ydev(k), 7)
 
+    i320 = lax.broadcasted_iota(jnp.int32, (320, 320), 0)
+    k320 = lax.broadcasted_iota(jnp.int32, (320, 320), 1)
+    tens = lax.shift_right_logical(i320 * 6554, 16)
+    source = ((tens & 3) * 8 + lax.shift_right_logical(tens, 2)) * 10 + i320 - tens * 10
+    perm = jnp.where(k320 == source, 1.0, 0.0).astype(F32).astype(BF16)
+    for q in range(4):
+        hidt[320 * q : 320 * q + 320, :] = mm(perm, hidf[:, 320 * q : 320 * q + 320], NT).astype(BF16)
+    w_forward(1)
+    got(28, wf.at[:, ds(896 - 256 * c, 128)])
+    maps(0, pl.ds(0, 128))
+    w_across_far(3)
+    maps(1, pl.ds(128, 128))
+    maps(2, pl.ds(256, 128))
+    w_forward_other(1)
+    maps(3, pl.ds(384, 128))
+
     def total(b, cj):
         return tot[8 * b : 8 * b + 1, cj]
 
     def pair_forward(j):
         cj = slice(128 * j, 128 * j + 128)
 
+        wide = slice(128 * j, min(128 * j + 256, 640))
+
         def project(b, rows):
-            projv[rows, cj] = mm(hidf[rows, :], wf[:, cj])
+            projv[rows, wide] = mm(hidf[rows, :], wf[:, wide])
 
         def local_part(b, rows):
             ce = pair(cums[rows, :], j)
@@ -301,7 +320,8 @@
             sl[b, :, cj] = mm(bmf[rows, :].astype(BF16), x16, TN)
             dl[b, :, cj] = mm(cmf[rows, :].astype(BF16), o16, TN)
 
-        blocks(project)
+        if j % 2 == 0:
+            blocks(project)
         blocks(local_part)
         s = sl[0, :, cj]
         d = dl[3, :, cj]
@@ -342,13 +362,6 @@
 
         blocks(inside)
 
-    i320 = lax.broadcasted_iota(jnp.int32, (320, 320), 0)
-    k320 = lax.broadcasted_iota(jnp.int32, (320, 320), 1)
-    tens = lax.shift_right_logical(i320 * 6554, 16)
-    source = ((tens & 3) * 8 + lax.shift_right_logical(tens, 2)) * 10 + i320 - tens * 10
-    perm = jnp.where(k320 == source, 1.0, 0.0).astype(F32).astype(BF16)
-    for q in range(4):
-        hidt[320 * q : 320 * q + 320, :] = mm(perm, hidf[:, 320 * q : 320 * q + 320], NT).astype(BF16)
     got(27, cot.at[0:384, :])
     w_done(2)
     pair_forward(2)
@@ -431,7 +444,8 @@
         def first(self):
             for i in (2, 1, 3, 0):
                 rows = ds(lax.rem(self.index + i, 4) * 320, 320)
-                self.dw[rows, :] = mm(self.left[rows, :], rr[:, self.lo : self.hi])
+                cols = slice(self.lo, self.hi) if self.hi else ds(640 + 128 * c, 256, 128)
+                self.dw[rows, :] = mm(self.left[rows, :], rr[:, cols])
                 if i == 2:
                     self.s1[...] = self.dw[rows, :].astype(BF16)
                     self.one = (
@@ -485,7 +499,7 @@
 
     alpha = Stream(46, 13, 256, 640, 0, (dwa, sa1, ra1, sa2, ra2, sa3, ra3, sa4, ra4, sda, rda))
     beta = Stream(52, 14, 0, 256, 1, (dwb, sb1, rb1, sb2, rb2, sb3, rb3, sb4, rb4, sdb, rdb))
-    gamma = Stream(58, 15, 640, 896, 1, (dwc, sc1, rc1, sc2, rc2, sc3, rc3, sc4, rc4, sdc, rdc))
+    gamma = Stream(58, 15, 640, None, 1, (dwc, sc1, rc1, sc2, rc2, sc3, rc3, sc4, rc4, sdc, rdc))
 
     pair_outside(2)
     pair_outside(3)
@@ -524,15 +538,12 @@
     alpha.second()
     t1.wait_recv()
     mixed = jnp.where(first, dbf[...], dcf[...]) + t1r[...]
-    rr[:, 640:768] = (mixed * silu_grad(projs[:, ds(256 * c, 128, 128)])).astype(BF16)
+    rr[:, ds(lane0, 128)] = (mixed * silu_grad(projs[:, ds(256 * c, 128, 128)])).astype(BF16)
+    rr[:, ds(896 - 256 * c, 128)] = jnp.zeros((512, 128), BF16)
     gamma.first()
     for n in range(5):
         part = slice(256 * n, 256 * n + 256)
-        hgp[:, part] = (
-            mm(rr[:, 0:640], wf[part, 0:640], NT)
-            + mm(rr[:, 640:768], wf[part, ds(lane0, 128)], NT)
-            + mm(rr[:, 768:896], wf[part, 768:896], NT)
-        )
+        hgp[:, part] = mm(rr[...], wf[part, :], NT)
     mate_row = ds((zl * 2 + 1 - c) * 128, 128)
     far_mate = ds(((1 - zl) * 2 + 1 - c) * 128, 128)
     far_row = ds(((1 - zl) * 2 + c) * 128, 128)
@@ -544,22 +555,22 @@
     hg_far.wait_recv()
     hgs[2] = (hgp[far_row, :] + hgr[1].astype(F32)).astype(BF16)
     hg_z = send(44, hgs.at[2], hgr.at[2], rank(2)[2], 11)
+    gamma.second()
     alpha.third()
-    gamma.second()
     beta.third()
     got(38, heads_y.at[0:3])
     heads_x[x] = (heads_y[0] + heads_y[1]) + (heads_y[2] + heads_y[3])
     for k in (1, 2, 3):
         send(39, heads_x.at[x], heads_x.at[x], xdev(k), 10)
-    alpha.fourth()
     gamma.third()
     beta.fourth()
     got(39, heads_x.at[0:3])
     heads_z[zh] = (heads_x[0] + heads_x[1]) + (heads_x[2] + heads_x[3])
     head_z = send(40, heads_z.at[zh], heads_z.at[zh], zpair, 10)
-    alpha.owners()
+    alpha.fourth()
     gamma.fourth()
     beta.owners()
+    alpha.owners()
     hg_near.wait_recv()
     hg_z.wait_recv()
     hgo[...] = (hgp[here_id, :] + hgr[0].astype(F32) + hgr[2].astype(F32)).astype(BF16)
@@ -570,21 +581,22 @@
     for k in (1, 2, 3):
         send(41, heads_g.at[r], heads_g.at[r], rank(k)[2], 10)
     gamma.owners()
+    beta.finish()
+    for k in range(4):
+        wgo[:, 640 * k : 640 * k + 256] = rdb[k, 0:10, :]
     alpha.finish()
     for k in range(4):
         wgo[:, 640 * k + 256 : 640 * k + 640] = rda[k, 0:10, :]
-    beta.finish()
-    for k in range(4):
-        wgo[:, 640 * k : 640 * k + 256] = rdb[k, 0:10, :]
     got(41, heads_g.at[0:3])
     hdo[...] = (heads_g[0] + heads_g[1]) + (heads_g[2] + heads_g[3])
     hd_out = pltpu.make_async_copy(hdo, hd_ref, ls.at[6])
     hd_out.start()
     gamma.finish()
     wgo[:, 2560:2688] = rdc[0, 0:10, 0:128] + rdc[2, 0:10, 0:128]
-    wgo[:, 2688:2816] = rdc[1, 0:10, 0:128] + rdc[3, 0:10, 0:128]
+    wgo[:, 2688:2816] = rdc[1, 0:10, 128:256] + rdc[3, 0:10, 128:256]
     for k in range(4):
-        wgo[:, 2816 + 10 * k : 2826 + 10 * k] = rdc[k, 0:10, 128:138]
+        lane = 128 - 128 * (k % 2)
+        wgo[:, 2816 + 10 * k : 2826 + 10 * k] = rdc[k, 0:10, lane : lane + 10]
     wg_out = pltpu.make_async_copy(wgo, wg_ref, ls.at[7])
     wg_out.start()
     for m in range(4):
@@ -624,7 +636,7 @@
         v((4, 128, COLS)), v((4, 128, COLS)), v((2, 128, COLS), BF16), v((8, COLS)),
         v((3, 128, COLS), BF16), v((3, 8, COLS)), wide, wide, thin, thin,
         v((4, 128, COLS), BF16), v((4, 128, COLS), BF16), v((4, 128, 128)), v((4, 384, 128)),
-        v((512, 896), BF16), thin, thin,
+        v((512, 1024), BF16), thin, thin,
         v((512, D)), v((3, 128, D), BF16), v((3, 128, D), BF16),
         *stream(384), *stream(256), *stream(256),
         v((4, 8, 128)), v((4, 8, 128)), v((2, 8, 128)), v((4, 8, 128)),

time: 69.7 us -> 67.5 us (0.968)
  Pallas kernels: 68.9 us -> 66.7 us
    pallas_call x1, Pallas kernels: 67.1 us -> 64.8 us  [body(): pl.pallas_call(kernel, out_shape=(jax.ShapeDtypeStruct((128, D), BF16), j...]
where the time goes in v6:
time: 67.5 us; the launch traced here: 67.3 us
  Pallas kernels  66.7 us (99%)
    pallas_call x1, Pallas kernels, body(): pl.pallas_call(kernel, out_shape=(jax.ShapeDtypeStruct((128, D), BF16), j...  64.8 us
    pallas_call x1, Pallas kernels, body(): pl.pallas_call(emit, out_shape=(jax.ShapeDtypeStruct((128, D), BF16), jax...  1.88 us

profile of v6, /device:TPU:1, one launch (start us, length us, event | category | flops | bytes accessed | tf_op | source)
XLA Modules:
  0.0 67.3 jit_solution(7112882716183900031)
XLA Ops:
  0.6 64.8 %shard_map.85 = (bf16[128,1280]{1,0:T(8,128)(2,1)}, f32[10,2856]{1,0:T(8,128)}, f32[8,128]{1,0:T(8,128)}) custom-call(bf16[128,1280]{1,0:T(8,128)(2,1)} %bitcast.7, bf16[128,2560]{1,0:T(8,128)(2,1)} %bitcast.6, bf16[160,2856]{1,0:T(8,128)(2,1)} %w_ref.1, f32[1,40]{1,0:T(1,128)} %bitcast.8, f32[1,40]{1,0:T(1,128)} %bitcast.9, f32[1,40]{1,0:T(1,128)} %bitcast.10), custom_call_target="tpu_custom_call" | custom-call | tf_op jit(solution)/shard_map/pallas_call | solution.py:657
  65.4 1.9 %shard_map.86 = (bf16[128,1280]{1,0:T(8,128)(2,1)}, f32[10,2856]{1,0:T(8,128)}, f32[3,40]{1,0:T(4,128)}) custom-call(bf16[128,1280]{1,0:T(8,128)(2,1)} %get-tuple-element.9.hg_ref, f32[10,2856]{1,0:T(8,128)} %get-tuple-element.10.wg_ref, f32[8,128]{1,0:T(8,128)} %get-tuple-element.11.hd_ref), custom_call_target="tpu_custom_call" | custom-call | tf_op jit(solution)/shard_map/pallas_call | solution.py:669

commit v7 on v6

--- a/solution.py
+++ b/solution.py
@@ -381,10 +381,9 @@
     pair_inside(1)
 
     def turn(b, rows):
-        dcf[rows, :] = mm(dgs[b], bmf[rows, :], NN, highest)
-        dbf[rows, :] = mm(dgs[b], cmf[rows, :], TN, highest)
-
-    blocks(turn)
+        dcf[rows, :] = mm(dgs[b], bmf[rows, :], NN, highest) + mm(oe[rows, :], sb[b], NT)
+        dbf[rows, :] = mm(dgs[b], cmf[rows, :], TN, highest) + mm(xt[rows, :], db[b], NT)
+
     got(29, ttr)
 
     lanes = lax.broadcasted_iota(jnp.int32, (256, 128), 0)
@@ -433,8 +432,8 @@
         blocks(outside)
 
     class Stream:
-        def __init__(self, base, group, lo, hi, kind, bufs):
-            self.base, self.group, self.lo, self.hi, self.left = base, group, lo, hi, hidx if kind else hidt
+        def __init__(self, base, group, parts, kind, bufs):
+            self.base, self.group, self.parts, self.left = base, group, parts, hidx if kind else hidt
             self.dw, self.s1, self.r1, self.s2, self.r2, self.s3, self.r3, self.s4, self.r4, self.sd, self.rd = bufs
             self.index, self.dev, self.index2, self.dev2 = (y, ydev, x, xdev) if kind == 0 else (x, xdev, y, ydev)
 
@@ -444,8 +443,8 @@
         def first(self):
             for i in (2, 1, 3, 0):
                 rows = ds(lax.rem(self.index + i, 4) * 320, 320)
-                cols = slice(self.lo, self.hi) if self.hi else ds(640 + 128 * c, 256, 128)
-                self.dw[rows, :] = mm(self.left[rows, :], rr[:, cols])
+                for cols, target in self.parts:
+                    self.dw[rows, target] = mm(self.left[rows, :], rr[:, cols])
                 if i == 2:
                     self.s1[...] = self.dw[rows, :].astype(BF16)
                     self.one = (
@@ -497,9 +496,9 @@
         def close(self):
             sent(self.group, self.dw.at[0:688, :])
 
-    alpha = Stream(46, 13, 256, 640, 0, (dwa, sa1, ra1, sa2, ra2, sa3, ra3, sa4, ra4, sda, rda))
-    beta = Stream(52, 14, 0, 256, 1, (dwb, sb1, rb1, sb2, rb2, sb3, rb3, sb4, rb4, sdb, rdb))
-    gamma = Stream(58, 15, 640, None, 1, (dwc, sc1, rc1, sc2, rc2, sc3, rc3, sc4, rc4, sdc, rdc))
+    alpha = Stream(46, 13, [(slice(256, 640), slice(0, 384))], 0, (dwa, sa1, ra1, sa2, ra2, sa3, ra3, sa4, ra4, sda, rda))
+    beta = Stream(52, 14, [(slice(0, 256), slice(0, 256)), (slice(768, 896), slice(256, 384))], 1, (dwb, sb1, rb1, sb2, rb2, sb3, rb3, sb4, rb4, sdb, rdb))
+    gamma = Stream(58, 15, [(ds(lane0, 128), slice(0, 128))], 0, (dwc, sc1, rc1, sc2, rc2, sc3, rc3, sc4, rc4, sdc, rdc))
 
     pair_outside(2)
     pair_outside(3)
@@ -508,12 +507,15 @@
     pair_outside(0)
     pair_outside(1)
 
+    blocks(turn)
+    first = c == 0
+    t1s[...] = jnp.where(first, dcf[...], dbf[...])
+    t1 = send(35, t1s, t1r, core, 9)
+
     ownl = coli < 10
     bias_sum = decay_sum = jnp.zeros((8, 128), F32)
     for b in range(4):
         rows = slice(128 * b, 128 * b + 128)
-        dcf[rows, :] = dcf[rows, :] + mm(oe[rows, :], sb[b], NT)
-        dbf[rows, :] = dbf[rows, :] + mm(xt[rows, :], db[b], NT)
         dlog = mm(upper, red[b, 0:128], NN, highest) + mm(strict, red[b, 128:256], NN, highest)
         dlog = jnp.where(ownl, dlog + inner[b].sum(axis=0, keepdims=True), 0.0)
         ddt = (red[b, 256:384] + neg * dlog) * jax.nn.sigmoid(projs[rows, 128:256] + bias)
@@ -521,10 +523,7 @@
         rr[rows, 768:896] = ddt.astype(BF16)
         bias_sum = bias_sum + ddt.reshape(16, 8, 128).sum(axis=0)
         decay_sum = decay_sum + (dlog * lgd[rows, :]).reshape(16, 8, 128).sum(axis=0)
-    first = c == 0
     place = jnp.where(jnp.logical_and(rowi < 10, coli == rowi + 10 * g), 1.0, 0.0).astype(F32)
-    t1s[...] = jnp.where(first, dcf[...], dbf[...])
-    t1 = send(35, t1s, t1r, core, 9)
     beta.first()
     row8 = lax.broadcasted_iota(jnp.int32, (8, 128), 0)
     packed = jnp.where(
@@ -555,22 +554,22 @@
     hg_far.wait_recv()
     hgs[2] = (hgp[far_row, :] + hgr[1].astype(F32)).astype(BF16)
     hg_z = send(44, hgs.at[2], hgr.at[2], rank(2)[2], 11)
+    alpha.third()
     gamma.second()
-    alpha.third()
     beta.third()
     got(38, heads_y.at[0:3])
     heads_x[x] = (heads_y[0] + heads_y[1]) + (heads_y[2] + heads_y[3])
     for k in (1, 2, 3):
         send(39, heads_x.at[x], heads_x.at[x], xdev(k), 10)
     gamma.third()
-    beta.fourth()
+    alpha.fourth()
     got(39, heads_x.at[0:3])
     heads_z[zh] = (heads_x[0] + heads_x[1]) + (heads_x[2] + heads_x[3])
     head_z = send(40, heads_z.at[zh], heads_z.at[zh], zpair, 10)
-    alpha.fourth()
     gamma.fourth()
-    beta.owners()
+    beta.fourth()
     alpha.owners()
+    gamma.owners()
     hg_near.wait_recv()
     hg_z.wait_recv()
     hgo[...] = (hgp[here_id, :] + hgr[0].astype(F32) + hgr[2].astype(F32)).astype(BF16)
@@ -580,10 +579,7 @@
     heads_g[r] = heads_z[0] + heads_z[1]
     for k in (1, 2, 3):
         send(41, heads_g.at[r], heads_g.at[r], rank(k)[2], 10)
-    gamma.owners()
-    beta.finish()
-    for k in range(4):
-        wgo[:, 640 * k : 640 * k + 256] = rdb[k, 0:10, :]
+    beta.owners()
     alpha.finish()
     for k in range(4):
         wgo[:, 640 * k + 256 : 640 * k + 640] = rda[k, 0:10, :]
@@ -592,11 +588,12 @@
     hd_out = pltpu.make_async_copy(hdo, hd_ref, ls.at[6])
     hd_out.start()
     gamma.finish()
-    wgo[:, 2560:2688] = rdc[0, 0:10, 0:128] + rdc[2, 0:10, 0:128]
-    wgo[:, 2688:2816] = rdc[1, 0:10, 128:256] + rdc[3, 0:10, 128:256]
+    wgo[:, 2560:2688] = rdc[0, 0:10, :] + rdc[2, 0:10, :]
+    wgo[:, 2688:2816] = rdc[1, 0:10, :] + rdc[3, 0:10, :]
+    beta.finish()
     for k in range(4):
-        lane = 128 - 128 * (k % 2)
-        wgo[:, 2816 + 10 * k : 2826 + 10 * k] = rdc[k, 0:10, lane : lane + 10]
+        wgo[:, 640 * k : 640 * k + 256] = rdb[k, 0:10, 0:256]
+        wgo[:, 2816 + 10 * k : 2826 + 10 * k] = rdb[k, 0:10, 256:266]
     wg_out = pltpu.make_async_copy(wgo, wg_ref, ls.at[7])
     wg_out.start()
     for m in range(4):
@@ -638,7 +635,7 @@
         v((4, 128, COLS), BF16), v((4, 128, COLS), BF16), v((4, 128, 128)), v((4, 384, 128)),
         v((512, 1024), BF16), thin, thin,
         v((512, D)), v((3, 128, D), BF16), v((3, 128, D), BF16),
-        *stream(384), *stream(256), *stream(256),
+        *stream(384), *stream(384), *stream(128),
         v((4, 8, 128)), v((4, 8, 128)), v((2, 8, 128)), v((4, 8, 128)),
         v((128, D), BF16), v((10, 2856)), v((8, 128)),
         pltpu.SemaphoreType.DMA((16,)), pltpu.SemaphoreType.DMA((64,)), pltpu.SemaphoreType.DMA((8,)),

time: 67.5 us -> 66.8 us (0.990)
  Pallas kernels: 66.7 us -> 66 us
    pallas_call x1, Pallas kernels: 64.8 us -> 64.1 us  [body(): pl.pallas_call(kernel, out_shape=(jax.ShapeDtypeStruct((128, D), BF16), j...]
where the time goes in v7:
time: 66.8 us; the launch traced here: 66.6 us
  Pallas kernels  66 us (99%)
    pallas_call x1, Pallas kernels, body(): pl.pallas_call(kernel, out_shape=(jax.ShapeDtypeStruct((128, D), BF16), j...  64.1 us
    pallas_call x1, Pallas kernels, body(): pl.pallas_call(emit, out_shape=(jax.ShapeDtypeStruct((128, D), BF16), jax...  1.88 us

profile of v7, /device:TPU:1, one launch (start us, length us, event | category | flops | bytes accessed | tf_op | source)
XLA Modules:
  0.0 66.6 jit_solution(11487887655246012912)
XLA Ops:
  0.6 64.1 %shard_map.85 = (bf16[128,1280]{1,0:T(8,128)(2,1)}, f32[10,2856]{1,0:T(8,128)}, f32[8,128]{1,0:T(8,128)}) custom-call(bf16[128,1280]{1,0:T(8,128)(2,1)} %bitcast.7, bf16[128,2560]{1,0:T(8,128)(2,1)} %bitcast.6, bf16[160,2856]{1,0:T(8,128)(2,1)} %w_ref.1, f32[1,40]{1,0:T(1,128)} %bitcast.8, f32[1,40]{1,0:T(1,128)} %bitcast.9, f32[1,40]{1,0:T(1,128)} %bitcast.10), custom_call_target="tpu_custom_call" | custom-call | tf_op jit(solution)/shard_map/pallas_call | solution.py:654
  64.7 1.9 %shard_map.86 = (bf16[128,1280]{1,0:T(8,128)(2,1)}, f32[10,2856]{1,0:T(8,128)}, f32[3,40]{1,0:T(4,128)}) custom-call(bf16[128,1280]{1,0:T(8,128)(2,1)} %get-tuple-element.9.hg_ref, f32[10,2856]{1,0:T(8,128)} %get-tuple-element.10.wg_ref, f32[8,128]{1,0:T(8,128)} %get-tuple-element.11.hd_ref), custom_call_target="tpu_custom_call" | custom-call | tf_op jit(solution)/shard_map/pallas_call | solution.py:666

commit v8 on v7

--- a/solution.py
+++ b/solution.py
@@ -29,6 +29,20 @@
     return lax.dot_general(a, b, dims, preferred_element_type=F32, precision=precision)
 
 
+def parts(v, count):
+    out = []
+    for _ in range(count):
+        out.append(v.astype(BF16))
+        v = v - out[-1].astype(F32)
+    return out
+
+
+def mm3(a, b, dims=NN):
+    (ah, al), (bh, bl) = parts(a, 2), parts(b, 2)
+    (ka,), (kb,) = dims[0]
+    return mm(jnp.concatenate([ah, al, ah], axis=ka), jnp.concatenate([bh, bh, bl], axis=kb), dims)
+
+
 def ds(start, size, align=None):
     return pl.ds(pl.multiple_of(start, align or size), size)
 
@@ -48,6 +62,7 @@
     dwa, sa1, ra1, sa2, ra2, sa3, ra3, sa4, ra4, sda, rda,
     dwb, sb1, rb1, sb2, rb2, sb3, rb3, sb4, rb4, sdb, rdb,
     dwc, sc1, rc1, sc2, rc2, sc3, rc3, sc4, rc4, sdc, rdc,
+    dwd, sd1, rd1, sd2, rd2, sd3, rd3, sd4, rd4, sdd, rdd,
     heads_y, heads_x, heads_z, heads_g, hgo, wgo, hdo,
     ss, rs, ls,
 ):
@@ -223,9 +238,11 @@
     low = coli < 64
     causal = rowi >= coli
     anti = rowi <= coli
-    tri = causal.astype(F32)
-    upper = anti.astype(F32)
-    strict = (rowi > coli).astype(F32)
+    tri = causal.astype(F32).astype(BF16)
+    tri3 = jnp.concatenate([tri] * 3, axis=1)
+    upper = anti.astype(F32).astype(BF16)
+    strict = (rowi > coli).astype(F32).astype(BF16)
+    sums4 = jnp.concatenate([upper] * 3 + [strict] * 3, axis=1)
 
     def pair(v, j):
         return jnp.where(low[0 : v.shape[0]], v[:, 2 * j : 2 * j + 1], v[:, 2 * j + 1 : 2 * j + 2])
@@ -246,7 +263,7 @@
         pre = projs[rows, 128:256] + bias
         step = jnp.maximum(pre, 0.0) + jnp.log1p(jnp.exp(-jnp.abs(pre)))
         lg = neg * step
-        cum = mm(tri, lg, NN, highest)
+        cum = mm(tri3, jnp.concatenate(parts(lg, 3), axis=0))
         stp[rows, :] = step
         lgd[rows, :] = lg
         cums[rows, :] = cum
@@ -260,7 +277,7 @@
         cm = jax.nn.silu(projs[rows, 256:384])
         bmf[rows, :] = bm
         cmf[rows, :] = cm
-        scores = mm(cm, bm, NT, highest)
+        scores = mm3(cm, bm, NT)
         gs[b] = scores
         gts[b] = scores.T
 
@@ -381,8 +398,8 @@
     pair_inside(1)
 
     def turn(b, rows):
-        dcf[rows, :] = mm(dgs[b], bmf[rows, :], NN, highest) + mm(oe[rows, :], sb[b], NT)
-        dbf[rows, :] = mm(dgs[b], cmf[rows, :], TN, highest) + mm(xt[rows, :], db[b], NT)
+        dcf[rows, :] = mm3(dgs[b], bmf[rows, :], NN) + mm(oe[rows, :], sb[b], NT)
+        dbf[rows, :] = mm3(dgs[b], cmf[rows, :], TN) + mm(xt[rows, :], db[b], NT)
 
     got(29, ttr)
 
@@ -440,17 +457,23 @@
         def send(self, i, src, dst, dev):
             return send(self.base + i, src, dst, dev, self.group)
 
+        def block(self, i):
+            rows = ds(lax.rem(self.index + i, 4) * 320, 320)
+            for cols, target in self.parts:
+                self.dw[rows, target] = mm(self.left[rows, :], rr[:, cols])
+            return rows
+
         def first(self):
-            for i in (2, 1, 3, 0):
-                rows = ds(lax.rem(self.index + i, 4) * 320, 320)
-                for cols, target in self.parts:
-                    self.dw[rows, target] = mm(self.left[rows, :], rr[:, cols])
-                if i == 2:
-                    self.s1[...] = self.dw[rows, :].astype(BF16)
-                    self.one = (
-                        self.send(0, self.s1.at[0:160, :], self.r1.at[0], self.dev(1)),
-                        self.send(1, self.s1.at[160:320, :], self.r1.at[1], self.dev(-1)),
-                    )
+            rows = self.block(2)
+            self.s1[...] = self.dw[rows, :].astype(BF16)
+            self.one = (
+                self.send(0, self.s1.at[0:160, :], self.r1.at[0], self.dev(1)),
+                self.send(1, self.s1.at[160:320, :], self.r1.at[1], self.dev(-1)),
+            )
+
+        def rest(self):
+            for i in (1, 3, 0):
+                self.block(i)
 
         def second(self):
             nxt = lax.rem(self.index + 1, 4) * 320
@@ -497,8 +520,9 @@
             sent(self.group, self.dw.at[0:688, :])
 
     alpha = Stream(46, 13, [(slice(256, 640), slice(0, 384))], 0, (dwa, sa1, ra1, sa2, ra2, sa3, ra3, sa4, ra4, sda, rda))
-    beta = Stream(52, 14, [(slice(0, 256), slice(0, 256)), (slice(768, 896), slice(256, 384))], 1, (dwb, sb1, rb1, sb2, rb2, sb3, rb3, sb4, rb4, sdb, rdb))
+    beta = Stream(52, 14, [(slice(0, 256), slice(0, 256))], 1, (dwb, sb1, rb1, sb2, rb2, sb3, rb3, sb4, rb4, sdb, rdb))
     gamma = Stream(58, 15, [(ds(lane0, 128), slice(0, 128))], 0, (dwc, sc1, rc1, sc2, rc2, sc3, rc3, sc4, rc4, sdc, rdc))
+    delta = Stream(64, 16, [(slice(768, 896), slice(0, 128))], 1, (dwd, sd1, rd1, sd2, rd2, sd3, rd3, sd4, rd4, sdd, rdd))
 
     pair_outside(2)
     pair_outside(3)
@@ -506,17 +530,20 @@
     alpha.first()
     pair_outside(0)
     pair_outside(1)
+    beta.first()
 
     blocks(turn)
     first = c == 0
     t1s[...] = jnp.where(first, dcf[...], dbf[...])
     t1 = send(35, t1s, t1r, core, 9)
+    alpha.rest()
+    alpha.second()
 
     ownl = coli < 10
     bias_sum = decay_sum = jnp.zeros((8, 128), F32)
     for b in range(4):
         rows = slice(128 * b, 128 * b + 128)
-        dlog = mm(upper, red[b, 0:128], NN, highest) + mm(strict, red[b, 128:256], NN, highest)
+        dlog = mm(sums4, jnp.concatenate(parts(red[b, 0:128], 3) + parts(red[b, 128:256], 3), axis=0))
         dlog = jnp.where(ownl, dlog + inner[b].sum(axis=0, keepdims=True), 0.0)
         ddt = (red[b, 256:384] + neg * dlog) * jax.nn.sigmoid(projs[rows, 128:256] + bias)
         ddt = jnp.where(ownl, ddt, 0.0)
@@ -524,7 +551,7 @@
         bias_sum = bias_sum + ddt.reshape(16, 8, 128).sum(axis=0)
         decay_sum = decay_sum + (dlog * lgd[rows, :]).reshape(16, 8, 128).sum(axis=0)
     place = jnp.where(jnp.logical_and(rowi < 10, coli == rowi + 10 * g), 1.0, 0.0).astype(F32)
-    beta.first()
+    delta.first()
     row8 = lax.broadcasted_iota(jnp.int32, (8, 128), 0)
     packed = jnp.where(
         row8 == 0, bias_sum.sum(axis=0, keepdims=True),
@@ -534,12 +561,15 @@
     heads_y[y] = mm(packed, place, NN, highest)
     for k in (1, 2, 3):
         send(38, heads_y.at[y], heads_y.at[y], ydev(k), 10)
-    alpha.second()
     t1.wait_recv()
     mixed = jnp.where(first, dbf[...], dcf[...]) + t1r[...]
     rr[:, ds(lane0, 128)] = (mixed * silu_grad(projs[:, ds(256 * c, 128, 128)])).astype(BF16)
     rr[:, ds(896 - 256 * c, 128)] = jnp.zeros((512, 128), BF16)
     gamma.first()
+    beta.rest()
+    beta.second()
+    delta.rest()
+    gamma.rest()
     for n in range(5):
         part = slice(256 * n, 256 * n + 256)
         hgp[:, part] = mm(rr[...], wf[part, :], NT)
@@ -550,26 +580,29 @@
     hg_far = send(43, hgs.at[1], hgr.at[1], core, 11)
     hgs[0] = hgp[mate_row, :].astype(BF16)
     hg_near = send(42, hgs.at[0], hgr.at[0], core, 11)
-    beta.second()
+    delta.second()
     hg_far.wait_recv()
     hgs[2] = (hgp[far_row, :] + hgr[1].astype(F32)).astype(BF16)
     hg_z = send(44, hgs.at[2], hgr.at[2], rank(2)[2], 11)
     alpha.third()
+    beta.third()
     gamma.second()
-    beta.third()
+    delta.third()
     got(38, heads_y.at[0:3])
     heads_x[x] = (heads_y[0] + heads_y[1]) + (heads_y[2] + heads_y[3])
     for k in (1, 2, 3):
         send(39, heads_x.at[x], heads_x.at[x], xdev(k), 10)
+    beta.fourth()
+    alpha.fourth()
     gamma.third()
-    alpha.fourth()
     got(39, heads_x.at[0:3])
     heads_z[zh] = (heads_x[0] + heads_x[1]) + (heads_x[2] + heads_x[3])
     head_z = send(40, heads_z.at[zh], heads_z.at[zh], zpair, 10)
+    delta.fourth()
+    beta.owners()
+    alpha.owners()
     gamma.fourth()
-    beta.fourth()
-    alpha.owners()
-    gamma.owners()
+    delta.owners()
     hg_near.wait_recv()
     hg_z.wait_recv()
     hgo[...] = (hgp[here_id, :] + hgr[0].astype(F32) + hgr[2].astype(F32)).astype(BF16)
@@ -579,7 +612,10 @@
     heads_g[r] = heads_z[0] + heads_z[1]
     for k in (1, 2, 3):
         send(41, heads_g.at[r], heads_g.at[r], rank(k)[2], 10)
-    beta.owners()
+    beta.finish()
+    for k in range(4):
+        wgo[:, 640 * k : 640 * k + 256] = rdb[k, 0:10, :]
+    gamma.owners()
     alpha.finish()
     for k in range(4):
         wgo[:, 640 * k + 256 : 640 * k + 640] = rda[k, 0:10, :]
@@ -587,13 +623,12 @@
     hdo[...] = (heads_g[0] + heads_g[1]) + (heads_g[2] + heads_g[3])
     hd_out = pltpu.make_async_copy(hdo, hd_ref, ls.at[6])
     hd_out.start()
+    delta.finish()
+    for k in range(4):
+        wgo[:, 2816 + 10 * k : 2826 + 10 * k] = rdd[k, 0:10, 0:10]
     gamma.finish()
     wgo[:, 2560:2688] = rdc[0, 0:10, :] + rdc[2, 0:10, :]
     wgo[:, 2688:2816] = rdc[1, 0:10, :] + rdc[3, 0:10, :]
-    beta.finish()
-    for k in range(4):
-        wgo[:, 640 * k : 640 * k + 256] = rdb[k, 0:10, 0:256]
-        wgo[:, 2816 + 10 * k : 2826 + 10 * k] = rdb[k, 0:10, 256:266]
     wg_out = pltpu.make_async_copy(wgo, wg_ref, ls.at[7])
     wg_out.start()
     for m in range(4):
@@ -606,7 +641,7 @@
     sent(9, t1r)
     sent(10, bmf.at[0:80, :])
     sent(11, hgs)
-    for stream in (alpha, beta, gamma):
+    for stream in (alpha, beta, gamma, delta):
         stream.close()
     hg_out.wait()
     hd_out.wait()
@@ -635,10 +670,10 @@
         v((4, 128, COLS), BF16), v((4, 128, COLS), BF16), v((4, 128, 128)), v((4, 384, 128)),
         v((512, 1024), BF16), thin, thin,
         v((512, D)), v((3, 128, D), BF16), v((3, 128, D), BF16),
-        *stream(384), *stream(384), *stream(128),
+        *stream(384), *stream(256), *stream(128), *stream(128),
         v((4, 8, 128)), v((4, 8, 128)), v((2, 8, 128)), v((4, 8, 128)),
         v((128, D), BF16), v((10, 2856)), v((8, 128)),
-        pltpu.SemaphoreType.DMA((16,)), pltpu.SemaphoreType.DMA((64,)), pltpu.SemaphoreType.DMA((8,)),
+        pltpu.SemaphoreType.DMA((17,)), pltpu.SemaphoreType.DMA((70,)), pltpu.SemaphoreType.DMA((8,)),
     ]
 
 

time: 66.8 us -> 65.6 us (0.982)
  Pallas kernels: 66 us -> 64.8 us
    pallas_call x1, Pallas kernels: 64.1 us -> 63 us  [body(): pl.pallas_call(kernel, out_shape=(jax.ShapeDtypeStruct((128, D), BF16), j...]
where the time goes in v8:
time: 65.6 us; the launch traced here: 65.5 us
  Pallas kernels  64.8 us (99%)
    pallas_call x1, Pallas kernels, body(): pl.pallas_call(kernel, out_shape=(jax.ShapeDtypeStruct((128, D), BF16), j...  63 us
    pallas_call x1, Pallas kernels, body(): pl.pallas_call(emit, out_shape=(jax.ShapeDtypeStruct((128, D), BF16), jax...  1.88 us

profile of v8, /device:TPU:1, one launch (start us, length us, event | category | flops | bytes accessed | tf_op | source)
XLA Modules:
  0.0 65.5 jit_solution(17953449174740853105)
XLA Ops:
  0.6 63.0 %shard_map.85 = (bf16[128,1280]{1,0:T(8,128)(2,1)}, f32[10,2856]{1,0:T(8,128)}, f32[8,128]{1,0:T(8,128)}) custom-call(bf16[128,1280]{1,0:T(8,128)(2,1)} %bitcast.7, bf16[128,2560]{1,0:T(8,128)(2,1)} %bitcast.6, bf16[160,2856]{1,0:T(8,128)(2,1)} %w_ref.1, f32[1,40]{1,0:T(1,128)} %bitcast.8, f32[1,40]{1,0:T(1,128)} %bitcast.9, f32[1,40]{1,0:T(1,128)} %bitcast.10), custom_call_target="tpu_custom_call" | custom-call | tf_op jit(solution)/shard_map/pallas_call | solution.py:689
  63.6 1.9 %shard_map.86 = (bf16[128,1280]{1,0:T(8,128)(2,1)}, f32[10,2856]{1,0:T(8,128)}, f32[3,40]{1,0:T(4,128)}) custom-call(bf16[128,1280]{1,0:T(8,128)(2,1)} %get-tuple-element.9.hg_ref, f32[10,2856]{1,0:T(8,128)} %get-tuple-element.10.wg_ref, f32[8,128]{1,0:T(8,128)} %get-tuple-element.11.hd_ref), custom_call_target="tpu_custom_call" | custom-call | tf_op jit(solution)/shard_map/pallas_call | solution.py:701

commit v9 on v8

--- a/solution.py
+++ b/solution.py
@@ -55,7 +55,7 @@
 def kernel(
     hid_ref, cot_ref, w_ref, bias_ref, decay_ref, skip_ref,
     hg_ref, wg_ref, hd_ref,
-    hidf, hidt, hidx, cot, wraw, wf, projs, projv, bmf, cmf, lgd, cums, cumt, stp, gs, gts, dgs,
+    stepw, stepa, hidf, hidt, hidx, cot, wraw, wf, projs, projv, bmf, cmf, lgd, cums, cumt, stp, gs, gts, dgs,
     sexp, ecs, tls, vv, xb, xt, oe, tot,
     sl, dl, stt, tts, str_, ttr, q1s, dxin, dbf, dcf, sb, db, dd, red,
     rr, t1s, t1r, hgp, hgs, hgr,
@@ -135,10 +135,12 @@
     coli = lax.broadcasted_iota(jnp.int32, (128, 128), 1)
     rowi = lax.broadcasted_iota(jnp.int32, (128, 128), 0)
     local[0].wait()
+    stepa[...] = jnp.zeros_like(stepa)
     tail = jnp.concatenate([wraw[:, 2816:2856].astype(F32), jnp.zeros((160, 88), F32)], axis=1)
     tail = pltpu.roll(tail, lax.rem(128 - 10 * g, 128), 1)
     keep10 = lax.broadcasted_iota(jnp.int32, (160, 128), 1) < 10
-    wf[own, 768:896] = jnp.where(keep10, tail, 0.0).astype(BF16)
+    tail = jnp.concatenate([jnp.where(keep10, tail, 0.0), jnp.zeros((96, 128), F32)], axis=0)
+    stepw[x * 2 + zh] = tail.T[0:16, :].astype(BF16)
 
     def lanes10(ref):
         full = jnp.concatenate([ref[...], jnp.zeros((1, 88), F32)], axis=1)
@@ -152,7 +154,7 @@
     pl.semaphore_wait(barrier, 10)
 
     def cols(m):
-        return (ds(640 + 128 * c, 256, 128), slice(0, 256), slice(256, 512), slice(512, 640))[m]
+        return (ds(lane0, 128), slice(0, 256), slice(256, 512), slice(512, 640))[m]
 
     w = {}
 
@@ -198,10 +200,16 @@
     def w_done(m):
         got(6 * m + 5, wf.at[0 : 320 if m < 2 else 640, cols(m)])
 
+    def step_send(i, xk, zk, dev):
+        ref = stepw.at[lax.rem(x + xk + 4, 4) * 2 + zk]
+        return send(i, ref, ref, dev, 17)
+
     def hand(k):
         ref = wf.at[ds(lax.rem(x + k + 4, 4) * 320, 320), ds(lane0, 128)]
         send(28, ref, ref, core, 6)
 
+    step_z = step_send(70, 0, zh, zpair)
+    step_x = [step_send(71, 0, zh, xdev(1)), step_send(72, 0, zh, xdev(-1))]
     w_own_z(0)
     w_own_x(0)
     h_z = send(24, hid_ref, hidf.at[here_id, :], rank(2)[2], 4)
@@ -214,11 +222,19 @@
         send(27, cot_ref.at[:, ds(gk * COLS, COLS, 128)], cot.at[here_id, :], dev, 5)
     w_own_z(2)
     w_own_z(3)
+    step_z.wait_recv()
+    step_o = [step_send(73, 0, 1 - zh, xdev(1)), step_send(74, 0, 1 - zh, xdev(-1))]
     w_other(0)
+    for copy in step_x:
+        copy.wait_recv()
+    step_send(75, -1, zh, xdev(1))
     w_forward(0)
     w_forward(2)
     w_across(2)
     w_own_x(3)
+    for copy in step_o:
+        copy.wait_recv()
+    step_send(75, -1, 1 - zh, xdev(1))
     w_forward_other(0)
     w_own_x(1)
     for k in (-1, 0, 1):
@@ -232,6 +248,10 @@
     w_other(1)
     w_done(0)
     hand(2)
+    got(75, stepw.at[0:2])
+    for k in range(8):
+        stepa[0:16, 160 * k : 160 * k + 160] = stepw[k][:, 0:160].astype(F32)
+    wf[:, 768:896] = stepa[...].T.astype(BF16)
     h_c.wait_recv()
     h_f.wait_recv()
 
@@ -585,23 +605,24 @@
     hgs[2] = (hgp[far_row, :] + hgr[1].astype(F32)).astype(BF16)
     hg_z = send(44, hgs.at[2], hgr.at[2], rank(2)[2], 11)
     alpha.third()
+    gamma.second()
     beta.third()
-    gamma.second()
     delta.third()
     got(38, heads_y.at[0:3])
     heads_x[x] = (heads_y[0] + heads_y[1]) + (heads_y[2] + heads_y[3])
     for k in (1, 2, 3):
         send(39, heads_x.at[x], heads_x.at[x], xdev(k), 10)
+    gamma.third()
+    alpha.fourth()
     beta.fourth()
-    alpha.fourth()
-    gamma.third()
     got(39, heads_x.at[0:3])
     heads_z[zh] = (heads_x[0] + heads_x[1]) + (heads_x[2] + heads_x[3])
     head_z = send(40, heads_z.at[zh], heads_z.at[zh], zpair, 10)
+    gamma.fourth()
     delta.fourth()
+    alpha.owners()
     beta.owners()
-    alpha.owners()
-    gamma.fourth()
+    gamma.owners()
     delta.owners()
     hg_near.wait_recv()
     hg_z.wait_recv()
@@ -615,7 +636,6 @@
     beta.finish()
     for k in range(4):
         wgo[:, 640 * k : 640 * k + 256] = rdb[k, 0:10, :]
-    gamma.owners()
     alpha.finish()
     for k in range(4):
         wgo[:, 640 * k + 256 : 640 * k + 640] = rda[k, 0:10, :]
@@ -634,6 +654,7 @@
     for m in range(4):
         sent(m, wf.at[0:1120, cols(m)])
     sent(4, hidf.at[0:384, :])
+    sent(17, stepw.at[0:7])
     sent(5, cot.at[0:384, :])
     sent(6, wf.at[:, ds(lane0, 128)])
     sent(7, ttr)
@@ -661,6 +682,7 @@
     wide, wide16 = v((512, COLS)), v((512, COLS), BF16)
     thin = v((512, 128))
     return [
+        v((8, 16, 256), BF16), v((128, D)),
         v((512, D), BF16), v((D, 512), BF16), v((D, 512), BF16), wide16, v((160, 2856), BF16), v((D, 1024), BF16),
         v((512, 384)), wide, thin, thin, thin, thin, v((4, 16, 128)), thin,
         v((4, 128, 128)), v((4, 128, 128)), v((4, 128, 128)),
@@ -673,7 +695,7 @@
         *stream(384), *stream(256), *stream(128), *stream(128),
         v((4, 8, 128)), v((4, 8, 128)), v((2, 8, 128)), v((4, 8, 128)),
         v((128, D), BF16), v((10, 2856)), v((8, 128)),
-        pltpu.SemaphoreType.DMA((17,)), pltpu.SemaphoreType.DMA((70,)), pltpu.SemaphoreType.DMA((8,)),
+        pltpu.SemaphoreType.DMA((18,)), pltpu.SemaphoreType.DMA((76,)), pltpu.SemaphoreType.DMA((8,)),
     ]
 
 

time: 65.6 us -> 66 us (level)
  no operation moved by 1% of the time
where the time goes in v9:
time: 66 us; the launch traced here: 65.8 us
  Pallas kernels  65.2 us (99%)
    pallas_call x1, Pallas kernels, body(): pl.pallas_call(kernel, out_shape=(jax.ShapeDtypeStruct((128, D), BF16), j...  63.3 us
    pallas_call x1, Pallas kernels, body(): pl.pallas_call(emit, out_shape=(jax.ShapeDtypeStruct((128, D), BF16), jax...  1.88 us

profile of v9, /device:TPU:1, one launch (start us, length us, event | category | flops | bytes accessed | tf_op | source)
XLA Modules:
  0.0 65.8 jit_solution(17600315052199970020)
XLA Ops:
  0.6 63.3 %shard_map.85 = (bf16[128,1280]{1,0:T(8,128)(2,1)}, f32[10,2856]{1,0:T(8,128)}, f32[8,128]{1,0:T(8,128)}) custom-call(bf16[128,1280]{1,0:T(8,128)(2,1)} %bitcast.7, bf16[128,2560]{1,0:T(8,128)(2,1)} %bitcast.6, bf16[160,2856]{1,0:T(8,128)(2,1)} %w_ref.1, f32[1,40]{1,0:T(1,128)} %bitcast.8, f32[1,40]{1,0:T(1,128)} %bitcast.9, f32[1,40]{1,0:T(1,128)} %bitcast.10), custom_call_target="tpu_custom_call" | custom-call | tf_op jit(solution)/shard_map/pallas_call | solution.py:711
  63.9 1.9 %shard_map.86 = (bf16[128,1280]{1,0:T(8,128)(2,1)}, f32[10,2856]{1,0:T(8,128)}, f32[3,40]{1,0:T(4,128)}) custom-call(bf16[128,1280]{1,0:T(8,128)(2,1)} %get-tuple-element.9.hg_ref, f32[10,2856]{1,0:T(8,128)} %get-tuple-element.10.wg_ref, f32[8,128]{1,0:T(8,128)} %get-tuple-element.11.hd_ref), custom_call_target="tpu_custom_call" | custom-call | tf_op jit(solution)/shard_map/pallas_call | solution.py:723

commit v10 on v9

--- a/solution.py
+++ b/solution.py
@@ -59,12 +59,8 @@
     sexp, ecs, tls, vv, xb, xt, oe, tot,
     sl, dl, stt, tts, str_, ttr, q1s, dxin, dbf, dcf, sb, db, dd, red,
     rr, t1s, t1r, hgp, hgs, hgr,
-    dwa, sa1, ra1, sa2, ra2, sa3, ra3, sa4, ra4, sda, rda,
-    dwb, sb1, rb1, sb2, rb2, sb3, rb3, sb4, rb4, sdb, rdb,
-    dwc, sc1, rc1, sc2, rc2, sc3, rc3, sc4, rc4, sdc, rdc,
-    dwd, sd1, rd1, sd2, rd2, sd3, rd3, sd4, rd4, sdd, rdd,
     heads_y, heads_x, heads_z, heads_g, hgo, wgo, hdo,
-    ss, rs, ls,
+    ss, rs, ls, *bufs,
 ):
     y, zl, c = (lax.axis_index(n) for n in SEQ)
     x, zh = (lax.axis_index(n) for n in ZERO)
@@ -202,14 +198,14 @@
 
     def step_send(i, xk, zk, dev):
         ref = stepw.at[lax.rem(x + xk + 4, 4) * 2 + zk]
-        return send(i, ref, ref, dev, 17)
+        return send(i, ref, ref, dev, 20)
 
     def hand(k):
         ref = wf.at[ds(lax.rem(x + k + 4, 4) * 320, 320), ds(lane0, 128)]
         send(28, ref, ref, core, 6)
 
-    step_z = step_send(70, 0, zh, zpair)
-    step_x = [step_send(71, 0, zh, xdev(1)), step_send(72, 0, zh, xdev(-1))]
+    step_z = step_send(88, 0, zh, zpair)
+    step_x = [step_send(89, 0, zh, xdev(1)), step_send(90, 0, zh, xdev(-1))]
     w_own_z(0)
     w_own_x(0)
     h_z = send(24, hid_ref, hidf.at[here_id, :], rank(2)[2], 4)
@@ -223,18 +219,18 @@
     w_own_z(2)
     w_own_z(3)
     step_z.wait_recv()
-    step_o = [step_send(73, 0, 1 - zh, xdev(1)), step_send(74, 0, 1 - zh, xdev(-1))]
+    step_o = [step_send(91, 0, 1 - zh, xdev(1)), step_send(92, 0, 1 - zh, xdev(-1))]
     w_other(0)
     for copy in step_x:
         copy.wait_recv()
-    step_send(75, -1, zh, xdev(1))
+    step_send(93, -1, zh, xdev(1))
     w_forward(0)
     w_forward(2)
     w_across(2)
     w_own_x(3)
     for copy in step_o:
         copy.wait_recv()
-    step_send(75, -1, 1 - zh, xdev(1))
+    step_send(93, -1, 1 - zh, xdev(1))
     w_forward_other(0)
     w_own_x(1)
     for k in (-1, 0, 1):
@@ -248,12 +244,10 @@
     w_other(1)
     w_done(0)
     hand(2)
-    got(75, stepw.at[0:2])
+    got(93, stepw.at[0:2])
     for k in range(8):
         stepa[0:16, 160 * k : 160 * k + 160] = stepw[k][:, 0:160].astype(F32)
     wf[:, 768:896] = stepa[...].T.astype(BF16)
-    h_c.wait_recv()
-    h_f.wait_recv()
 
     low = coli < 64
     causal = rowi >= coli
@@ -301,7 +295,12 @@
         gs[b] = scores
         gts[b] = scores.T
 
-    blocks(steps)
+    h_c.wait_recv()
+    for k in range(4):
+        if k == 3:
+            h_f.wait_recv()
+        b = rank(k)[0] * 2 + rank(k)[1]
+        steps(b, ds(b * 128, 128))
     for j in range(5):
         cj = slice(128 * j, 128 * j + 128)
         for b in range(4):
@@ -539,25 +538,33 @@
         def close(self):
             sent(self.group, self.dw.at[0:688, :])
 
-    alpha = Stream(46, 13, [(slice(256, 640), slice(0, 384))], 0, (dwa, sa1, ra1, sa2, ra2, sa3, ra3, sa4, ra4, sda, rda))
-    beta = Stream(52, 14, [(slice(0, 256), slice(0, 256))], 1, (dwb, sb1, rb1, sb2, rb2, sb3, rb3, sb4, rb4, sdb, rdb))
-    gamma = Stream(58, 15, [(ds(lane0, 128), slice(0, 128))], 0, (dwc, sc1, rc1, sc2, rc2, sc3, rc3, sc4, rc4, sdc, rdc))
-    delta = Stream(64, 16, [(slice(768, 896), slice(0, 128))], 1, (dwd, sd1, rd1, sd2, rd2, sd3, rd3, sd4, rd4, sdd, rdd))
+    tiles = [slice(128 * t, 128 * t + 128) for t in range(5)] + [slice(768, 896), ds(lane0, 128)]
+    kinds = (0, 1, 0, 1, 0, 1, 0)
+    p0, p1, p2, p3, p4, st, mp = streams = [
+        Stream(46 + 6 * t, 13 + t, [(tiles[t], slice(0, 128))], kinds[t], bufs[11 * t : 11 * t + 11]) for t in range(7)
+    ]
 
     pair_outside(2)
+    p2.first()
     pair_outside(3)
+    p3.first()
+    p2.rest()
     pair_outside(4)
-    alpha.first()
+    p4.first()
+    p3.rest()
     pair_outside(0)
+    p0.first()
+    p2.second()
     pair_outside(1)
-    beta.first()
+    p1.first()
+    p3.second()
 
     blocks(turn)
     first = c == 0
     t1s[...] = jnp.where(first, dcf[...], dbf[...])
     t1 = send(35, t1s, t1r, core, 9)
-    alpha.rest()
-    alpha.second()
+    p4.rest()
+    p4.second()
 
     ownl = coli < 10
     bias_sum = decay_sum = jnp.zeros((8, 128), F32)
@@ -571,7 +578,7 @@
         bias_sum = bias_sum + ddt.reshape(16, 8, 128).sum(axis=0)
         decay_sum = decay_sum + (dlog * lgd[rows, :]).reshape(16, 8, 128).sum(axis=0)
     place = jnp.where(jnp.logical_and(rowi < 10, coli == rowi + 10 * g), 1.0, 0.0).astype(F32)
-    delta.first()
+    st.first()
     row8 = lax.broadcasted_iota(jnp.int32, (8, 128), 0)
     packed = jnp.where(
         row8 == 0, bias_sum.sum(axis=0, keepdims=True),
@@ -585,14 +592,27 @@
     mixed = jnp.where(first, dbf[...], dcf[...]) + t1r[...]
     rr[:, ds(lane0, 128)] = (mixed * silu_grad(projs[:, ds(256 * c, 128, 128)])).astype(BF16)
     rr[:, ds(896 - 256 * c, 128)] = jnp.zeros((512, 128), BF16)
-    gamma.first()
-    beta.rest()
-    beta.second()
-    delta.rest()
-    gamma.rest()
-    for n in range(5):
-        part = slice(256 * n, 256 * n + 256)
-        hgp[:, part] = mm(rr[...], wf[part, :], NT)
+    mp.first()
+    p0.rest()
+    p0.second()
+    p1.rest()
+    p1.second()
+    p2.third()
+
+    def token(lo, hi):
+        for n in range(lo, hi):
+            part = slice(256 * n, 256 * n + 256)
+            hgp[:, part] = mm(rr[...], wf[part, :], NT)
+
+    st.rest()
+    token(0, 2)
+    p3.third()
+    mp.rest()
+    st.second()
+    token(2, 4)
+    mp.second()
+    p4.third()
+    token(4, 5)
     mate_row = ds((zl * 2 + 1 - c) * 128, 128)
     far_mate = ds(((1 - zl) * 2 + 1 - c) * 128, 128)
     far_row = ds(((1 - zl) * 2 + c) * 128, 128)
@@ -600,30 +620,34 @@
     hg_far = send(43, hgs.at[1], hgr.at[1], core, 11)
     hgs[0] = hgp[mate_row, :].astype(BF16)
     hg_near = send(42, hgs.at[0], hgr.at[0], core, 11)
-    delta.second()
+    p2.fourth()
+    p0.third()
     hg_far.wait_recv()
     hgs[2] = (hgp[far_row, :] + hgr[1].astype(F32)).astype(BF16)
     hg_z = send(44, hgs.at[2], hgr.at[2], rank(2)[2], 11)
-    alpha.third()
-    gamma.second()
-    beta.third()
-    delta.third()
+    p1.third()
+    p3.fourth()
     got(38, heads_y.at[0:3])
     heads_x[x] = (heads_y[0] + heads_y[1]) + (heads_y[2] + heads_y[3])
     for k in (1, 2, 3):
         send(39, heads_x.at[x], heads_x.at[x], xdev(k), 10)
-    gamma.third()
-    alpha.fourth()
-    beta.fourth()
+    st.third()
+    mp.third()
+    p4.fourth()
+    p2.owners()
+    p0.fourth()
     got(39, heads_x.at[0:3])
     heads_z[zh] = (heads_x[0] + heads_x[1]) + (heads_x[2] + heads_x[3])
     head_z = send(40, heads_z.at[zh], heads_z.at[zh], zpair, 10)
-    gamma.fourth()
-    delta.fourth()
-    alpha.owners()
-    beta.owners()
-    gamma.owners()
-    delta.owners()
+    p3.owners()
+    p1.fourth()
+    p4.owners()
+    st.fourth()
+    mp.fourth()
+    p0.owners()
+    p1.owners()
+    st.owners()
+    mp.owners()
     hg_near.wait_recv()
     hg_z.wait_recv()
     hgo[...] = (hgp[here_id, :] + hgr[0].astype(F32) + hgr[2].astype(F32)).astype(BF16)
@@ -633,28 +657,26 @@
     heads_g[r] = heads_z[0] + heads_z[1]
     for k in (1, 2, 3):
         send(41, heads_g.at[r], heads_g.at[r], rank(k)[2], 10)
-    beta.finish()
-    for k in range(4):
-        wgo[:, 640 * k : 640 * k + 256] = rdb[k, 0:10, :]
-    alpha.finish()
-    for k in range(4):
-        wgo[:, 640 * k + 256 : 640 * k + 640] = rda[k, 0:10, :]
     got(41, heads_g.at[0:3])
     hdo[...] = (heads_g[0] + heads_g[1]) + (heads_g[2] + heads_g[3])
     hd_out = pltpu.make_async_copy(hdo, hd_ref, ls.at[6])
     hd_out.start()
-    delta.finish()
+    for t, stream in ((2, p2), (3, p3), (4, p4), (0, p0), (1, p1)):
+        stream.finish()
+        for k in range(4):
+            wgo[:, 640 * k + 128 * t : 640 * k + 128 * t + 128] = stream.rd[k, 0:10, :]
+    st.finish()
     for k in range(4):
-        wgo[:, 2816 + 10 * k : 2826 + 10 * k] = rdd[k, 0:10, 0:10]
-    gamma.finish()
-    wgo[:, 2560:2688] = rdc[0, 0:10, :] + rdc[2, 0:10, :]
-    wgo[:, 2688:2816] = rdc[1, 0:10, :] + rdc[3, 0:10, :]
+        wgo[:, 2816 + 10 * k : 2826 + 10 * k] = st.rd[k, 0:10, 0:10]
+    mp.finish()
+    wgo[:, 2560:2688] = mp.rd[0, 0:10, :] + mp.rd[2, 0:10, :]
+    wgo[:, 2688:2816] = mp.rd[1, 0:10, :] + mp.rd[3, 0:10, :]
     wg_out = pltpu.make_async_copy(wgo, wg_ref, ls.at[7])
     wg_out.start()
     for m in range(4):
         sent(m, wf.at[0:1120, cols(m)])
     sent(4, hidf.at[0:384, :])
-    sent(17, stepw.at[0:7])
+    sent(20, stepw.at[0:7])
     sent(5, cot.at[0:384, :])
     sent(6, wf.at[:, ds(lane0, 128)])
     sent(7, ttr)
@@ -662,7 +684,7 @@
     sent(9, t1r)
     sent(10, bmf.at[0:80, :])
     sent(11, hgs)
-    for stream in (alpha, beta, gamma, delta):
+    for stream in streams:
         stream.close()
     hg_out.wait()
     hd_out.wait()
@@ -692,10 +714,10 @@
         v((4, 128, COLS), BF16), v((4, 128, COLS), BF16), v((4, 128, 128)), v((4, 384, 128)),
         v((512, 1024), BF16), thin, thin,
         v((512, D)), v((3, 128, D), BF16), v((3, 128, D), BF16),
-        *stream(384), *stream(256), *stream(128), *stream(128),
         v((4, 8, 128)), v((4, 8, 128)), v((2, 8, 128)), v((4, 8, 128)),
         v((128, D), BF16), v((10, 2856)), v((8, 128)),
-        pltpu.SemaphoreType.DMA((18,)), pltpu.SemaphoreType.DMA((76,)), pltpu.SemaphoreType.DMA((8,)),
+        pltpu.SemaphoreType.DMA((21,)), pltpu.SemaphoreType.DMA((94,)), pltpu.SemaphoreType.DMA((8,)),
+        *(buf for _ in range(7) for buf in stream(128)),
     ]
 
 

time: 66 us -> 63.5 us (0.962)
  Pallas kernels: 65.2 us -> 62.7 us
    pallas_call x1, Pallas kernels: 63.3 us -> 60.8 us  [body(): pl.pallas_call(kernel, out_shape=(jax.ShapeDtypeStruct((128, D), BF16), j...]
where the time goes in v10:
time: 63.5 us; the launch traced here: 63.3 us
  Pallas kernels  62.7 us (99%)
  between operations  0.64 us (1%)
    pallas_call x1, Pallas kernels, body(): pl.pallas_call(kernel, out_shape=(jax.ShapeDtypeStruct((128, D), BF16), j...  60.8 us
    pallas_call x1, Pallas kernels, body(): pl.pallas_call(emit, out_shape=(jax.ShapeDtypeStruct((128, D), BF16), jax...  1.88 us

profile of v10, /device:TPU:1, one launch (start us, length us, event | category | flops | bytes accessed | tf_op | source)
XLA Modules:
  0.0 63.3 jit_solution(18087882383786307481)
XLA Ops:
  0.6 60.8 %shard_map.85 = (bf16[128,1280]{1,0:T(8,128)(2,1)}, f32[10,2856]{1,0:T(8,128)}, f32[8,128]{1,0:T(8,128)}) custom-call(bf16[128,1280]{1,0:T(8,128)(2,1)} %bitcast.7, bf16[128,2560]{1,0:T(8,128)(2,1)} %bitcast.6, bf16[160,2856]{1,0:T(8,128)(2,1)} %w_ref.1, f32[1,40]{1,0:T(1,128)} %bitcast.8, f32[1,40]{1,0:T(1,128)} %bitcast.9, f32[1,40]{1,0:T(1,128)} %bitcast.10), custom_call_target="tpu_custom_call" | custom-call | tf_op jit(solution)/shard_map/pallas_call | solution.py:733
  61.5 1.9 %shard_map.86 = (bf16[128,1280]{1,0:T(8,128)(2,1)}, f32[10,2856]{1,0:T(8,128)}, f32[3,40]{1,0:T(4,128)}) custom-call(bf16[128,1280]{1,0:T(8,128)(2,1)} %get-tuple-element.9.hg_ref, f32[10,2856]{1,0:T(8,128)} %get-tuple-element.10.wg_ref, f32[8,128]{1,0:T(8,128)} %get-tuple-element.11.hd_ref), custom_call_target="tpu_custom_call" | custom-call | tf_op jit(solution)/shard_map/pallas_call | solution.py:745

commit v11 on v10

--- a/solution.py
+++ b/solution.py
@@ -235,6 +235,21 @@
     w_own_x(1)
     for k in (-1, 0, 1):
         hand(k)
+    i320 = lax.broadcasted_iota(jnp.int32, (320, 320), 0)
+    k320 = lax.broadcasted_iota(jnp.int32, (320, 320), 1)
+    tens = lax.shift_right_logical(i320 * 6554, 16)
+    source = ((tens & 3) * 8 + lax.shift_right_logical(tens, 2)) * 10 + i320 - tens * 10
+    perm = jnp.where(k320 == source, 1.0, 0.0).astype(F32).astype(BF16)
+
+    def transpose(k):
+        rows = ds((rank(k)[0] * 2 + rank(k)[1]) * 128, 128)
+        for q in range(4):
+            part = slice(320 * q, 320 * q + 320)
+            hidt[part, rows] = mm(perm, hidf[rows, part], NT).astype(BF16)
+
+    transpose(0)
+    h_c.wait_recv()
+    transpose(1)
     h_z.wait_recv()
     zrows = ds((rank(2)[0] * 2 + c) * 128, 128)
     h_f = send(26, hidf.at[zrows, :], hidf.at[zrows, :], core, 4)
@@ -295,7 +310,6 @@
         gs[b] = scores
         gts[b] = scores.T
 
-    h_c.wait_recv()
     for k in range(4):
         if k == 3:
             h_f.wait_recv()
@@ -310,13 +324,8 @@
     for k in (1, 2, 3):
         send(29, tts, ttr.at[k - 1], ydev(k), 7)
 
-    i320 = lax.broadcasted_iota(jnp.int32, (320, 320), 0)
-    k320 = lax.broadcasted_iota(jnp.int32, (320, 320), 1)
-    tens = lax.shift_right_logical(i320 * 6554, 16)
-    source = ((tens & 3) * 8 + lax.shift_right_logical(tens, 2)) * 10 + i320 - tens * 10
-    perm = jnp.where(k320 == source, 1.0, 0.0).astype(F32).astype(BF16)
-    for q in range(4):
-        hidt[320 * q : 320 * q + 320, :] = mm(perm, hidf[:, 320 * q : 320 * q + 320], NT).astype(BF16)
+    transpose(2)
+    transpose(3)
     w_forward(1)
     got(28, wf.at[:, ds(896 - 256 * c, 128)])
     maps(0, pl.ds(0, 128))
@@ -593,38 +602,38 @@
     rr[:, ds(lane0, 128)] = (mixed * silu_grad(projs[:, ds(256 * c, 128, 128)])).astype(BF16)
     rr[:, ds(896 - 256 * c, 128)] = jnp.zeros((512, 128), BF16)
     mp.first()
+
+    def token(half):
+        rows = ds(half * 256, 256)
+        for n in range(5):
+            part = slice(256 * n, 256 * n + 256)
+            hgp[rows, part] = mm(rr[rows, :], wf[part, :], NT)
+
+    mate_row = ds((zl * 2 + 1 - c) * 128, 128)
+    far_mate = ds(((1 - zl) * 2 + 1 - c) * 128, 128)
+    far_row = ds(((1 - zl) * 2 + c) * 128, 128)
+    token(1 - zl)
+    hgs[1] = hgp[far_mate, :].astype(BF16)
+    hg_far = send(43, hgs.at[1], hgr.at[1], core, 11)
     p0.rest()
     p0.second()
     p1.rest()
     p1.second()
     p2.third()
-
-    def token(lo, hi):
-        for n in range(lo, hi):
-            part = slice(256 * n, 256 * n + 256)
-            hgp[:, part] = mm(rr[...], wf[part, :], NT)
-
+    hg_far.wait_recv()
+    hgs[2] = (hgp[far_row, :] + hgr[1].astype(F32)).astype(BF16)
+    hg_z = send(44, hgs.at[2], hgr.at[2], rank(2)[2], 11)
     st.rest()
-    token(0, 2)
+    st.second()
     p3.third()
     mp.rest()
-    st.second()
-    token(2, 4)
     mp.second()
     p4.third()
-    token(4, 5)
-    mate_row = ds((zl * 2 + 1 - c) * 128, 128)
-    far_mate = ds(((1 - zl) * 2 + 1 - c) * 128, 128)
-    far_row = ds(((1 - zl) * 2 + c) * 128, 128)
-    hgs[1] = hgp[far_mate, :].astype(BF16)
-    hg_far = send(43, hgs.at[1], hgr.at[1], core, 11)
+    token(zl)
     hgs[0] = hgp[mate_row, :].astype(BF16)
     hg_near = send(42, hgs.at[0], hgr.at[0], core, 11)
     p2.fourth()
     p0.third()
-    hg_far.wait_recv()
-    hgs[2] = (hgp[far_row, :] + hgr[1].astype(F32)).astype(BF16)
-    hg_z = send(44, hgs.at[2], hgr.at[2], rank(2)[2], 11)
     p1.third()
     p3.fourth()
     got(38, heads_y.at[0:3])
@@ -644,15 +653,15 @@
     p4.owners()
     st.fourth()
     mp.fourth()
-    p0.owners()
-    p1.owners()
-    st.owners()
-    mp.owners()
     hg_near.wait_recv()
     hg_z.wait_recv()
     hgo[...] = (hgp[here_id, :] + hgr[0].astype(F32) + hgr[2].astype(F32)).astype(BF16)
     hg_out = pltpu.make_async_copy(hgo, hg_ref, ls.at[5])
     hg_out.start()
+    p0.owners()
+    p1.owners()
+    st.owners()
+    mp.owners()
     head_z.wait_recv()
     heads_g[r] = heads_z[0] + heads_z[1]
     for k in (1, 2, 3):

time: 63.5 us -> 63.5 us (level)
  no operation moved by 1% of the time
where the time goes in v11:
time: 63.5 us; the launch traced here: 63.3 us
  Pallas kernels  62.7 us (99%)
  between operations  0.64 us (1%)
    pallas_call x1, Pallas kernels, body(): pl.pallas_call(kernel, out_shape=(jax.ShapeDtypeStruct((128, D), BF16), j...  60.8 us
    pallas_call x1, Pallas kernels, body(): pl.pallas_call(emit, out_shape=(jax.ShapeDtypeStruct((128, D), BF16), jax...  1.88 us

profile of v11, /device:TPU:1, one launch (start us, length us, event | category | flops | bytes accessed | tf_op | source)
XLA Modules:
  0.0 63.3 jit_solution(623423410136556107)
XLA Ops:
  0.6 60.8 %shard_map.85 = (bf16[128,1280]{1,0:T(8,128)(2,1)}, f32[10,2856]{1,0:T(8,128)}, f32[8,128]{1,0:T(8,128)}) custom-call(bf16[128,1280]{1,0:T(8,128)(2,1)} %bitcast.7, bf16[128,2560]{1,0:T(8,128)(2,1)} %bitcast.6, bf16[160,2856]{1,0:T(8,128)(2,1)} %w_ref.1, f32[1,40]{1,0:T(1,128)} %bitcast.8, f32[1,40]{1,0:T(1,128)} %bitcast.9, f32[1,40]{1,0:T(1,128)} %bitcast.10), custom_call_target="tpu_custom_call" | custom-call | tf_op jit(solution)/shard_map/pallas_call | solution.py:742
  61.4 1.9 %shard_map.86 = (bf16[128,1280]{1,0:T(8,128)(2,1)}, f32[10,2856]{1,0:T(8,128)}, f32[3,40]{1,0:T(4,128)}) custom-call(bf16[128,1280]{1,0:T(8,128)(2,1)} %get-tuple-element.9.hg_ref, f32[10,2856]{1,0:T(8,128)} %get-tuple-element.10.wg_ref, f32[8,128]{1,0:T(8,128)} %get-tuple-element.11.hd_ref), custom_call_target="tpu_custom_call" | custom-call | tf_op jit(solution)/shard_map/pallas_call | solution.py:754

commit v12 on v11

--- a/solution.py
+++ b/solution.py
@@ -597,6 +597,8 @@
     heads_y[y] = mm(packed, place, NN, highest)
     for k in (1, 2, 3):
         send(38, heads_y.at[y], heads_y.at[y], ydev(k), 10)
+    p0.rest()
+    p0.second()
     t1.wait_recv()
     mixed = jnp.where(first, dbf[...], dcf[...]) + t1r[...]
     rr[:, ds(lane0, 128)] = (mixed * silu_grad(projs[:, ds(256 * c, 128, 128)])).astype(BF16)
@@ -612,53 +614,51 @@
     mate_row = ds((zl * 2 + 1 - c) * 128, 128)
     far_mate = ds(((1 - zl) * 2 + 1 - c) * 128, 128)
     far_row = ds(((1 - zl) * 2 + c) * 128, 128)
+    p1.rest()
+    p1.second()
+    p2.third()
+    st.rest()
+    st.second()
+    p3.third()
     token(1 - zl)
     hgs[1] = hgp[far_mate, :].astype(BF16)
     hg_far = send(43, hgs.at[1], hgr.at[1], core, 11)
-    p0.rest()
-    p0.second()
-    p1.rest()
-    p1.second()
-    p2.third()
+    mp.rest()
+    mp.second()
+    p4.third()
     hg_far.wait_recv()
     hgs[2] = (hgp[far_row, :] + hgr[1].astype(F32)).astype(BF16)
     hg_z = send(44, hgs.at[2], hgr.at[2], rank(2)[2], 11)
-    st.rest()
-    st.second()
-    p3.third()
-    mp.rest()
-    mp.second()
-    p4.third()
+    p0.third()
     token(zl)
     hgs[0] = hgp[mate_row, :].astype(BF16)
     hg_near = send(42, hgs.at[0], hgr.at[0], core, 11)
+    p1.third()
     p2.fourth()
-    p0.third()
-    p1.third()
     p3.fourth()
+    st.third()
+    mp.third()
     got(38, heads_y.at[0:3])
     heads_x[x] = (heads_y[0] + heads_y[1]) + (heads_y[2] + heads_y[3])
     for k in (1, 2, 3):
         send(39, heads_x.at[x], heads_x.at[x], xdev(k), 10)
-    st.third()
-    mp.third()
     p4.fourth()
+    p0.fourth()
     p2.owners()
-    p0.fourth()
+    p3.owners()
+    p1.fourth()
+    st.fourth()
     got(39, heads_x.at[0:3])
     heads_z[zh] = (heads_x[0] + heads_x[1]) + (heads_x[2] + heads_x[3])
     head_z = send(40, heads_z.at[zh], heads_z.at[zh], zpair, 10)
-    p3.owners()
-    p1.fourth()
+    mp.fourth()
     p4.owners()
-    st.fourth()
-    mp.fourth()
+    p0.owners()
     hg_near.wait_recv()
     hg_z.wait_recv()
     hgo[...] = (hgp[here_id, :] + hgr[0].astype(F32) + hgr[2].astype(F32)).astype(BF16)
     hg_out = pltpu.make_async_copy(hgo, hg_ref, ls.at[5])
     hg_out.start()
-    p0.owners()
     p1.owners()
     st.owners()
     mp.owners()
@@ -666,14 +666,14 @@
     heads_g[r] = heads_z[0] + heads_z[1]
     for k in (1, 2, 3):
         send(41, heads_g.at[r], heads_g.at[r], rank(k)[2], 10)
+    for t, stream in ((2, p2), (3, p3), (4, p4), (0, p0), (1, p1)):
+        stream.finish()
+        for k in range(4):
+            wgo[:, 640 * k + 128 * t : 640 * k + 128 * t + 128] = stream.rd[k, 0:10, :]
     got(41, heads_g.at[0:3])
     hdo[...] = (heads_g[0] + heads_g[1]) + (heads_g[2] + heads_g[3])
     hd_out = pltpu.make_async_copy(hdo, hd_ref, ls.at[6])
     hd_out.start()
-    for t, stream in ((2, p2), (3, p3), (4, p4), (0, p0), (1, p1)):
-        stream.finish()
-        for k in range(4):
-            wgo[:, 640 * k + 128 * t : 640 * k + 128 * t + 128] = stream.rd[k, 0:10, :]
     st.finish()
     for k in range(4):
         wgo[:, 2816 + 10 * k : 2826 + 10 * k] = st.rd[k, 0:10, 0:10]

time: 63.5 us -> 62.7 us (0.987)
  Pallas kernels: 62.7 us -> 61.9 us
    pallas_call x1, Pallas kernels: 60.8 us -> 60 us  [body(): pl.pallas_call(kernel, out_shape=(jax.ShapeDtypeStruct((128, D), BF16), j...]
where the time goes in v12:
time: 62.7 us; the launch traced here: 62.5 us
  Pallas kernels  61.9 us (99%)
  between operations  0.64 us (1%)
    pallas_call x1, Pallas kernels, body(): pl.pallas_call(kernel, out_shape=(jax.ShapeDtypeStruct((128, D), BF16), j...  60 us
    pallas_call x1, Pallas kernels, body(): pl.pallas_call(emit, out_shape=(jax.ShapeDtypeStruct((128, D), BF16), jax...  1.88 us

profile of v12, /device:TPU:1, one launch (start us, length us, event | category | flops | bytes accessed | tf_op | source)
XLA Modules:
  0.0 62.5 jit_solution(16577364561032934140)
XLA Ops:
  0.6 60.0 %shard_map.85 = (bf16[128,1280]{1,0:T(8,128)(2,1)}, f32[10,2856]{1,0:T(8,128)}, f32[8,128]{1,0:T(8,128)}) custom-call(bf16[128,1280]{1,0:T(8,128)(2,1)} %bitcast.7, bf16[128,2560]{1,0:T(8,128)(2,1)} %bitcast.6, bf16[160,2856]{1,0:T(8,128)(2,1)} %w_ref.1, f32[1,40]{1,0:T(1,128)} %bitcast.8, f32[1,40]{1,0:T(1,128)} %bitcast.9, f32[1,40]{1,0:T(1,128)} %bitcast.10), custom_call_target="tpu_custom_call" | custom-call | tf_op jit(solution)/shard_map/pallas_call | solution.py:742
  60.7 1.9 %shard_map.86 = (bf16[128,1280]{1,0:T(8,128)(2,1)}, f32[10,2856]{1,0:T(8,128)}, f32[3,40]{1,0:T(4,128)}) custom-call(bf16[128,1280]{1,0:T(8,128)(2,1)} %get-tuple-element.9.hg_ref, f32[10,2856]{1,0:T(8,128)} %get-tuple-element.10.wg_ref, f32[8,128]{1,0:T(8,128)} %get-tuple-element.11.hd_ref), custom_call_target="tpu_custom_call" | custom-call | tf_op jit(solution)/shard_map/pallas_call | solution.py:754

commit v13 on v12

--- a/solution.py
+++ b/solution.py
@@ -654,11 +654,6 @@
     mp.fourth()
     p4.owners()
     p0.owners()
-    hg_near.wait_recv()
-    hg_z.wait_recv()
-    hgo[...] = (hgp[here_id, :] + hgr[0].astype(F32) + hgr[2].astype(F32)).astype(BF16)
-    hg_out = pltpu.make_async_copy(hgo, hg_ref, ls.at[5])
-    hg_out.start()
     p1.owners()
     st.owners()
     mp.owners()
@@ -666,6 +661,11 @@
     heads_g[r] = heads_z[0] + heads_z[1]
     for k in (1, 2, 3):
         send(41, heads_g.at[r], heads_g.at[r], rank(k)[2], 10)
+    hg_near.wait_recv()
+    hg_z.wait_recv()
+    hgo[...] = (hgp[here_id, :] + hgr[0].astype(F32) + hgr[2].astype(F32)).astype(BF16)
+    hg_out = pltpu.make_async_copy(hgo, hg_ref, ls.at[5])
+    hg_out.start()
     for t, stream in ((2, p2), (3, p3), (4, p4), (0, p0), (1, p1)):
         stream.finish()
         for k in range(4):

time: 62.7 us -> 62.5 us (level)
  no operation moved by 1% of the time
where the time goes in v13:
time: 62.5 us; the launch traced here: 62.3 us
  Pallas kernels  61.7 us (99%)
  between operations  0.64 us (1%)
    pallas_call x1, Pallas kernels, body(): pl.pallas_call(kernel, out_shape=(jax.ShapeDtypeStruct((128, D), BF16), j...  59.8 us
    pallas_call x1, Pallas kernels, body(): pl.pallas_call(emit, out_shape=(jax.ShapeDtypeStruct((128, D), BF16), jax...  1.88 us

profile of v13, /device:TPU:1, one launch (start us, length us, event | category | flops | bytes accessed | tf_op | source)
XLA Modules:
  0.0 62.3 jit_solution(1904787549612133358)
XLA Ops:
  0.6 59.8 %shard_map.85 = (bf16[128,1280]{1,0:T(8,128)(2,1)}, f32[10,2856]{1,0:T(8,128)}, f32[8,128]{1,0:T(8,128)}) custom-call(bf16[128,1280]{1,0:T(8,128)(2,1)} %bitcast.7, bf16[128,2560]{1,0:T(8,128)(2,1)} %bitcast.6, bf16[160,2856]{1,0:T(8,128)(2,1)} %w_ref.1, f32[1,40]{1,0:T(1,128)} %bitcast.8, f32[1,40]{1,0:T(1,128)} %bitcast.9, f32[1,40]{1,0:T(1,128)} %bitcast.10), custom_call_target="tpu_custom_call" | custom-call | tf_op jit(solution)/shard_map/pallas_call | solution.py:742
  60.4 1.9 %shard_map.86 = (bf16[128,1280]{1,0:T(8,128)(2,1)}, f32[10,2856]{1,0:T(8,128)}, f32[3,40]{1,0:T(4,128)}) custom-call(bf16[128,1280]{1,0:T(8,128)(2,1)} %get-tuple-element.9.hg_ref, f32[10,2856]{1,0:T(8,128)} %get-tuple-element.10.wg_ref, f32[8,128]{1,0:T(8,128)} %get-tuple-element.11.hd_ref), custom_call_target="tpu_custom_call" | custom-call | tf_op jit(solution)/shard_map/pallas_call | solution.py:754

commit v14 on v13

--- a/solution.py
+++ b/solution.py
@@ -560,13 +560,11 @@
     p2.rest()
     pair_outside(4)
     p4.first()
-    p3.rest()
     pair_outside(0)
     p0.first()
     p2.second()
     pair_outside(1)
     p1.first()
-    p3.second()
 
     blocks(turn)
     first = c == 0
@@ -574,6 +572,8 @@
     t1 = send(35, t1s, t1r, core, 9)
     p4.rest()
     p4.second()
+    p3.rest()
+    p3.second()
 
     ownl = coli < 10
     bias_sum = decay_sum = jnp.zeros((8, 128), F32)

time: 62.5 us -> 63.7 us (1.019)
  Pallas kernels: 61.7 us -> 62.8 us
    pallas_call x1, Pallas kernels: 59.8 us -> 61 us  [body(): pl.pallas_call(kernel, out_shape=(jax.ShapeDtypeStruct((128, D), BF16), j...]
where the time goes in v14:
time: 63.7 us; the launch traced here: 63.5 us
  Pallas kernels  62.8 us (99%)
  between operations  0.64 us (1%)
    pallas_call x1, Pallas kernels, body(): pl.pallas_call(kernel, out_shape=(jax.ShapeDtypeStruct((128, D), BF16), j...  61 us
    pallas_call x1, Pallas kernels, body(): pl.pallas_call(emit, out_shape=(jax.ShapeDtypeStruct((128, D), BF16), jax...  1.88 us

profile of v14, /device:TPU:1, one launch (start us, length us, event | category | flops | bytes accessed | tf_op | source)
XLA Modules:
  0.0 63.5 jit_solution(1430850121263893893)
XLA Ops:
  0.6 61.0 %shard_map.85 = (bf16[128,1280]{1,0:T(8,128)(2,1)}, f32[10,2856]{1,0:T(8,128)}, f32[8,128]{1,0:T(8,128)}) custom-call(bf16[128,1280]{1,0:T(8,128)(2,1)} %bitcast.7, bf16[128,2560]{1,0:T(8,128)(2,1)} %bitcast.6, bf16[160,2856]{1,0:T(8,128)(2,1)} %w_ref.1, f32[1,40]{1,0:T(1,128)} %bitcast.8, f32[1,40]{1,0:T(1,128)} %bitcast.9, f32[1,40]{1,0:T(1,128)} %bitcast.10), custom_call_target="tpu_custom_call" | custom-call | tf_op jit(solution)/shard_map/pallas_call | solution.py:742
  61.6 1.9 %shard_map.86 = (bf16[128,1280]{1,0:T(8,128)(2,1)}, f32[10,2856]{1,0:T(8,128)}, f32[3,40]{1,0:T(4,128)}) custom-call(bf16[128,1280]{1,0:T(8,128)(2,1)} %get-tuple-element.9.hg_ref, f32[10,2856]{1,0:T(8,128)} %get-tuple-element.10.wg_ref, f32[8,128]{1,0:T(8,128)} %get-tuple-element.11.hd_ref), custom_call_target="tpu_custom_call" | custom-call | tf_op jit(solution)/shard_map/pallas_call | solution.py:754
